TPU v7x, 32 devices: a whole 2x2x4 slice. The times are simulated.
32 devices in a mesh: dp: 8 (over z, y), head: 4 (over x, core).
Axes of the slice: x: 2, y: 2, z: 4, core: 2. Of those that a mesh axis runs over, the one named last changes fastest.
Arguments:
- inputs: bfloat16 [8, 1024, 768], P('dp', 'head'), may hold values from -6 to 6
- norm_gains: bfloat16 [2, 768], replicated, may hold values from 0.5 to 1.5
- norm_shifts: bfloat16 [2, 768], replicated, may hold values from -1.75 to 1.75
- w_qkv: bfloat16 [768, 2304], replicated, may hold values from -0.21875 to 0.21875
- qv_bias: bfloat16 [2, 768], replicated, may hold values from -1.75 to 1.75
- w_out: bfloat16 [768, 768], replicated, may hold values from -1.75 to 1.75
- out_biases: bfloat16 [2, 768], replicated, may hold values from -1.75 to 1.75
- w_up: bfloat16 [768, 3072], replicated, may hold values from -0.21875 to 0.21875
- up_bias: bfloat16 [3072], replicated, may hold values from -1.75 to 1.75
- w_down: bfloat16 [3072, 768], replicated, may hold values from -0.21875 to 0.21875
- lengths: int32 [8, 4], P('dp'), may hold values from 0 to 1024, as said below
- d_out: bfloat16 [8, 1024, 768], P('dp', 'head'), may hold values from -8 to 8
Outputs:
- block_out: bfloat16 [8, 1024, 768], P('dp', 'head')
- grad_inputs: float32 [8, 1024, 768], P('dp', 'head')
- grad_norm_gains: float32 [2, 768], P(None, 'dp')
- grad_norm_shifts: float32 [2, 768], P(None, 'dp')
- grad_qkv: float32 [768, 2304], P(None, 'dp')
- grad_qv_bias: float32 [2, 768], P(None, 'dp')
- grad_out: float32 [768, 768], P(None, 'dp')
- grad_out_biases: float32 [2, 768], P(None, 'dp')
- grad_up: float32 [768, 3072], P(None, 'dp')
- grad_up_bias: float32 [3072], P('dp')
- grad_down: float32 [3072, 768], P(None, 'dp')
Inputs may be any that keep to these rules, and one draw needn't show every extreme that they name: Each slot holds either one image of 1024 patches (lengths 1024, then zeros) or 1 to 4 images of 256 patches in its first entries, then zeros. The first slot holds one image of 1024 patches.
All inputs are finite; a program needn't handle non-finite values.
Results may differ from a plain program's by a relative error of at most 0.014.
Values may be sent and summed in bfloat16 or wider, within the bound.
A program may use at most 256 MiB of HBM per device.

v0:
```python
import jax
import jax.numpy as jnp
from jax import lax
from jax.sharding import PartitionSpec as P

D = 768
HEADS = 12
HDIM = 64
SLOT = 1024
ITEMS = 4


EPSILON = 1e-06


def norm_parts(values, norm_gain, norm_shift):
    average = jnp.mean(values, axis=-1, keepdims=True)
    centered = values - average
    variance = jnp.mean(centered * centered, axis=-1, keepdims=True)
    inverse = lax.rsqrt(variance + EPSILON)
    normal_unit = centered * inverse
    return (normal_unit, inverse, normal_unit * norm_gain + norm_shift)


def norm_back(grad_normed, normal_unit, inverse, norm_gain):
    grad_unit = grad_normed * norm_gain
    first_mean = jnp.mean(grad_unit, axis=-1, keepdims=True)
    second_mean = jnp.mean(grad_unit * normal_unit, axis=-1, keepdims=True)
    return inverse * (grad_unit - first_mean - normal_unit * second_mean)


def exact_gelu(values):
    return jax.nn.gelu(values, approximate=False)


def slot_allowed(lengths_row):
    item_ends = jnp.cumsum(lengths_row)
    positions = jnp.arange(SLOT, dtype=jnp.int32)
    segment = jnp.sum((positions[:, None] >= item_ends[None, :]).astype(jnp.int32), axis=1)
    is_real = positions < item_ends[ITEMS - 1]
    same_item = (segment[:, None] == segment[None, :]) & is_real[None, :]
    return (same_item | (positions[:, None] == positions[None, :]))[None]


def block_scores(query_part, key_part, allowed):
    scores = jnp.einsum("hbqe,hbke->hbqk", query_part, key_part, preferred_element_type=jnp.float32)
    scores = scores * query_part.shape[-1] ** (-0.5)
    return jnp.where(allowed[None], scores, -jnp.inf)


def block_forward(query_part, key_part, value_part, allowed):
    masked = block_scores(query_part, key_part, allowed)
    row_max = jnp.max(masked, axis=-1, keepdims=True)
    weights = jnp.exp(masked - row_max)
    row_sum = jnp.sum(weights, axis=-1, keepdims=True)
    low_weights = (weights / row_sum).astype(jnp.bfloat16)
    mixed_out = jnp.einsum(
        "hbqk,hbke->hbqe", low_weights, value_part, preferred_element_type=jnp.float32
    )
    return (mixed_out.astype(jnp.bfloat16), (row_max + jnp.log(row_sum))[..., 0])


def block_backward(query_part, key_part, value_part, allowed, grad_mixed, log_totals):
    masked = block_scores(query_part, key_part, allowed)
    attn_weights = jnp.exp(masked - log_totals[..., None])
    grad_weights = jnp.einsum(
        "hbqe,hbke->hbqk", grad_mixed, value_part, preferred_element_type=jnp.float32
    )
    row_inner = jnp.sum(attn_weights * grad_weights, axis=-1, keepdims=True)
    grad_scores = (attn_weights * (grad_weights - row_inner)).astype(jnp.bfloat16)
    score_scale = query_part.shape[-1] ** (-0.5)
    grad_query = (
        jnp.einsum("hbqk,hbke->hbqe", grad_scores, key_part, preferred_element_type=jnp.float32)
        * score_scale
    )
    grad_key = (
        jnp.einsum("hbqk,hbqe->hbke", grad_scores, query_part, preferred_element_type=jnp.float32)
        * score_scale
    )
    grad_value = jnp.einsum(
        "hbqk,hbqe->hbke",
        attn_weights.astype(jnp.bfloat16),
        grad_mixed,
        preferred_element_type=jnp.float32,
    )
    return jnp.stack([grad_query, grad_key, grad_value]).astype(jnp.bfloat16)


def slot_attend(packed, lengths_row):
    head_count = packed.shape[1]

    def whole_slot(operand):
        blocked = operand.reshape(3, head_count, 1, SLOT, HDIM)
        mixed_out, log_totals = block_forward(
            blocked[0], blocked[1], blocked[2], slot_allowed(lengths_row)
        )
        return (mixed_out.reshape(head_count, SLOT * HDIM), log_totals.reshape(head_count, SLOT))

    return whole_slot(packed)


def slot_attend_back(packed, grad_mixed, log_totals, lengths_row):
    head_count = packed.shape[1]

    def whole_slot(operands):
        blocked = operands[0].reshape(3, head_count, 1, SLOT, HDIM)
        result = block_backward(
            blocked[0],
            blocked[1],
            blocked[2],
            slot_allowed(lengths_row),
            operands[1].reshape(head_count, 1, SLOT, HDIM),
            operands[2].reshape(head_count, 1, SLOT),
        )
        return result.reshape(3, head_count, SLOT * HDIM)

    return whole_slot((packed, grad_mixed, log_totals))


def forward_slot(operands):
    return slot_attend(operands[0], operands[1])


def backward_slot(operands):
    return slot_attend_back(operands[0], operands[1], operands[2], operands[3])


def per_device(
    inputs,
    norm_gains,
    norm_shifts,
    w_qkv,
    qv_bias,
    w_out,
    out_biases,
    w_up,
    up_bias,
    w_down,
    lengths,
    d_out,
):
    groups = lax.axis_size("head")
    group_index = lax.axis_index("head")
    slot_count = inputs.shape[0]
    row_count = inputs.shape[1]
    local_heads = HEADS // groups
    gains = norm_gains.astype(jnp.float32)
    shifts = norm_shifts.astype(jnp.float32)
    biases = out_biases.astype(jnp.float32)
    up_shift = up_bias.astype(jnp.float32)
    query_bias = qv_bias.astype(jnp.float32)
    tokens = inputs.astype(jnp.float32)
    first_unit, first_inverse, first_normed = norm_parts(tokens, gains[0], shifts[0])
    normed_one = first_normed.astype(jnp.bfloat16)
    qkv_weight = w_qkv.reshape(D, 3, groups, local_heads, HDIM)
    full_bias = jnp.stack([query_bias[0], jnp.zeros_like(query_bias[0]), query_bias[1]])
    bias_grid = full_bias.reshape(3, groups, local_heads, HDIM).transpose(1, 0, 2, 3)[
        :, :, :, None, :
    ]
    projected = jnp.einsum(
        "srd,dcghe->sgchre", normed_one, qkv_weight, preferred_element_type=jnp.float32
    )
    packed = (
        (projected + bias_grid)
        .astype(jnp.bfloat16)
        .reshape(slot_count, groups, 3, local_heads, row_count * HDIM)
    )
    heads_side = lax.all_to_all(packed, "head", split_axis=1, concat_axis=4, tiled=True)[:, 0]
    mixed_heads, log_totals = lax.map(forward_slot, (heads_side, lengths))
    mixed_patch = lax.all_to_all(
        mixed_heads[:, None], "head", split_axis=3, concat_axis=1, tiled=True
    )
    mixed_patch = mixed_patch.reshape(slot_count, groups, local_heads, row_count, HDIM)
    out_weight = w_out.reshape(groups, local_heads, HDIM, D)
    attention = jnp.einsum(
        "sghre,ghef->srf", mixed_patch, out_weight, preferred_element_type=jnp.float32
    )
    hidden = (tokens + attention + biases[0]).reshape(-1, D)
    second_unit, second_inverse, second_normed = norm_parts(hidden, gains[1], shifts[1])
    normed_two = second_normed.astype(jnp.bfloat16)
    up_values = jnp.dot(normed_two, w_up, preferred_element_type=jnp.float32) + up_shift
    gelu_values, gelu_back = jax.vjp(exact_gelu, up_values)
    activated = gelu_values.astype(jnp.bfloat16)
    down_values = jnp.dot(activated, w_down, preferred_element_type=jnp.float32)
    block_out = (
        (hidden + down_values + biases[1]).astype(jnp.bfloat16).reshape(slot_count, row_count, D)
    )
    positions = group_index * row_count + jnp.arange(row_count, dtype=jnp.int32)
    totals = jnp.sum(lengths, axis=1)
    is_real = (positions[None, :] < totals[:, None]).astype(jnp.float32)
    grad_block = (d_out.astype(jnp.float32) * is_real[:, :, None]).reshape(-1, D)
    grad_low = grad_block.astype(jnp.bfloat16)
    down_grad = jnp.einsum("tf,td->fd", activated, grad_low, preferred_element_type=jnp.float32)
    grad_activated = jnp.einsum("td,fd->tf", grad_low, w_down, preferred_element_type=jnp.float32)
    grad_up = gelu_back(grad_activated)[0]
    grad_up_low = grad_up.astype(jnp.bfloat16)
    up_grad = jnp.einsum("td,tf->df", normed_two, grad_up_low, preferred_element_type=jnp.float32)
    upb_grad = jnp.sum(grad_up, axis=0)
    grad_normed_two = jnp.einsum("tf,df->td", grad_up_low, w_up, preferred_element_type=jnp.float32)
    grad_hidden = grad_block + norm_back(grad_normed_two, second_unit, second_inverse, gains[1])
    grad_hidden_low = grad_hidden.astype(jnp.bfloat16).reshape(slot_count, row_count, D)
    out_grad = jnp.einsum(
        "sghre,srf->ghef", mixed_patch, grad_hidden_low, preferred_element_type=jnp.float32
    ).reshape(D, D)
    grad_mixed = jnp.einsum(
        "srf,ghef->sghre", grad_hidden_low, out_weight, preferred_element_type=jnp.float32
    )
    grad_mixed = grad_mixed.astype(jnp.bfloat16).reshape(
        slot_count, groups, local_heads, row_count * HDIM
    )
    grad_heads = lax.all_to_all(grad_mixed, "head", split_axis=1, concat_axis=3, tiled=True)[:, 0]
    grad_packed = lax.map(backward_slot, (heads_side, grad_heads, log_totals, lengths))
    grad_patch = lax.all_to_all(
        grad_packed[:, None], "head", split_axis=4, concat_axis=1, tiled=True
    )
    grad_patch = grad_patch.reshape(slot_count, groups, 3, local_heads, row_count, HDIM)
    qkv_grad = jnp.einsum(
        "srd,sgchre->dcghe", normed_one, grad_patch, preferred_element_type=jnp.float32
    ).reshape(D, 3 * D)
    bias_sums = jnp.sum(grad_patch, axis=(0, 4), dtype=jnp.float32)
    bias_rows = bias_sums.transpose(1, 0, 2, 3).reshape(3, D)
    qv_grad = jnp.stack([bias_rows[0], bias_rows[2]])
    grad_normed_one = jnp.einsum(
        "sgchre,dcghe->srd", grad_patch, qkv_weight, preferred_element_type=jnp.float32
    )
    grad_inputs = grad_hidden.reshape(slot_count, row_count, D) + norm_back(
        grad_normed_one, first_unit, first_inverse, gains[0]
    )
    gains_grad = jnp.stack(
        [
            jnp.sum(grad_normed_one * first_unit, axis=(0, 1)),
            jnp.sum(grad_normed_two * second_unit, axis=0),
        ]
    )
    shifts_grad = jnp.stack(
        [jnp.sum(grad_normed_one, axis=(0, 1)), jnp.sum(grad_normed_two, axis=0)]
    )
    outb_grad = jnp.stack([jnp.sum(grad_hidden, axis=0), jnp.sum(grad_block, axis=0)])
    shared = (
        lax.psum_scatter(gains_grad, "dp", scatter_dimension=1, tiled=True),
        lax.psum_scatter(shifts_grad, "dp", scatter_dimension=1, tiled=True),
        lax.psum_scatter(qkv_grad, "dp", scatter_dimension=1, tiled=True),
        lax.psum_scatter(qv_grad, "dp", scatter_dimension=1, tiled=True),
        lax.psum_scatter(out_grad, "dp", scatter_dimension=1, tiled=True),
        lax.psum_scatter(outb_grad, "dp", scatter_dimension=1, tiled=True),
        lax.psum_scatter(up_grad, "dp", scatter_dimension=1, tiled=True),
        lax.psum_scatter(upb_grad, "dp", scatter_dimension=0, tiled=True),
        lax.psum_scatter(down_grad, "dp", scatter_dimension=1, tiled=True),
    )
    summed = (
        lax.psum(shared[0].astype(jnp.bfloat16), "head").astype(jnp.float32),
        lax.psum(shared[1].astype(jnp.bfloat16), "head").astype(jnp.float32),
        lax.psum(shared[2].astype(jnp.bfloat16), "head").astype(jnp.float32),
        lax.psum(shared[3].astype(jnp.bfloat16), "head").astype(jnp.float32),
        lax.psum(shared[4].astype(jnp.bfloat16), "head").astype(jnp.float32),
        lax.psum(shared[5].astype(jnp.bfloat16), "head").astype(jnp.float32),
        lax.psum(shared[6].astype(jnp.bfloat16), "head").astype(jnp.float32),
        lax.psum(shared[7].astype(jnp.bfloat16), "head").astype(jnp.float32),
        lax.psum(shared[8].astype(jnp.bfloat16), "head").astype(jnp.float32),
    )
    return (
        block_out,
        grad_inputs,
        summed[0],
        summed[1],
        summed[2],
        summed[3],
        summed[4],
        summed[5],
        summed[6],
        summed[7],
        summed[8],
    )


def solution(mesh):
    placed = (
        P("dp", "head", None),
        P(),
        P(),
        P(),
        P(),
        P(),
        P(),
        P(),
        P(),
        P(),
        P("dp", None),
        P("dp", "head", None),
    )
    return jax.shard_map(
        per_device,
        mesh=mesh,
        in_specs=placed,
        out_specs=(
            P("dp", "head", None),
            P("dp", "head", None),
            P(None, "dp"),
            P(None, "dp"),
            P(None, "dp"),
            P(None, "dp"),
            P(None, "dp"),
            P(None, "dp"),
            P(None, "dp"),
            P("dp"),
            P(None, "dp"),
        ),
        check_vma=False,
    )
```

profile of v0, /device:TPU:3, one launch (start us, length us, event | category | flops | bytes accessed | tf_op | source)
XLA Modules:
  0.0 1839.7 jit_solution(6899083665494931901)
XLA Ops:
  32.1 13.1 all-to-all-done
  66.0 50.4 %copy.160 = bf16[1,1,3,65536]{2,1,0,3:T(2,128)(2,1)} copy(bf16[1,1,3,65536]{3,2,1,0:T(4,128)(2,1)S(1)} %broadcast_in_dim.90) | data formatting | bytes 786432 | tf_op jit(solution)/shard_map/broadcast_in_dim | solution.py:171
  116.9 356.2 %reduce.28 = bf16[65536,3]{1,0:T(8,128)(2,1)} reduce(bf16[65536,1,1,3]{3,2,1,0:T(2,128)(2,1)} %bitcast.161, bf16[]{:T(256)} %broadcast.195), dimensions={1,2}, to_apply=%bitcast.124.reduce_sub_computation | reduce | bytes 786434
  473.1 33.0 %reshape.486 = bf16[4,2,24576]{2,1,0:T(2,128)(2,1)} reshape(bf16[65536,3]{1,0:T(8,128)(2,1)} %reduce.28) | data formatting | bytes 786432
  506.1 5.5 all-to-all-start.1
  512.3 4.8 all-to-all-done.1
  517.1 51.9 %reshape.487 = bf16[65536,1,1,3]{3,2,1,0:T(2,128)(2,1)} reshape(bf16[4,2,24576]{2,1,0:T(2,128)(2,1)S(1)} %all-to-all-done.1) | data formatting | bytes 786432
  569.0 61.0 %copy.161 = bf16[1,1,3,65536]{3,2,1,0:T(4,128)(2,1)S(1)} copy(bf16[1,1,3,65536]{2,1,0,3:T(2,128)(2,1)} %bitcast.162) | data formatting | bytes 786432 | tf_op jit(solution)/shard_map/all_to_all | solution.py:170
  633.9 11.7 multiply_convert_fusion.1
  653.9 5.4 all-to-all-start.2
  667.2 6.4 multiply_reduce_fusion
  673.7 10.1 multiply_convert_fusion
  683.8 5.1 fusion.23
  700.8 62.5 %copy.177 = bf16[1,1,3,3,65536]{3,2,1,0,4:T(4,128)(2,1)} copy(bf16[1,1,3,3,65536]{4,3,2,1,0:T(4,128)(2,1)S(1)} %pad_maximum_fusion) | data formatting | bytes 2359296 | tf_op jit(solution)/shard_map/while/body/eval_jaxpr/stack | solution.py:86
  763.3 88.2 %reshape.488 = bf16[4,2,73728]{2,1,0:T(2,128)(2,1)S(1)} reshape(bf16[65536,1,1,3,3]{4,3,2,1,0:T(4,128)(2,1)} %bitcast.126) | data formatting | bytes 2359296
  851.4 18.5 %all_to_all.60 = bf16[4,2,73728]{2,1,0:T(2,128)(2,1)S(1)} all-to-all(bf16[4,2,73728]{2,1,0:T(2,128)(2,1)S(1)} %reshape.488), channel_id=1, replica_groups=mesh['dp'=8,'head'=4] {'head'}, dimensions={0} | all-to-all | bytes 2359296 | tf_op jit(solution)/shard_map/all_to_all | solution.py:213
  869.9 89.1 %reshape.489 = bf16[65536,1,1,3,3]{4,3,2,1,0:T(4,128)(2,1)} reshape(bf16[4,2,73728]{2,1,0:T(2,128)(2,1)S(1)} %all_to_all.60) | data formatting | bytes 2359296
  959.0 90.3 %copy.178 = bf16[1,1,3,3,4,16384]{5,4,3,2,1,0:T(4,128)(2,1)} copy(bf16[1,1,3,3,4,16384]{3,2,5,4,1,0:T(4,128)(2,1)} %bitcast.30) | data formatting | bytes 2359296 | tf_op jit(solution)/shard_map/all_to_all | solution.py:213
  1058.9 6.6 fusion.43
  1066.2 6.6 fusion.57
  1072.9 5.8 copy.149
  1098.4 89.6 %reduce-scatter.17.cloned.1.call-done = f32[768,288]{0,1:T(8,128)} async-done(((f32[768,2304]{0,1:T(8,128)}), f32[768,288]{0,1:T(8,128)}) %reduce-scatter.17.cloned.1.call-update) | async-done | bytes 884752 | tf_op jit(solution)/shard_map/reduce_scatter | solution.py:242
  1190.1 165.6 %reduce-scatter.21.cloned.1.call-done = f32[768,384]{1,0:T(8,128)} async-done(((f32[768,3072]{1,0:T(8,128)}), f32[768,384]{1,0:T(8,128)}) %reduce-scatter.21.cloned.1.call-update) | async-done | bytes 1179664 | tf_op jit(solution)/shard_map/reduce_scatter | solution.py:246
  1357.8 164.3 %reduce-scatter.23.cloned.1.call-done = f32[3072,96]{0,1:T(8,128)} async-done(((f32[3072,768]{0,1:T(8,128)}), f32[3072,96]{0,1:T(8,128)}) %reduce-scatter.23.cloned.1.call-update) | async-done | bytes 1179664 | tf_op jit(solution)/shard_map/reduce_scatter | solution.py:248
  1524.3 5.1 fusion.27
  1529.4 28.2 %all-reduce = bf16[3072]{0:T(1024)(128)(2,1)S(1)} all-reduce(f32[3072]{0:T(1024)S(1)} %copy-done.33), channel_id=9, replica_groups=mesh['dp'=8,'head'=4] {'dp'}, use_global_device_ids=true, to_apply=%region_36.37.clone | all-reduce | flops 3072 | bytes 18432
  1557.7 26.4 %reduce-scatter.31.cloned.1.call-done = f32[96,2]{1,0:T(8,128)} async-done(((f32[768,2]{1,0:T(8,128)}), f32[96,2]{1,0:T(8,128)}) %reduce-scatter.31.cloned.1.call-update) | async-done | bytes 784
  1586.2 61.8 %reduce-scatter.29.cloned.1.call-done = f32[96,2]{1,0:T(8,128)} async-done(((f32[768,2]{1,0:T(8,128)}), f32[96,2]{1,0:T(8,128)}) %reduce-scatter.29.cloned.1.call-update) | async-done | bytes 784
  1648.9 63.2 %reduce-scatter.27.cloned.1.call-done = f32[96,2]{1,0:T(8,128)} async-done(((f32[768,2]{1,0:T(8,128)}), f32[96,2]{1,0:T(8,128)}) %reduce-scatter.27.cloned.1.call-update) | async-done | bytes 784
  1713.0 63.2 %reduce-scatter.25.cloned.1.call-done = f32[96,2]{1,0:T(8,128)} async-done(((f32[768,2]{1,0:T(8,128)}), f32[96,2]{1,0:T(8,128)}) %reduce-scatter.25.cloned.1.call-update) | async-done | bytes 784
  1777.0 7.6 all-reduce.1
  1787.5 39.3 %all-reduce.5.cloned.1.call-done = (bf16[768,288]{0,1:T(8,128)(2,1)}, bf16[768,96]{0,1:T(8,128)(2,1)}, bf16[768,384]{1,0:T(8,128)(2,1)}, bf16[3072,96]{0,1:T(8,128)(2,1)}) async-done(((bf16[768,288]{0,1:T(8,128)(2,1)}, bf16[768,96]{0,1:T(8,128)(2,1)}, bf16[768,384]{1,0:T(8,128)(2,1)}, bf16[3072,96]{0,1:T(8,128)(2,1)}), (bf16[768,288]{0,1:T(8,128)(2,1)}, bf16[768,96]{0,1:T(8,128)(2,1)}, ...) | async-done | bytes 1769488 | tf_op jit(solution)/shard_map/psum | solution.py:253
  (246 shorter events, 127.7 us)
Async XLA Ops:
  7.2 625.8 %copy-start = (bf16[768,768]{1,0:T(8,128)(2,1)S(1)}, bf16[768,768]{1,0:T(8,128)(2,1)}, u32[]{:S(2)}) copy-start(bf16[768,768]{1,0:T(8,128)(2,1)} %param.17) | copy-start | bytes 3538948
  23.1 22.1 %all-to-all-start = ((bf16[1,4,3,3,16384]{4,3,2,0,1:T(4,128)(2,1)}), bf16[1,4,3,3,16384]{4,3,2,0,1:T(4,128)(2,1)S(1)}, u32[]{:S(2)}, u32[]{:S(2)}) async-start(bf16[1,4,3,3,16384]{4,3,2,0,1:T(4,128)(2,1)} %reshape.468), calls=%async_computation | async-start | bytes 3145728 | tf_op jit(solution)/shard_map/all_to_all | solution.py:168
  506.1 11.0 all-to-all-start.1
  512.3 138.3 %copy-start.24 = (f32[256]{0:T(256)}, f32[256]{0:T(256)S(1)}, u32[]{:S(2)}) copy-start(f32[256]{0:T(256)S(1)} %compare_convert_fusion) | copy-start | bytes 3076
  569.0 64.0 %copy-start.8 = (bf16[1,256,768]{2,1,0:T(8,128)(2,1)S(1)}, bf16[1,256,768]{2,1,0:T(8,128)(2,1)}, u32[]{:S(2)}) copy-start(bf16[1,256,768]{2,1,0:T(8,128)(2,1)} %param.12) | copy-start | bytes 1179652
  633.0 12.6 slice-start.5
  633.0 15.4 slice-start.3
  633.6 17.0 copy-start.6
  633.9 16.8 copy-start.32
  633.9 11.7 copy-start.11
  633.9 11.7 slice-start.6
  633.9 14.5 slice-start.4
  653.9 12.3 all-to-all-start.2
  659.3 437.5 %reduce-scatter.19.cloned.1.call-start = ((), (), s32[]{:S(2)}) async-start(), calls=%async_computation.13 | async-start | bytes 2654208 | tf_op jit(solution)/shard_map/reduce_scatter | solution.py:244
  662.7 525.4 %reduce-scatter.17.cloned.1.call-start = ((), (), s32[]{:S(2)}) async-start(), calls=%async_computation.12 | async-start | bytes 7962624 | tf_op jit(solution)/shard_map/reduce_scatter | solution.py:242
  667.2 23.7 %slice-start = ((s8[12582912]{0:T(1024)(128)(4,1)}), s8[4194304]{0:T(1024)(128)(4,1)S(1)}, s32[]{:S(2)}) async-start(s8[12582912]{0:T(1024)(128)(4,1)} %bitcast.159), calls=%async_computation.21 | async-start | bytes 8388608
  667.2 23.7 %slice-start.1 = ((s8[12582912]{0:T(1024)(128)(4,1)}), s8[4194304]{0:T(1024)(128)(4,1)S(1)}, s32[]{:S(2)}) async-start(s8[12582912]{0:T(1024)(128)(4,1)} %bitcast.159), calls=%async_computation.22 | async-start | bytes 8388608
  673.7 17.3 slice-start.2
  1057.8 297.8 %reduce-scatter.21.cloned.1.call-start = ((), (), s32[]{:S(2)}) async-start(), calls=%async_computation.14 | async-start | bytes 10616832 | tf_op jit(solution)/shard_map/reduce_scatter | solution.py:246
  1065.5 456.5 %reduce-scatter.23.cloned.1.call-start = ((), (), s32[]{:S(2)}) async-start(), calls=%async_computation.15 | async-start | bytes 10616832 | tf_op jit(solution)/shard_map/reduce_scatter | solution.py:248
  1072.9 511.2 %reduce-scatter.31.cloned.1.call-start = ((), (), s32[]{:S(2)}) async-start(), calls=%async_computation.19 | async-start | bytes 442368
  1083.4 564.6 %reduce-scatter.29.cloned.1.call-start = ((), (), s32[]{:S(2)}) async-start(), calls=%async_computation.18 | async-start | bytes 442368
  1092.6 619.5 %reduce-scatter.27.cloned.1.call-start = ((), (), s32[]{:S(2)}) async-start(), calls=%async_computation.17 | async-start | bytes 442368
  1094.4 681.8 %reduce-scatter.25.cloned.1.call-start = ((), (), s32[]{:S(2)}) async-start(), calls=%async_computation.16 | async-start | bytes 442368
  1095.5 731.4 %all-reduce.5.cloned.1.call-start = ((), (), s32[]{:S(2)}) async-start(), calls=%async_computation.20 | async-start | bytes 3538944 | tf_op jit(solution)/shard_map/psum | solution.py:253
  1098.4 425.8 %copy-start.42 = (f32[768]{0:T(1024)S(1)}, f32[768]{0:T(1024)}, u32[]{:S(2)}) copy-start(f32[768]{0:T(1024)} %get-tuple-element.52) | copy-start | bytes 9220
  1524.3 60.7 %copy-start.44 = (f32[256]{0:T(256)S(1)}, f32[256]{0:T(256)}, u32[]{:S(2)}) copy-start(f32[256]{0:T(256)} %get-tuple-element.47) | copy-start | bytes 3076
  1524.3 60.7 %copy-start.5 = (f32[256,768]{1,0:T(8,128)S(1)}, f32[256,768]{1,0:T(8,128)}, u32[]{:S(2)}) copy-start(f32[256,768]{1,0:T(8,128)} %copy-done.4) | copy-start | bytes 2359300
  1524.3 60.7 %copy-start.10 = (bf16[1,256,768]{2,1,0:T(8,128)(2,1)S(1)}, bf16[1,256,768]{2,1,0:T(8,128)(2,1)}, u32[]{:S(2)}) copy-start(bf16[1,256,768]{2,1,0:T(8,128)(2,1)} %param.12) | copy-start | bytes 1179652
  1524.3 60.7 %copy-start.16 = (f32[256,768,1,1,1]{1,0,4,3,2:T(8,128)S(1)}, f32[256,768,1,1,1]{1,0,4,3,2:T(8,128)}, u32[]{:S(2)}) copy-start(f32[256,768,1,1,1]{1,0,4,3,2:T(8,128)} %copy-done.15) | copy-start | bytes 2359300
  1524.3 60.7 %copy-start.40 = (f32[256]{0:T(256)S(1)}, f32[256]{0:T(256)}, u32[]{:S(2)}) copy-start(f32[256]{0:T(256)} %copy-done.38) | copy-start | bytes 3076
  1585.0 247.9 %copy-start.1 = (bf16[768,768]{1,0:T(8,128)(2,1)S(1)}, bf16[768,768]{1,0:T(8,128)(2,1)}, u32[]{:S(2)}) copy-start(bf16[768,768]{1,0:T(8,128)(2,1)} %param.17) | copy-start | bytes 3538948
  (34 other events, 160.4 us)
Sparse Core Ops, SparseCore 0:
  663.6 69.6 reduce-scatter.18
  1057.9 130.1 reduce-scatter.16
  1192.1 163.4 reduce-scatter.20
  1359.5 162.5 reduce-scatter.22
  1525.5 58.5 reduce-scatter.30
  1587.6 60.3 reduce-scatter.28
  1651.6 60.4 reduce-scatter.26
  1715.7 60.4 reduce-scatter.24
  1780.1 46.6 all-reduce.4
where the time goes:
time: 1850 us; the launch traced here: 1840 us
  waiting for transfers between devices  695 us (38%)
  local copies, waits for them, and re-layouts  587 us (32%)
  other arithmetic  401 us (22%)
  matrix products  70.8 us (4%)
  blocking collectives  54.3 us (3%)
    unnamed x4, other arithmetic  356 us
    unnamed x124, local copies, waits for them, and re-layouts  282 us
    unnamed x13, waiting for transfers between devices  215 us
    reduce_scatter x1, waiting for transfers between devices, per_device(): lax.psum_scatter(up_grad, 'dp', scatter_dimension=1, tiled=True)  166 us
    reduce_scatter x1, waiting for transfers between devices, per_device(): lax.psum_scatter(down_grad, 'dp', scatter_dimension=1, tiled=True)  164 us
    all_to_all x1, local copies, waits for them, and re-layouts, per_device(): lax.all_to_all(grad_packed[:, None], 'head', split_axis=4, concat_axis=1,...  90.3 us
    reduce_scatter x1, waiting for transfers between devices, per_device(): lax.psum_scatter(qkv_grad, 'dp', scatter_dimension=1, tiled=True)  89.6 us
    another operation x4, local copies, waits for them, and re-layouts, block_backward(): return jnp.stack([grad_query, grad_key, grad_value]).astype(jnp.bfloat16)  65.8 us
  transfers between devices with their start and end apart: 12, of which 11 were waited for; matrix products, arithmetic and copies ran while one was open for 24% of the time, Pallas kernels for 0%

commit v1 on v0

v1 whole, which is shorter than its diff:
```python
import functools

import jax
import jax.numpy as jnp
from jax import lax
from jax.experimental import pallas as pl
from jax.experimental.pallas import tpu as pltpu
from jax.sharding import PartitionSpec as P

D = 768
HEADS = 12
HDIM = 64
FF = 3072
SLOT = 1024
EPSILON = 1e-06
BF = jnp.bfloat16
F32 = jnp.float32
FAR = -1e30
VMEM_LIMIT = 60 * 1024 * 1024


def nn(a, b):
    return lax.dot_general(a, b, (((1,), (0,)), ((), ())), preferred_element_type=F32)


def nt(a, b):
    return lax.dot_general(a, b, (((1,), (1,)), ((), ())), preferred_element_type=F32)


def tn(a, b):
    return lax.dot_general(a, b, (((0,), (0,)), ((), ())), preferred_element_type=F32)


def norm_parts(values, norm_gain, norm_shift):
    average = jnp.mean(values, axis=-1, keepdims=True)
    centered = values - average
    variance = jnp.mean(centered * centered, axis=-1, keepdims=True)
    inverse = lax.rsqrt(variance + EPSILON)
    unit = centered * inverse
    return unit, inverse, unit * norm_gain + norm_shift


def norm_back(grad_normed, unit, inverse, norm_gain):
    grad_unit = grad_normed * norm_gain
    first_mean = jnp.mean(grad_unit, axis=-1, keepdims=True)
    second_mean = jnp.mean(grad_unit * unit, axis=-1, keepdims=True)
    return inverse * (grad_unit - first_mean - unit * second_mean)


def gelu_parts(values):
    cumulative = 0.5 + 0.5 * lax.erf(values * 0.7071067811865476)
    density = jnp.exp(values * values * -0.5) * 0.3989422804014327
    return values * cumulative, cumulative + values * density


def lanes_of(width=256):
    return lax.broadcasted_iota(jnp.int32, (1, width), 1)


def head_mask(head):
    lane = lanes_of()
    return jnp.where((lane >= head * HDIM) & (lane < (head + 1) * HDIM), 1.0, 0.0)


def lane_is(index):
    return jnp.where(lanes_of() == index, 1.0, 0.0)


def split_three(column):
    high = column.astype(BF).astype(F32)
    rest = column - high
    middle = rest.astype(BF).astype(F32)
    return high, middle, rest - middle


def attend_forward(normed, weight, bias, lengths, q_ref, k_ref, v_ref, mixed_ref, exact_ref, lse_ref):
    whole = lengths[:, 0:1] == SLOT
    total = jnp.sum(lengths, axis=1, keepdims=True)
    onlane = lanes_of()
    aux_k = jnp.where((onlane >= 196) & (onlane < 199), 1.0, 0.0)
    aux_v = jnp.where((onlane >= 192) & (onlane < 199) & (onlane != 195), 1.0, 0.0)
    for block in range(4):
        rows = pl.ds(block * 256, 256)
        projected = nn(normed[rows, :], weight[...]) + bias
        projected = projected.astype(BF).astype(F32)
        q_ref[rows, :] = (projected[:, :256] * 0.125 + lane_is(192 + block)).astype(BF)
        other = jnp.where((onlane >= 192) & (onlane < 196) & (onlane != 192 + block), 1.0, 0.0)
        far = other * jnp.where(whole, 0.0, FAR)
        k_ref[rows, :] = (projected[:, 256:512] + (aux_k + far)).astype(BF)
        v_ref[rows, :] = (projected[:, 512:] + aux_v).astype(BF)
    on_aux = jnp.where(onlane >= 192, 1.0, 0.0)

    def block_step(block, carry):
        rows = pl.ds(pl.multiple_of(block * 256, 256), 256)
        queries = q_ref[rows, :]
        mixed = jnp.zeros((256, 256), F32)
        tops = []
        for head in range(3):
            scores = nt(queries * (head_mask(head) + on_aux).astype(BF), k_ref[...])
            top = jnp.max(scores, axis=1, keepdims=True)
            weights = jnp.exp(scores - top).astype(BF)
            mixed += nn(weights, v_ref[...] * (head_mask(head) + lane_is(192 + head)).astype(BF))
            tops.append(top)
        lse = jnp.zeros((256, 128), F32)
        scale = jnp.zeros((256, 256), F32)
        small = lax.broadcasted_iota(jnp.int32, (1, 128), 1)
        for head in range(3):
            row_sum = jnp.sum(mixed * lane_is(192 + head), axis=1, keepdims=True)
            lse += (tops[head] + jnp.log(row_sum)) * jnp.where(small == head, 1.0, 0.0)
            scale += (1.0 / row_sum) * head_mask(head)
        mixed = mixed * scale
        position = block * 256 + lax.broadcasted_iota(jnp.int32, (256, 1), 0)
        on_heads = jnp.where(onlane < 192, 1.0, 0.0)
        mixed = jnp.where(position < total, mixed, v_ref[rows, :].astype(F32) * on_heads)
        exact_ref[rows, :] = mixed
        mixed_ref[rows, :] = mixed[:, :192].astype(BF)
        lse_ref[rows, :] = lse
        return carry

    lax.fori_loop(0, 4, block_step, 0)


def attend_backward(q_ref, k_ref, v_ref, exact_ref, lse_ref, grad_mixed, q_aug, g_aug, scores_low, dq_acc, dk_acc, dv_acc):
    for head in range(3):
        mask = head_mask(head)

        def augment(block, carry):
            rows = pl.ds(pl.multiple_of(block * 256, 256), 256)
            grads = grad_mixed[rows, :].astype(F32) * mask
            inner = jnp.sum(grads * exact_ref[rows, :], axis=1, keepdims=True)
            lse = lse_ref[rows, :][:, head : head + 1]
            queries = q_ref[rows, :].astype(F32) * (mask + jnp.where(lanes_of() >= 192, 1.0, 0.0))
            for place, part in enumerate(split_three(-lse)):
                queries = queries + part * lane_is(196 + place)
            for place, part in enumerate(split_three(-inner)):
                grads = grads + part * lane_is(196 + place)
            q_aug[rows, :] = queries.astype(BF)
            g_aug[rows, :] = grads.astype(BF)
            return carry

        lax.fori_loop(0, 4, augment, 0)

        def block_step(block, carry):
            rows = pl.ds(pl.multiple_of(block * 256, 256), 256)
            probs = jnp.exp(nt(k_ref[rows, :], q_aug[...]))
            grad_probs = nt(v_ref[rows, :], g_aug[...])
            grad_scores = (probs * grad_probs).astype(BF)
            scores_low[rows, :] = grad_scores
            key_part = nn(grad_scores, q_aug[...]) * mask
            value_part = nn(probs.astype(BF), g_aug[...]) * mask
            if head == 0:
                dk_acc[rows, :] = key_part
                dv_acc[rows, :] = value_part
            else:
                dk_acc[rows, :] += key_part
                dv_acc[rows, :] += value_part
            return carry

        lax.fori_loop(0, 4, block_step, 0)
        query_part = tn(scores_low[...], k_ref[...] * mask.astype(BF)) * 0.125
        if head == 0:
            dq_acc[...] = query_part
        else:
            dq_acc[...] += query_part


def forward_kernel(normed, weight, bias, lengths, q_ref, k_ref, v_ref, mixed_ref, exact_ref, lse_ref):
    attend_forward(normed, weight, bias[...], lengths[...], q_ref, k_ref, v_ref, mixed_ref, exact_ref, lse_ref)


def middle_kernel(
    mixed_in, x_in, d_low, w_out, w_up, w_down, gains, shifts, biases, up_bias,
    block_ref, second_ref, hid_ref, low_ref, sums_ref, mixed_rows, act_ref,
):
    rows = x_in.shape[0]
    for group in range(4):
        mixed_rows[:, group * 192 : (group + 1) * 192] = mixed_in[group]
    hidden = x_in[...].astype(F32) + nn(mixed_rows[...], w_out[...]) + biases[0:1, :]
    unit, inverse, normed = norm_parts(hidden, gains[1:2, :], shifts[1:2, :])
    second = normed.astype(BF)
    second_ref[...] = second
    grad_low = d_low[...]
    down = jnp.zeros((rows, D), F32)
    back = jnp.zeros((rows, D), F32)
    step = 768
    for tile in range(FF // step):
        cut = slice(tile * step, (tile + 1) * step)
        up = nn(second, w_up[:, cut]) + up_bias[:, cut]
        value, slope = gelu_parts(up)
        down += nn(value.astype(BF), w_down[cut, :])
        grad_up = nt(grad_low, w_down[cut, :]) * slope
        back += nt(grad_up.astype(BF), w_up[:, cut])
    block_ref[...] = (hidden + down + biases[1:2, :]).astype(BF)
    grad_block = grad_low.astype(F32)
    grad_hidden = grad_block + norm_back(back, unit, inverse, gains[1:2, :])
    hid_ref[...] = grad_hidden
    low_ref[...] = grad_hidden.astype(BF)
    sums_ref[...] = jnp.zeros_like(sums_ref)
    sums_ref[0:1, :] = jnp.sum(back * unit, axis=0, keepdims=True)
    sums_ref[1:2, :] = jnp.sum(back, axis=0, keepdims=True)
    sums_ref[2:3, :] = jnp.sum(grad_hidden, axis=0, keepdims=True)
    sums_ref[3:4, :] = jnp.sum(grad_block, axis=0, keepdims=True)


def feed_kernel(second, d_low, w_up, w_down, up_bias, up_grad, down_grad, bias_grad, act_ref, grad_ref):
    width = w_up.shape[1]
    bias_grad[...] = jnp.zeros_like(bias_grad)

    def step(block, carry):
        rows = pl.ds(pl.multiple_of(block * 256, 256), 256)
        up = nn(second[rows, :], w_up[...]) + up_bias[...]
        value, slope = gelu_parts(up)
        act_ref[rows, :] = value.astype(BF)
        grad_up = nt(d_low[rows, :], w_down[...]) * slope
        bias_grad[0:1, :] += jnp.sum(grad_up, axis=0, keepdims=True)
        grad_ref[rows, :] = grad_up.astype(BF)
        return carry

    lax.fori_loop(0, 4, step, 0)
    down_grad[...] = tn(d_low[...], act_ref[...]).astype(BF)
    up_grad[...] = tn(grad_ref[...], second[...]).astype(BF)


def backward_kernel(
    grad_low, w_out, normed, mixed, q_ref, k_ref, v_ref, exact_ref, lse_ref,
    grad_ref, out_grad, qkv_grad, bias_grad,
    grad_mixed, q_aug, g_aug, scores_low, dq_acc, dk_acc, dv_acc,
):
    padded = jnp.zeros((64, D), BF)
    weight = jnp.concatenate([w_out[...], padded], axis=0)
    grad_mixed[...] = nt(grad_low[...], weight).astype(BF)
    out_grad[...] = tn(grad_low[...], mixed[...]).astype(BF)
    attend_backward(q_ref, k_ref, v_ref, exact_ref, lse_ref, grad_mixed, q_aug, g_aug, scores_low, dq_acc, dk_acc, dv_acc)
    for place, part in enumerate((dq_acc, dk_acc, dv_acc)):
        grad_ref[:, place * 192 : (place + 1) * 192] = part[:, :192].astype(BF)
    bias_grad[...] = jnp.zeros_like(bias_grad)
    bias_grad[0:1, :] = jnp.sum(grad_ref[...].astype(F32), axis=0, keepdims=True)
    qkv_grad[...] = tn(grad_ref[...], normed[...]).astype(BF)


def last_kernel(grad_in, w_qkv, x_in, hid, gains, shifts, out_ref, sums_ref, grad_rows):
    for part in range(3):
        for group in range(4):
            place = part * D + group * 192
            grad_rows[:, place : place + 192] = grad_in[group][:, part * 192 : (part + 1) * 192]
    grad_first = nt(grad_rows[...], w_qkv[...])
    unit, inverse, _ = norm_parts(x_in[...].astype(F32), gains[0:1, :], shifts[0:1, :])
    out_ref[...] = hid[...] + norm_back(grad_first, unit, inverse, gains[0:1, :])
    sums_ref[...] = jnp.zeros_like(sums_ref)
    sums_ref[0:1, :] = jnp.sum(grad_first * unit, axis=0, keepdims=True)
    sums_ref[1:2, :] = jnp.sum(grad_first, axis=0, keepdims=True)


def whole_call(kernel, outs, scratch=(), name=None):
    return pl.pallas_call(
        kernel,
        out_shape=[jax.ShapeDtypeStruct(*out) for out in outs],
        scratch_shapes=[pltpu.VMEM(*item) for item in scratch],
        compiler_params=pltpu.CompilerParams(vmem_limit_bytes=VMEM_LIMIT),
        name=name,
    )


def per_device(x, norm_gains, norm_shifts, w_qkv, qv_bias, w_out, out_biases, w_up, up_bias, w_down, lengths, d_out):
    groups = lax.axis_size("head")
    shards = lax.axis_size("dp")
    group = lax.axis_index("head")
    rows = x.shape[1]
    own = D // groups
    x = x[0]
    gains = norm_gains.astype(F32)
    shifts = norm_shifts.astype(F32)
    biases = out_biases.astype(F32)
    up_shift = up_bias.astype(F32)
    full_bias = jnp.stack([qv_bias[0], jnp.zeros_like(qv_bias[0]), qv_bias[1]]).astype(F32)

    weight_own = lax.dynamic_index_in_dim(w_qkv.reshape(D, 3, groups, own), group, 2, False)
    weight_own = jnp.pad(weight_own, ((0, 0), (0, 0), (0, 256 - own))).reshape(D, 768)
    bias_own = lax.dynamic_index_in_dim(full_bias.reshape(3, groups, own), group, 1, False)
    bias_own = jnp.pad(bias_own, ((0, 0), (0, 256 - own))).reshape(1, 768)
    out_own = lax.dynamic_slice_in_dim(w_out, group * own, own, 0)
    unit_ff = FF // (shards * groups)
    up_own = lax.dynamic_index_in_dim(w_up.reshape(D, shards, groups, unit_ff), group, 2, False).reshape(D, D)
    down_own = lax.dynamic_index_in_dim(w_down.reshape(shards, groups, unit_ff, D), group, 1, False).reshape(D, D)
    ub_own = lax.dynamic_index_in_dim(up_shift.reshape(shards, groups, unit_ff), group, 1, False).reshape(1, D)

    normed = norm_parts(x.astype(F32), gains[0], shifts[0])[2].astype(BF)
    normed_all = lax.all_gather(normed, "head", axis=0, tiled=True)
    total = jnp.sum(lengths[0])
    position = group * rows + jnp.arange(rows, dtype=jnp.int32)
    d_low = jnp.where((position < total)[:, None], d_out[0], jnp.zeros_like(d_out[0]))
    d_all = lax.all_gather(d_low, "head", axis=0, tiled=True)

    q, k, v, mixed, exact, lse = whole_call(
        forward_kernel,
        [((SLOT, 256), BF)] * 3 + [((SLOT, own), BF), ((SLOT, 256), F32), ((SLOT, 128), F32)],
        name="attend_forward",
    )(normed_all, weight_own, bias_own, lengths)
    mixed_in = lax.all_to_all(mixed.reshape(groups, rows, own), "head", 0, 0, tiled=True)
    block_out, second, hid, hid_low, sums_mid = whole_call(
        middle_kernel,
        [((rows, D), BF), ((rows, D), BF), ((rows, D), F32), ((rows, D), BF), ((8, D), F32)],
        [((rows, D), BF), ((rows, FF), BF)],
        name="middle",
    )(mixed_in, x, d_low, w_out, w_up, w_down, gains, shifts, biases, up_shift.reshape(1, FF))
    second_all = lax.all_gather(second, "head", axis=0, tiled=True)
    low_all = lax.all_gather(hid_low, "head", axis=0, tiled=True)
    up_grad, down_grad, ub_grad = whole_call(
        feed_kernel,
        [((D, D), BF), ((D, D), BF), ((8, D), F32)],
        [((SLOT, D), BF), ((SLOT, D), BF)],
        name="feed",
    )(second_all, d_all, up_own, down_own, ub_own)
    grad_own, out_grad, qkv_grad, qkv_sum = whole_call(
        backward_kernel,
        [((SLOT, 3 * own), BF), ((D, own), BF), ((3 * own, D), BF), ((8, 3 * own), F32)],
        [((SLOT, 256), BF)] * 3 + [((SLOT, SLOT), BF)] + [((SLOT, 256), F32)] * 3,
        name="attend_backward",
    )(low_all, out_own, normed_all, mixed, q, k, v, exact, lse)
    grad_in = lax.all_to_all(grad_own.reshape(groups, rows, 3 * own), "head", 0, 0, tiled=True)
    grad_inputs, sums_last = whole_call(
        last_kernel,
        [((rows, D), F32), ((8, D), F32)],
        [((rows, 3 * D), BF)],
        name="last",
    )(grad_in, w_qkv, x, hid, gains, shifts)

    def scatter(values):
        return lax.psum_scatter(values, "dp", scatter_dimension=0, tiled=True)

    up_part = lax.all_gather(scatter(up_grad), "head", axis=0, tiled=True)
    down_part = lax.all_gather(scatter(down_grad), "head", axis=1, tiled=True)
    out_part = lax.all_gather(scatter(out_grad), "head", axis=1, tiled=True)
    down_out = down_part.astype(F32).T.reshape(groups, shards, unit_ff, D // shards)
    down_out = down_out.transpose(1, 0, 2, 3).reshape(FF, D // shards)
    spread = jnp.zeros((3, groups, own, D), BF)
    spread = lax.dynamic_update_slice(spread, qkv_grad.reshape(3, 1, own, D), (0, group, 0, 0))
    qkv_part = lax.psum(scatter(spread.reshape(3 * D, D)), "head")

    def place_rows(values):
        parts = values.reshape(3, own)
        empty = jnp.zeros((3, groups, own), F32)
        return lax.dynamic_update_slice(empty, parts[:, None], (0, group, 0)).reshape(3, D)

    bias_rows = place_rows(qkv_sum[0])
    ub_rows = lax.dynamic_update_slice(
        jnp.zeros((shards, groups, unit_ff), F32), ub_grad[0].reshape(shards, 1, unit_ff), (0, group, 0)
    ).reshape(4, D)
    small = jnp.concatenate([sums_last[0:2], sums_mid[0:4], bias_rows[0:1], bias_rows[2:3], ub_rows], axis=0)
    small = lax.psum(small, ("dp", "head"))
    shard = lax.axis_index("dp")

    def cut(values):
        width = D // shards
        return lax.dynamic_slice_in_dim(values, shard * width, width, 1)

    ub_out = lax.dynamic_slice_in_dim(small[8:12].reshape(FF), shard * (FF // shards), FF // shards, 0)
    return (
        block_out[None],
        grad_inputs[None],
        cut(jnp.stack([small[0], small[2]])),
        cut(jnp.stack([small[1], small[3]])),
        qkv_part.astype(F32).T,
        cut(small[6:8]),
        out_part.astype(F32).T,
        cut(small[4:6]),
        up_part.astype(F32).T,
        ub_out,
        down_out,
    )


def solution(mesh):
    split = P("dp", "head", None)
    placed = (split,) + (P(),) * 9 + (P("dp", None), split)
    return jax.shard_map(
        per_device,
        mesh=mesh,
        in_specs=placed,
        out_specs=(split, split) + (P(None, "dp"),) * 7 + (P("dp"), P(None, "dp")),
        check_vma=False,
    )
```

time: 1850 us -> 460 us (0.25)
  local copies, waits for them, and re-layouts: 587 us -> 42.8 us
  waiting for transfers between devices: 695 us -> 249 us
  other arithmetic: 401 us -> 12.6 us
  matrix products: 70.8 us -> 0 us
  Pallas kernels: 0 us -> 60 us
    unnamed x4 -> x0, other arithmetic: 356 us -> none
    unnamed x124 -> x27, local copies, waits for them, and re-layouts: 282 us -> 16.6 us
    reduce_scatter x4, waiting for transfers between devices: 420 us -> 175 us  [scatter(): return lax.psum_scatter(values, 'dp', scatter_dimension=0, tiled=True)]
    unnamed x13 -> x9, waiting for transfers between devices: 215 us -> 2 us
    all_to_all x4 -> x2, local copies, waits for them, and re-layouts: 153 us -> 2.43 us  [the longest x1 1.43 us: per_device(): lax.all_to_all(grad_own.reshape(groups, rows, 3 * own), 'head', 0, 0, til...]
    another operation x20 -> x5, local copies, waits for them, and re-layouts: 79.5 us -> 0.39 us  [the longest x3 0.24 us: per_device(): jnp.stack([qv_bias[0], jnp.zeros_like(qv_bias[0]), qv_bias[1]]).astype(F32)]
    dot_general x17 -> x0, matrix products: 67.1 us -> none  [the longest x1 11.7 us: per_device(): jnp.dot(normed_two, w_up, preferred_element_type=jnp.float32) + up_shift]
    pallas_call x0 -> x5, Pallas kernels: none -> 60 us  [the longest x1 21.2 us: per_device(): whole_call(backward_kernel, [((SLOT, 3 * own), BF), ((D, own), BF), ((3 *...]
  transfers between devices with their start and end apart: 12 -> 11, of which waited for: 11 -> 9; matrix products, arithmetic and copies ran while one was open for 24% -> 9% of each run, Pallas kernels for 0% -> 8%
where the time goes in v1:
time: 460 us; the launch traced here: 455 us
  waiting for transfers between devices  249 us (54%)
  blocking collectives  65.7 us (14%)
  Pallas kernels  60 us (13%)
  local copies, waits for them, and re-layouts  42.8 us (9%)
  between operations  14.1 us (3%)
  other arithmetic  12.6 us (3%)
  starting transfers between devices  10.8 us (2%)
    reduce_scatter x4, waiting for transfers between devices, scatter(): return lax.psum_scatter(values, 'dp', scatter_dimension=0, tiled=True)  175 us
    psum x1, blocking collectives, per_device(): small = lax.psum(small, ('dp', 'head'))  39.2 us
    psum x1, waiting for transfers between devices, per_device(): qkv_part = lax.psum(scatter(spread.reshape(3 * D, D)), 'head')  31.9 us
    pallas_call x1, Pallas kernels, per_device(): whole_call(backward_kernel, [((SLOT, 3 * own), BF), ((D, own), BF), ((3 *...  21.2 us
    all_gather x1, waiting for transfers between devices, per_device(): low_all = lax.all_gather(hid_low, 'head', axis=0, tiled=True)  16.9 us
    unnamed x27, local copies, waits for them, and re-layouts  16.6 us
    all_gather x1, waiting for transfers between devices, per_device(): normed_all = lax.all_gather(normed, 'head', axis=0, tiled=True)  12.5 us
    pallas_call x1, Pallas kernels, per_device(): whole_call(forward_kernel, [((SLOT, 256), BF)] * 3 + [((SLOT, own), BF),...  12.2 us
  transfers between devices with their start and end apart: 11, of which 9 were waited for; matrix products, arithmetic and copies ran while one was open for 9% of the time, Pallas kernels for 8%

profile of v1, /device:TPU:3, one launch (start us, length us, event | category | flops | bytes accessed | tf_op | source)
XLA Modules:
  0.0 455.2 jit_solution(4823490220315743047)
XLA Ops:
  11.0 2.0 fusion.5
  14.0 4.5 copy.40
  18.8 1.5 copy.41.weight
  20.8 12.5 %all-gather.5.cloned.1.call-done.normed = bf16[1024,768]{1,0:T(8,128)(2,1)} async-done(((bf16[256,768]{1,0:T(8,128)(2,1)}), bf16[1024,768]{1,0:T(8,128)(2,1)}) %all-gather.5.cloned.1.call-update) | async-done | bytes 1572880 | tf_op jit(solution)/shard_map/all_gather | solution.py:288
  33.4 12.2 %attend_forward.1 = (bf16[1024,256]{1,0:T(8,128)(2,1)}, bf16[1024,256]{1,0:T(8,128)(2,1)}, bf16[1024,256]{1,0:T(8,128)(2,1)}, bf16[1024,192]{1,0:T(8,128)(2,1)},...) custom-call(bf16[1024,768]{1,0:T(8,128)(2,1)} %all-gather.5.cloned.1.call-done.normed, bf16[768,768]{1,0:T(8,128)(2,1)} %copy.41.weight, ...), custom_call_target="tpu_custom_call" | custom-call | tf_op jit(solution)/shard_map/attend_forward/pallas_call | solution.py:294
  45.5 2.0 copy.42
  47.6 5.0 %all-to-all-start = ((bf16[4,256,192]{1,2,0:T(8,128)(2,1)}), bf16[4,256,192]{1,2,0:T(8,128)(2,1)S(1)}, u32[]{:S(2)}, u32[]{:S(2)}) async-start(bf16[4,256,192]{1,2,0:T(8,128)(2,1)} %copy.42), calls=%async_computation | async-start | bytes 786432 | tf_op jit(solution)/shard_map/all_to_all | solution.py:299
  55.4 2.8 all-to-all-done
  59.2 12.0 %middle.1 = (bf16[256,768]{1,0:T(8,128)(2,1)}, bf16[256,768]{1,0:T(8,128)(2,1)}, f32[256,768]{1,0:T(8,128)}, bf16[256,768]{1,0:T(8,128)(2,1)}, f32[8,768]{1,0:T(8,128)}) custom-call(bf16[4,256,192]{2,1,0:T(8,128)(2,1)} %copy.43.mixed_in, bf16[256,768]{1,0:T(8,128)(2,1)} %bitcast.47, bf16[256,768]{1,0:T(8,128)(2,1)} %bitcast_select_fusion.d_low, ...), custom_call_target="tpu_custom_call" | custom-call | tf_op jit(solution)/shard_map/middle/pallas_call | solution.py:300
  72.7 1.7 constant_dynamic-slice_fusion.4.w_out
  74.4 16.9 %all-gather.7.cloned.1.call-done.grad_low = bf16[1024,768]{1,0:T(8,128)(2,1)} async-done(((bf16[256,768]{1,0:T(8,128)(2,1)}), bf16[1024,768]{1,0:T(8,128)(2,1)}) %all-gather.7.cloned.1.call-update) | async-done | bytes 1572880 | tf_op jit(solution)/shard_map/all_gather | solution.py:307
  91.3 21.2 %attend_backward.1 = (bf16[1024,576]{1,0:T(8,128)(2,1)}, bf16[768,192]{1,0:T(8,128)(2,1)}, bf16[576,768]{1,0:T(8,128)(2,1)}, f32[8,576]{1,0:T(8,128)}) custom-call(bf16[1024,768]{1,0:T(8,128)(2,1)} %all-gather.7.cloned.1.call-done.grad_low, bf16[192,768]{1,0:T(8,128)(2,1)} %constant_dynamic-slice_fusion.4.w_out, ...), custom_call_target="tpu_custom_call" | custom-call | tf_op jit(solution)/shard_map/attend_backward/pallas_call | solution.py:314
  112.6 6.7 %copy.47 = bf16[768,3072]{0,1:T(8,128)(2,1)} copy(bf16[768,3072]{1,0:T(8,128)(2,1)} %w_up.1) | data formatting | bytes 9437184 | tf_op args[7]
  120.7 1.5 copy.49.w_up
  122.8 2.4 constant_dynamic-slice_fusion.2
  125.2 8.4 %all-gather.9.cloned.1.call-done.second = bf16[1024,768]{1,0:T(8,128)(2,1)} async-done(((bf16[256,768]{1,0:T(8,128)(2,1)}), bf16[1024,768]{1,0:T(8,128)(2,1)}) %all-gather.9.cloned.1.call-update) | async-done | bytes 1572880 | tf_op jit(solution)/shard_map/all_gather | solution.py:306
  133.7 9.5 %feed.1 = (bf16[768,768]{1,0:T(8,128)(2,1)}, bf16[768,768]{1,0:T(8,128)(2,1)}, f32[8,768]{1,0:T(8,128)}) custom-call(bf16[1024,768]{1,0:T(8,128)(2,1)} %all-gather.9.cloned.1.call-done.second, bf16[1024,768]{1,0:T(8,128)(2,1)} %all-gather.11.cloned.1.call-done.d_low, bf16[768,768]{1,0:T(8,128)(2,1)} %copy.49.w_up, bf16[768,768]{1,0:T(8,128)(2,1)} %bitcast.55, ...), custom_call_target="tpu_custom_call" | custom-call | tf_op jit(solution)/shard_map/feed/pallas_call | solution.py:308
  145.2 1.7 copy-done
  147.0 2.4 copy.44
  149.4 5.3 %all-to-all-start.1 = ((bf16[4,256,576]{1,2,0:T(8,128)(2,1)}), bf16[4,256,576]{1,2,0:T(8,128)(2,1)S(1)}, u32[]{:S(2)}, u32[]{:S(2)}) async-start(bf16[4,256,576]{1,2,0:T(8,128)(2,1)} %copy.44), calls=%async_computation.1 | async-start | bytes 2359296 | tf_op jit(solution)/shard_map/all_to_all | solution.py:320
  156.7 40.4 %reduce-scatter.7.cloned.1.call-done = bf16[96,192]{1,0:T(8,128)(2,1)} async-done(((bf16[768,192]{1,0:T(8,128)(2,1)}), bf16[96,192]{1,0:T(8,128)(2,1)}) %reduce-scatter.7.cloned.1.call-update) | async-done | bytes 36880 | tf_op jit(solution)/shard_map/reduce_scatter | solution.py:329
  198.0 8.3 %all_gather.25 = bf16[96,768]{0,1:T(8,128)(2,1)S(1)} all-gather(bf16[96,192]{0,1:T(8,128)(2,1)S(1)} %copy.52), channel_id=1, replica_groups=mesh['dp'=8,'head'=4] {'head'}, dimensions={1}, use_global_device_ids=true | all-gather | bytes 184320 | tf_op jit(solution)/shard_map/all_gather | solution.py:333
  208.6 5.1 %last.1 = (f32[256,768]{1,0:T(8,128)}, f32[8,768]{1,0:T(8,128)}) custom-call(bf16[4,256,576]{2,1,0:T(8,128)(2,1)} %copy.45.grad_in, bf16[768,2304]{1,0:T(8,128)(2,1)} %w_qkv.1, bf16[256,768]{1,0:T(8,128)(2,1)} %bitcast.48, f32[256,768]{1,0:T(8,128)} %get-tuple-element.40.hid, f32[2,768]{1,0:T(2,128)} %copy-done.3, f32[2,768]{1,0:T(2,128)} %copy-done.4), custom_call_target="tpu_custom_call" | custom-call | tf_op jit(solution)/shard_map/last/pallas_call | solution.py:321
  214.5 39.2 %psum.14 = f32[12,768]{1,0:T(8,128)S(1)} all-reduce(f32[12,768]{1,0:T(8,128)S(1)} %concatenate.4), channel_id=1, replica_groups=mesh['dp'=8,'head'=4] {'dp','head'}, use_global_device_ids=true, to_apply=%region_3.4 | all-reduce | flops 9216 | bytes 73728 | tf_op jit(solution)/shard_map/psum | solution.py:350
  256.9 6.7 %reduce-scatter.11.cloned.1.call-done = bf16[96,768]{1,0:T(8,128)(2,1)} async-done(((bf16[768,768]{1,0:T(8,128)(2,1)}), bf16[96,768]{1,0:T(8,128)(2,1)}) %reduce-scatter.11.cloned.1.call-update) | async-done | bytes 147472 | tf_op jit(solution)/shard_map/reduce_scatter | solution.py:329
  263.6 9.2 %all_gather.27 = bf16[96,3072]{1,0:T(8,128)(2,1)S(1)} all-gather(bf16[96,768]{1,0:T(8,128)(2,1)} %reduce-scatter.11.cloned.1.call-done), channel_id=1, replica_groups=mesh['dp'=8,'head'=4] {'head'}, dimensions={1}, use_global_device_ids=true | all-gather | bytes 737280 | tf_op jit(solution)/shard_map/all_gather | solution.py:332
  273.9 2.6 reshape.127
  276.6 53.5 %reduce-scatter.9.cloned.1.call-done = bf16[96,768]{1,0:T(8,128)(2,1)} async-done(((bf16[768,768]{1,0:T(8,128)(2,1)}), bf16[96,768]{1,0:T(8,128)(2,1)}) %reduce-scatter.9.cloned.1.call-update) | async-done | bytes 147472 | tf_op jit(solution)/shard_map/reduce_scatter | solution.py:329
  330.1 9.1 %all_gather.26 = bf16[384,768]{1,0:T(8,128)(2,1)S(1)} all-gather(bf16[96,768]{1,0:T(8,128)(2,1)} %reduce-scatter.9.cloned.1.call-done), channel_id=1, replica_groups=mesh['dp'=8,'head'=4] {'head'}, dimensions={0}, use_global_device_ids=true | all-gather | bytes 737280 | tf_op jit(solution)/shard_map/all_gather | solution.py:331
  339.2 74.1 %reduce-scatter.5.cloned.1.call-done = bf16[288,768]{1,0:T(8,128)(2,1)} async-done(((bf16[2304,768]{1,0:T(8,128)(2,1)}), bf16[288,768]{1,0:T(8,128)(2,1)}) %reduce-scatter.5.cloned.1.call-update) | async-done | bytes 442384 | tf_op jit(solution)/shard_map/reduce_scatter | solution.py:329
  414.8 31.9 %all-reduce.4.cloned.1.call-done = bf16[768,288]{0,1:T(8,128)(2,1)} async-done(((bf16[768,288]{0,1:T(8,128)(2,1)}), bf16[768,288]{0,1:T(8,128)(2,1)}) %all-reduce.4.cloned.1.call-update) | async-done | bytes 442384 | tf_op jit(solution)/shard_map/psum | solution.py:338
  446.7 2.0 transpose.32
  (101 shorter events, 26.9 us)
Async XLA Ops:
  7.2 5.9 %copy-start.6 = (bf16[2,768]{1,0:T(2,128)(2,1)S(1)}, bf16[2,768]{1,0:T(2,128)(2,1)}, u32[]{:S(2)}) copy-start(bf16[2,768]{1,0:T(2,128)(2,1)} %param.16) | copy-start | bytes 9220
  7.2 26.2 %all-gather.5.cloned.1.call-start = ((), (), s32[]{:S(2)}) async-start(), calls=%async_computation.6 | async-start | bytes 1966080 | tf_op jit(solution)/shard_map/all_gather | solution.py:288
  7.9 10.6 %copy-start.3 = (f32[2,768]{1,0:T(2,128)}, f32[2,768]{1,0:T(2,128)S(1)}, u32[]{:S(2)}) copy-start(f32[2,768]{1,0:T(2,128)S(1)} %convert_element_type.31.gains) | copy-start | bytes 18436
  8.6 10.0 %copy-start.4 = (f32[2,768]{1,0:T(2,128)}, f32[2,768]{1,0:T(2,128)S(1)}, u32[]{:S(2)}) copy-start(f32[2,768]{1,0:T(2,128)S(1)} %convert_element_type.32.shifts) | copy-start | bytes 18436
  18.7 1.5 copy-start.9
  45.5 7.8 %copy-start.5 = (bf16[3072]{0:T(1024)(128)(2,1)S(1)}, bf16[3072]{0:T(1024)(128)(2,1)}, u32[]{:S(2)}) copy-start(bf16[3072]{0:T(1024)(128)(2,1)} %param.20) | copy-start | bytes 18436
  45.5 8.4 %copy-start.8 = (bf16[2,768]{1,0:T(2,128)(2,1)S(1)}, bf16[2,768]{1,0:T(2,128)(2,1)}, u32[]{:S(2)}) copy-start(bf16[2,768]{1,0:T(2,128)(2,1)} %param.18) | copy-start | bytes 9220
  45.5 9.0 %copy-start.2 = (bf16[1,256,768]{2,1,0:T(8,128)(2,1)S(1)}, bf16[1,256,768]{2,1,0:T(8,128)(2,1)}, u32[]{:S(2)}) copy-start(bf16[1,256,768]{2,1,0:T(8,128)(2,1)} %param.23) | copy-start | bytes 1179652
  47.6 10.6 %all-to-all-start = ((bf16[4,256,192]{1,2,0:T(8,128)(2,1)}), bf16[4,256,192]{1,2,0:T(8,128)(2,1)S(1)}, u32[]{:S(2)}, u32[]{:S(2)}) async-start(bf16[4,256,192]{1,2,0:T(8,128)(2,1)} %copy.42), calls=%async_computation | async-start | bytes 786432 | tf_op jit(solution)/shard_map/all_to_all | solution.py:299
  52.6 38.6 %all-gather.7.cloned.1.call-start = ((), (), s32[]{:S(2)}) async-start(), calls=%async_computation.7 | async-start | bytes 1966080 | tf_op jit(solution)/shard_map/all_gather | solution.py:307
  71.2 54.1 %all-gather.11.cloned.1.call-start = ((), (), s32[]{:S(2)}) async-start(), calls=%async_computation.9 | async-start | bytes 1966080 | tf_op jit(solution)/shard_map/all_gather | solution.py:292
  71.9 61.8 %all-gather.9.cloned.1.call-start = ((), (), s32[]{:S(2)}) async-start(), calls=%async_computation.8 | async-start | bytes 1966080 | tf_op jit(solution)/shard_map/all_gather | solution.py:306
  72.5 124.6 %reduce-scatter.7.cloned.1.call-start = ((), (), s32[]{:S(2)}) async-start(), calls=%async_computation.12 | async-start | bytes 442368 | tf_op jit(solution)/shard_map/reduce_scatter | solution.py:329
  112.5 151.1 %reduce-scatter.11.cloned.1.call-start = ((), (), s32[]{:S(2)}) async-start(), calls=%async_computation.14 | async-start | bytes 1327104 | tf_op jit(solution)/shard_map/reduce_scatter | solution.py:329
  143.2 187.0 %reduce-scatter.9.cloned.1.call-start = ((), (), s32[]{:S(2)}) async-start(), calls=%async_computation.13 | async-start | bytes 1327104 | tf_op jit(solution)/shard_map/reduce_scatter | solution.py:329
  143.9 269.4 %reduce-scatter.5.cloned.1.call-start = ((), (), s32[]{:S(2)}) async-start(), calls=%async_computation.10 | async-start | bytes 3981312 | tf_op jit(solution)/shard_map/reduce_scatter | solution.py:329
  144.0 1.2 copy-start.1
  145.2 1.7 copy-start
  149.4 5.3 %copy-start.7 = (f32[8,768]{1,0:T(8,128)S(1)}, f32[8,768]{1,0:T(8,128)}, u32[]{:S(2)}) copy-start(f32[8,768]{1,0:T(8,128)} %get-tuple-element.43) | copy-start | bytes 73732
  149.4 57.8 %all-to-all-start.1 = ((bf16[4,256,576]{1,2,0:T(8,128)(2,1)}), bf16[4,256,576]{1,2,0:T(8,128)(2,1)S(1)}, u32[]{:S(2)}, u32[]{:S(2)}) async-start(bf16[4,256,576]{1,2,0:T(8,128)(2,1)} %copy.44), calls=%async_computation.1 | async-start | bytes 2359296 | tf_op jit(solution)/shard_map/all_to_all | solution.py:320
  154.6 292.0 %all-reduce.4.cloned.1.call-start = ((), (), s32[]{:S(2)}) async-start(), calls=%async_computation.11 | async-start | bytes 884736 | tf_op jit(solution)/shard_map/psum | solution.py:338
Sparse Core Ops, SparseCore 0:
  13.2 20.1 all-gather.4
  71.3 19.9 all-gather.6
  92.8 19.6 all-gather.10
  113.9 19.6 all-gather.8
  136.8 60.2 reduce-scatter.6
  200.3 63.2 reduce-scatter.10
  267.0 63.0 reduce-scatter.8
  333.8 79.4 reduce-scatter.4
  415.7 30.9 all-reduce.3

commit v2 on v1

--- a/solution.py
+++ b/solution.py
@@ -16,7 +16,7 @@
 BF = jnp.bfloat16
 F32 = jnp.float32
 FAR = -1e30
-VMEM_LIMIT = 60 * 1024 * 1024
+VMEM_LIMIT = 63 * 1024 * 1024
 
 
 def nn(a, b):
@@ -261,7 +261,7 @@
     )
 
 
-def per_device(x, norm_gains, norm_shifts, w_qkv, qv_bias, w_out, out_biases, w_up, up_bias, w_down, lengths, d_out):
+def general_device(x, norm_gains, norm_shifts, w_qkv, qv_bias, w_out, out_biases, w_up, up_bias, w_down, lengths, d_out):
     groups = lax.axis_size("head")
     shards = lax.axis_size("dp")
     group = lax.axis_index("head")
@@ -370,11 +370,713 @@
     )
 
 
+MESH = pl.DeviceIdType.MESH
+BLOCK = 256
+
+BUFFERS = (
+    ("xv", (256, D), BF),
+    ("dv", (256, D), BF),
+    ("wqkv", (D, 3 * D), BF),
+    ("wout", (D, D), BF),
+    ("wup", (D, FF), BF),
+    ("big", (3 * SLOT, SLOT), BF),
+    ("wqo", (D, D), BF),
+    ("wuo", (D, D), BF),
+    ("wdo", (D, D), BF),
+    ("woo", (256, D), BF),
+    ("nall", (SLOT, D), BF),
+    ("dall", (SLOT, D), BF),
+    ("sall", (SLOT, D), BF),
+    ("lall", (SLOT, D), BF),
+    ("qb", (SLOT, 256), BF),
+    ("kb", (SLOT, 256), BF),
+    ("vb", (SLOT, 256), BF),
+    ("mix", (SLOT, 256), BF),
+    ("exact", (SLOT, 256), F32),
+    ("lse", (SLOT, 128), F32),
+    ("mixin", (4, 256, 256), BF),
+    ("gh", (256, D), F32),
+    ("act", (SLOT, D), BF),
+    ("gup", (SLOT, D), BF),
+    ("gm", (SLOT, 256), BF),
+    ("dkv", (SLOT, 384), BF),
+    ("dq", (SLOT, 256), BF),
+    ("kvin", (4, 256, 384), BF),
+    ("qin", (4, 256, 256), BF),
+    ("pdn", (8, 96, D), BF),
+    ("pup", (6, 128, D), BF),
+    ("pou", (8, 96, 256), BF),
+    ("pqk", (6, 96, D), BF),
+    ("ydn", (4, 96, D), BF),
+    ("yup", (6, 128, D), BF),
+    ("you", (4, 96, 256), BF),
+    ("yqk", (6, 96, D), BF),
+    ("zdn", (4, 96, D), BF),
+    ("zup", (9, 128, D), BF),
+    ("zou", (4, 96, 256), BF),
+    ("zqk", (9, 96, D), BF),
+    ("vec", (8, D), F32),
+    ("small", (2, 4, 16, 128), F32),
+    ("ysm", (4, 16, 128), F32),
+    ("zsm", (4, 16, 128), F32),
+    ("fsm", (4, 16, 128), F32),
+)
+SEMAPHORES = (
+    ("load", 22),
+    ("ns", 5), ("nr", 5), ("ds", 5), ("dr", 5), ("ss", 5), ("sr", 5), ("ls", 5), ("lr", 5),
+    ("ms", 3), ("mr", 3), ("kvs", 3), ("kvr", 3), ("qs", 3), ("qr", 3),
+    ("ydns", 4), ("ydnr", 4), ("zdns", 4), ("zdnr", 4), ("fdns", 3), ("fdnr", 3),
+    ("yous", 4), ("your", 4), ("zous", 4), ("zour", 4), ("fous", 3), ("four", 3),
+    ("yups", 6), ("yupr", 6), ("zups", 6), ("zupr", 9), ("fups", 9), ("fupr", 9),
+    ("yqks", 6), ("yqkr", 6), ("zqks", 6), ("zqkr", 9), ("fqks", 9), ("fqkr", 9),
+    ("ysms", 1), ("ysmr", 1), ("zsms", 4), ("zsmr", 4), ("fsms", 3), ("fsmr", 3),
+)
+INPUTS = ("x", "gains", "shifts", "w_qkv", "full_bias", "w_out", "biases", "w_up", "up_bias", "w_down", "lengths", "d_out")
+IN_PLACE = ("x", "w_qkv", "w_out", "w_up", "w_down", "d_out")
+OUTPUTS = (
+    ("block_out", (256, D), BF),
+    ("grad_inputs", (256, D), F32),
+    ("fup", (3, 128, D), BF),
+    ("fqk", (3, 96, D), BF),
+    ("fdn", (4, 96, D), BF),
+    ("fou", (4, 96, 256), BF),
+    ("fsum", (16, 128), F32),
+)
+
+
+class Refs:
+    pass
+
+
+def block_rows(block, size=BLOCK, offset=0):
+    return pl.ds(pl.multiple_of(block * BLOCK + offset, 128), size)
+
+
+def one_kernel(*args):
+    r = Refs()
+    names = [*INPUTS] + [o[0] for o in OUTPUTS] + [b[0] for b in BUFFERS] + [s[0] for s in SEMAPHORES]
+    for name, ref in zip(names, args, strict=True):
+        setattr(r, name, ref)
+    dp, head = lax.axis_index("dp"), lax.axis_index("head")
+    z, y = lax.div(dp, 2), lax.rem(dp, 2)
+    px, pc = lax.div(head, 2), lax.rem(head, 2)
+
+    def peer(code):
+        return lax.rem(px + (code // 2 if isinstance(code, int) else lax.div(code, 2)), 2) * 2 + lax.rem(
+            pc + (code % 2 if isinstance(code, int) else lax.rem(code, 2)), 2
+        )
+
+    sib, far, diag = peer(1), peer(2), peer(3)
+    other_y = z * 2 + (1 - y)
+
+    def z_shard(k):
+        return lax.rem(z + k, 4)
+
+    sent = []
+
+    def push(src, dst, send, recv, to):
+        return pltpu.make_async_remote_copy(
+            src_ref=src, dst_ref=dst, send_sem=send, recv_sem=recv, device_id=to, device_id_type=MESH
+        )
+
+    def when(cond, body):
+        if cond is None:
+            body()
+        else:
+            pl.when(cond)(body)
+
+    def start(make, cond=None):
+        when(cond, lambda: make().start())
+        sent.append((make, cond))
+
+    loads = {}
+
+    def load(name, src, dst):
+        loads.setdefault(name, []).append(pltpu.make_async_copy(src, dst, r.load.at[sum(map(len, loads.values()))]))
+
+    load("x", r.x, r.xv)
+    load("d", r.d_out, r.dv)
+    load("wqkv", r.w_qkv, r.wqkv)
+    load("wout", r.w_out, r.wout)
+    load("wup", r.w_up, r.wup)
+    load("wdown", r.w_down, r.big.at[:, 0:D])
+    load("woo", r.w_out.at[pl.ds(pl.multiple_of(head * 192, 64), 192), :], r.woo.at[0:192, :])
+    for j in range(6):
+        unit = pl.ds(pl.multiple_of((4 * j + head) * 128, 128), 128)
+        load("wuo", r.w_up.at[:, unit], r.wuo.at[:, j * 128 : (j + 1) * 128])
+        load("wdo", r.w_down.at[unit, :], r.wdo.at[j * 128 : (j + 1) * 128, :])
+    for copies in loads.values():
+        for copy in copies:
+            copy.start()
+
+    def loaded(name):
+        for copy in loads[name]:
+            copy.wait()
+
+    barrier = pltpu.get_barrier_semaphore()
+    for to in [(dp, sib), (dp, far), (dp, diag), (other_y, head)] + [(z_shard(k) * 2 + y, head) for k in (1, 2, 3)]:
+        pl.semaphore_signal(barrier, inc=1, device_id=to, device_id_type=MESH)
+
+    gains = r.gains[...].astype(F32)
+    shifts = r.shifts[...].astype(F32)
+    biases = r.biases[...].astype(F32)
+    onlane = lanes_of()
+    lengths = r.lengths[...]
+    whole = lengths[:, 0:1] == SLOT
+    total = jnp.sum(lengths, axis=1, keepdims=True)
+
+    def gather(buf, send, recv):
+        def copy_of(index):
+            if index == 0:
+                rows, to = block_rows(head), sib
+            elif index < 3:
+                rows, to = block_rows(head, 128, (index - 1) * 128), far
+            else:
+                rows, to = block_rows(far, 128, (index - 3) * 128), sib
+            return push(buf.at[rows, :], buf.at[rows, :], send.at[index], recv.at[index], (dp, to))
+
+        def arrival(index):
+            return copy_of(index)
+
+        def begin():
+            for index in (1, 2, 0):
+                start(lambda index=index: copy_of(index))
+
+        def wait(index):
+            copy_of(index).wait_recv()
+
+        def relay():
+            for index in (1, 2):
+                wait(index)
+                start(lambda index=index: copy_of(index + 2))
+
+        def rest():
+            for index in (3, 4):
+                wait(index)
+
+        return begin, wait, relay, rest
+
+    n_begin, n_wait, n_relay, n_rest = gather(r.nall, r.ns, r.nr)
+    d_begin, d_wait, d_relay, d_rest = gather(r.dall, r.ds, r.dr)
+    s_begin, s_wait, s_relay, s_rest = gather(r.sall, r.ss, r.sr)
+    l_begin, l_wait, l_relay, l_rest = gather(r.lall, r.ls, r.lr)
+
+    loaded("x")
+    first = norm_parts(r.xv[...].astype(F32), gains[0:1, :], shifts[0:1, :])[2]
+    r.nall[block_rows(head), :] = first.astype(BF)
+    pl.semaphore_wait(barrier, 7)
+    n_begin()
+    position = head * BLOCK + lax.broadcasted_iota(jnp.int32, (BLOCK, 1), 0)
+    loaded("d")
+    r.dall[block_rows(head), :] = (r.dv[...].astype(F32) * jnp.where(position < total, 1.0, 0.0)).astype(BF)
+    loaded("wqkv")
+    aligned = lax.div(3 * head, 2) * 128
+    odd = jnp.where(lax.rem(head, 2) == 1, 1.0, 0.0)
+    on_heads = jnp.where(onlane < 192, 1.0, 0.0)
+
+    def own_window(values):
+        moved = pltpu.roll(values, 192, 1)
+        return (values * (1.0 - odd) + moved * odd) * on_heads
+
+    bias = []
+    for part in range(3):
+        window = pl.ds(pl.multiple_of(part * D + aligned, 128), 256)
+        r.wqo[:, part * 256 : (part + 1) * 256] = own_window(r.wqkv[:, window].astype(F32)).astype(BF)
+        bias.append(own_window(jnp.broadcast_to(r.full_bias[:, window], (8, 256)))[0:1])
+    bias = jnp.concatenate(bias, axis=1)
+
+    aux_k = jnp.where((onlane >= 196) & (onlane < 199), 1.0, 0.0)
+    aux_v = jnp.where((onlane >= 192) & (onlane < 199) & (onlane != 195), 1.0, 0.0)
+    on_aux = jnp.where(onlane >= 192, 1.0, 0.0)
+
+    def project(block):
+        rows = block_rows(block)
+        projected = (nn(r.nall[rows, :], r.wqo[...]) + bias).astype(BF).astype(F32)
+        r.qb[rows, :] = (projected[:, :256] * 0.125 + lane_is(192 + block)).astype(BF)
+        off = jnp.where((onlane >= 192) & (onlane < 196) & (onlane != 192 + block), 1.0, 0.0)
+        r.kb[rows, :] = (projected[:, 256:512] + (aux_k + off * jnp.where(whole, 0.0, FAR))).astype(BF)
+        r.vb[rows, :] = (projected[:, 512:] + aux_v).astype(BF)
+
+    project(head)
+    n_wait(0)
+    project(sib)
+    n_relay()
+    project(far)
+    d_begin()
+    n_rest()
+    project(diag)
+
+    def mix_copy(code):
+        rows = block_rows(peer(code))
+        return push(r.mix.at[rows, :], r.mixin.at[head], r.ms.at[code - 1], r.mr.at[code - 1], (dp, peer(code)))
+
+    small_lane = lax.broadcasted_iota(jnp.int32, (1, 128), 1)
+
+    def attend(step, carry):
+        code = 3 - step
+        block = peer(code)
+        rows = block_rows(block)
+        queries = r.qb[rows, :]
+        mixed = jnp.zeros((BLOCK, 256), F32)
+        tops = []
+        for n in range(3):
+            scores = nt(queries * (head_mask(n) + on_aux).astype(BF), r.kb[...])
+            top = jnp.max(scores, axis=1, keepdims=True)
+            weights = jnp.exp(scores - top).astype(BF)
+            mixed += nn(weights, r.vb[...] * (head_mask(n) + lane_is(192 + n)).astype(BF))
+            tops.append(top)
+        lse = jnp.zeros((BLOCK, 128), F32)
+        scale = jnp.zeros((BLOCK, 256), F32)
+        for n in range(3):
+            row_sum = jnp.sum(mixed * lane_is(192 + n), axis=1, keepdims=True)
+            lse += (tops[n] + jnp.log(row_sum)) * jnp.where(small_lane == n, 1.0, 0.0)
+            scale += (1.0 / row_sum) * head_mask(n)
+        place = block * BLOCK + lax.broadcasted_iota(jnp.int32, (BLOCK, 1), 0)
+        mixed = jnp.where(place < total, mixed * scale, r.vb[rows, :].astype(F32) * on_heads)
+        r.exact[rows, :] = mixed
+        r.lse[rows, :] = lse
+        r.mix[rows, :] = mixed.astype(BF)
+
+        @pl.when(step < 3)
+        def _():
+            mix_copy(code).start()
+
+        return carry
+
+    lax.fori_loop(0, 4, attend, 0)
+    r.mixin[head] = r.mix[block_rows(head), :]
+    d_relay()
+
+    loaded("wout")
+    loaded("wup")
+    loaded("wdown")
+    for code in (3, 2, 1):
+        mix_copy(code).wait_recv()
+    for group in range(4):
+        r.wqo[0:256, group * 192 : (group + 1) * 192] = r.mixin[group][:, :192]
+    hidden = r.xv[...].astype(F32) + nn(r.wqo[0:256, :], r.wout[...]) + biases[0:1, :]
+    unit, inverse, normed = norm_parts(hidden, gains[1:2, :], shifts[1:2, :])
+    second = normed.astype(BF)
+    r.sall[block_rows(head), :] = second
+    s_begin()
+    grad_low = r.dall[block_rows(head), :]
+    down = jnp.zeros((BLOCK, D), F32)
+    back = jnp.zeros((BLOCK, D), F32)
+    for tile in range(4):
+        cut = slice(tile * D, (tile + 1) * D)
+        up = nn(second, r.wup[:, cut]) + r.up_bias[:, cut]
+        value, slope = gelu_parts(up)
+        w_down = r.big[cut, 0:D]
+        down += nn(value.astype(BF), w_down)
+        grad_up = nt(grad_low, w_down) * slope
+        back += nt(grad_up.astype(BF), r.wup[:, cut])
+        if tile == 2:
+            s_relay()
+    r.block_out[...] = (hidden + down + biases[1:2, :]).astype(BF)
+    grad_block = grad_low.astype(F32)
+    grad_hidden = grad_block + norm_back(back, unit, inverse, gains[1:2, :])
+    r.gh[...] = grad_hidden
+    r.lall[block_rows(head), :] = grad_hidden.astype(BF)
+    l_begin()
+    r.vec[...] = jnp.zeros_like(r.vec)
+    r.vec[1:2, :] = jnp.sum(back * unit, axis=0, keepdims=True)
+    r.vec[3:4, :] = jnp.sum(back, axis=0, keepdims=True)
+    r.vec[6:7, :] = jnp.sum(grad_hidden, axis=0, keepdims=True)
+    r.vec[7:8, :] = jnp.sum(grad_block, axis=0, keepdims=True)
+
+    loaded("wuo")
+    loaded("wdo")
+    loaded("woo")
+    for wait in (s_wait, d_wait):
+        wait(0)
+    s_rest()
+    d_rest()
+    own_bias = jnp.concatenate(
+        [r.up_bias[:, pl.ds(pl.multiple_of((4 * j + head) * 128, 128), 128)] for j in range(6)], axis=1
+    )
+
+    def feed(step, sums):
+        rows = block_rows(peer(step))
+        up = nn(r.sall[rows, :], r.wuo[...]) + own_bias
+        value, slope = gelu_parts(up)
+        r.act[rows, :] = value.astype(BF)
+        grad_up = nt(r.dall[rows, :], r.wdo[...]) * slope
+        r.gup[rows, :] = grad_up.astype(BF)
+        return sums + jnp.sum(grad_up, axis=0, keepdims=True)
+
+    sums = lax.fori_loop(0, 3, feed, jnp.zeros((1, D), F32))
+    l_relay()
+    sums = feed(jnp.int32(3), sums)
+    r.small[...] = jnp.zeros_like(r.small)
+    for j in range(6):
+        number = 4 * j + head
+        shard = lax.div(number, 3)
+        r.small[lax.rem(shard, 2), lax.div(shard, 2), pl.ds(8 + lax.rem(number, 3), 1), :] = sums[
+            :, j * 128 : (j + 1) * 128
+        ]
+
+    def regular(name):
+        own, ybuf, zbuf, fin = (getattr(r, part + name) for part in ("p", "y", "z", "f"))
+        sems = [getattr(r, part + name + end) for part in ("y", "z", "f") for end in ("s", "r")]
+        ys, yr, zs, zr, fs, fr = sems
+
+        def y_copy(k):
+            src = own.at[z_shard(k) * 2 + (1 - y)]
+            return push(src, ybuf.at[k], ys.at[k], yr.at[k], (other_y, head))
+
+        def z_copy(k):
+            shard = z_shard(k) * 2 + y
+            return push(own.at[shard], zbuf.at[k], zs.at[k], zr.at[k], (shard, head))
+
+        def f_copy(code):
+            place = far if code == 3 else head
+            to = far if code == 2 else sib
+            return push(fin.at[place], fin.at[place], fs.at[code - 1], fr.at[code - 1], (dp, to))
+
+        def begin():
+            for k in (1, 2, 3, 0):
+                start(lambda k=k: y_copy(k))
+
+        def pair(k, last=None):
+            y_copy(k).wait_recv()
+            at = z_shard(k) * 2 + y
+            own[at] = (own[at].astype(F32) + ybuf[k].astype(F32)).astype(BF)
+            if isinstance(k, int):
+                if k:
+                    start(lambda: z_copy(k))
+            else:
+
+                @pl.when(k > 0)
+                def _():
+                    z_copy(k).start()
+
+        def total_up():
+            for k in (1, 2, 3):
+                z_copy(k).wait_recv()
+            value = own[dp].astype(F32)
+            for k in (1, 2, 3):
+                value += zbuf[k].astype(F32)
+            fin[head] = value.astype(BF)
+            for code in (2, 1):
+                start(lambda code=code: f_copy(code))
+
+        def relay():
+            f_copy(2).wait_recv()
+            start(lambda: f_copy(3))
+
+        def rest():
+            f_copy(1).wait_recv()
+            f_copy(3).wait_recv()
+
+        def pair_sends():
+            for k in (1, 2, 3):
+                sent.append((lambda k=k: z_copy(k), None))
+
+        return begin, pair, total_up, relay, rest, pair_sends
+
+    def irregular(name, number_of, owner_of):
+        own, ybuf, zbuf, fin = (getattr(r, part + name) for part in ("p", "y", "z", "f"))
+        sems = [getattr(r, part + name + end) for part in ("y", "z", "f") for end in ("s", "r")]
+        ys, yr, zs, zr, fs, fr = sems
+
+        def facts(j):
+            number = number_of(j)
+            shard = lax.div(number, 3)
+            return shard, lax.div(shard, 2), lax.rem(shard, 2), lax.rem(number, 3)
+
+        def y_copy(j):
+            return push(own.at[j], ybuf.at[j], ys.at[j], yr.at[j], (other_y, head))
+
+        def z_copy(j):
+            shard, shard_z, shard_y, place = facts(j)
+            slot = (lax.rem(shard_z + 4 - z, 4) - 1) * 3 + place
+            return push(own.at[j], zbuf.at[slot], zs.at[j], zr.at[slot], (shard, head))
+
+        def z_arrival(j, k):
+            slot = (k - 1) * 3 + facts(j)[3]
+            return push(own.at[j], zbuf.at[slot], zs.at[j], zr.at[slot], (dp, sib)), slot
+
+        def f_copy(code, place):
+            index = (code - 1) * 3 + place
+            to = far if code == 2 else sib
+            return push(fin.at[place], fin.at[place], fs.at[index], fr.at[index], (dp, to))
+
+        def begin(these=range(6)):
+            for j in these:
+                start(lambda j=j: y_copy(j), facts(j)[2] != y)
+
+        def z_goes(j):
+            shard, shard_z, shard_y, place = facts(j)
+            return (shard_y == y) & (shard_z != z)
+
+        def pair(j):
+            @pl.when(facts(j)[2] == y)
+            def _():
+                y_copy(j).wait_recv()
+                own[j] = (own[j].astype(F32) + ybuf[j].astype(F32)).astype(BF)
+
+            @pl.when(z_goes(j))
+            def _():
+                z_copy(j).start()
+
+        def pair_sends():
+            for j in range(6):
+                sent.append((lambda j=j: z_copy(j), z_goes(j)))
+
+        def total_up():
+            for j in range(6):
+                shard, shard_z, shard_y, place = facts(j)
+
+                def body(j=j, place=place):
+                    value = own[j].astype(F32)
+                    for k in (1, 2, 3):
+                        copy, slot = z_arrival(j, k)
+                        copy.wait_recv()
+                        value += zbuf[slot].astype(F32)
+                    fin[place] = value.astype(BF)
+                    f_copy(2, place).start()
+                    f_copy(1, place).start()
+
+                pl.when(shard == dp)(body)
+
+        def relay():
+            for place in range(3):
+                owner = owner_of(3 * dp + place)
+                for code in (1, 2):
+                    sent.append((lambda code=code, place=place: f_copy(code, place), owner == head))
+
+                def body(place=place):
+                    f_copy(2, place).wait_recv()
+                    f_copy(3, place).start()
+
+                pl.when(owner == far)(body)
+                sent.append((lambda place=place: f_copy(3, place), owner == far))
+
+        def rest():
+            for place in range(3):
+                owner = owner_of(3 * dp + place)
+                for code, source in ((1, sib), (3, diag)):
+                    pl.when(owner == source)(lambda code=code, place=place: f_copy(code, place).wait_recv())
+
+        return begin, pair, total_up, relay, rest, pair_sends
+
+    dn_begin, dn_pair, dn_total, dn_relay, dn_rest, dn_sends = regular("dn")
+    ou_begin, ou_pair, ou_total, ou_relay, ou_rest, ou_sends = regular("ou")
+    up_begin, up_pair, up_total, up_relay, up_rest, up_sends = irregular(
+        "up", lambda j: 4 * j + head, lambda number: lax.rem(number, 4)
+    )
+    qk_begin, qk_pair, qk_total, qk_relay, qk_rest, qk_sends = irregular(
+        "qk",
+        lambda j: (j // 2) * 8 + 2 * head + j % 2,
+        lambda number: lax.div(lax.rem(number, 8), 2),
+    )
+
+    r.pdn[...] = tn(r.dall[...], r.act[...]).astype(BF).reshape(8, 96, D)
+    dn_begin()
+    r.pup[...] = tn(r.gup[...], r.sall[...]).astype(BF).reshape(6, 128, D)
+    up_begin()
+
+    l_wait(0)
+    l_rest()
+    r.woo[192:256, :] = jnp.zeros((64, D), BF)
+    r.gm[...] = nt(r.lall[...], r.woo[...]).astype(BF)
+    r.pou[...] = tn(r.lall[...], r.mix[...]).astype(BF).reshape(8, 96, 256)
+    ou_begin()
+    q_aug, g_aug = r.act, r.gup
+    for n in range(3):
+        mask = head_mask(n)
+
+        def augment(block, carry, n=n, mask=mask):
+            rows = pl.ds(pl.multiple_of(block * 256, 256), 256)
+            grads = r.gm[rows, :].astype(F32) * mask
+            inner = jnp.sum(grads * r.exact[rows, :], axis=1, keepdims=True)
+            queries = r.qb[rows, :].astype(F32) * (mask + on_aux)
+            for place, part in enumerate(split_three(-r.lse[rows, :][:, n : n + 1])):
+                queries = queries + part * lane_is(196 + place)
+            for place, part in enumerate(split_three(-inner)):
+                grads = grads + part * lane_is(196 + place)
+            q_aug[rows, n * 256 : (n + 1) * 256] = queries.astype(BF)
+            g_aug[rows, n * 256 : (n + 1) * 256] = grads.astype(BF)
+            return carry
+
+        lax.fori_loop(0, 4, augment, 0)
+
+    def kv_copy(code):
+        rows = block_rows(peer(code))
+        return push(r.dkv.at[rows, :], r.kvin.at[head], r.kvs.at[code - 1], r.kvr.at[code - 1], (dp, peer(code)))
+
+    def q_copy(code):
+        rows = block_rows(peer(code))
+        return push(r.dq.at[rows, :], r.qin.at[head], r.qs.at[code - 1], r.qr.at[code - 1], (dp, peer(code)))
+
+    def attend_back(step, carry):
+        code = 3 - step
+        block = peer(code)
+        rows = block_rows(block)
+        key_grad = jnp.zeros((BLOCK, 256), F32)
+        value_grad = jnp.zeros((BLOCK, 256), F32)
+        for n in range(3):
+            mask = head_mask(n)
+            lanes = slice(n * 256, (n + 1) * 256)
+            probs = jnp.exp(nt(r.kb[rows, :], q_aug[:, lanes]))
+            grad_scores = (probs * nt(r.vb[rows, :], g_aug[:, lanes])).astype(BF)
+            r.big[pl.ds(pl.multiple_of(n * SLOT + block * BLOCK, 256), BLOCK), :] = grad_scores
+            key_grad += nn(grad_scores, q_aug[:, lanes]) * mask
+            value_grad += nn(probs.astype(BF), g_aug[:, lanes]) * mask
+        r.dkv[rows, 0:192] = key_grad[:, :192].astype(BF)
+        r.dkv[rows, 192:384] = value_grad[:, :192].astype(BF)
+
+        @pl.when(step < 3)
+        def _():
+            kv_copy(code).start()
+
+        dn_pair(lax.rem(step + 1, 4))
+        up_pair(step)
+        return carry
+
+    lax.fori_loop(0, 4, attend_back, 0)
+    r.kvin[head] = r.dkv[block_rows(head), :]
+
+    def query_back(step, carry):
+        code = 3 - step
+        block = peer(code)
+        rows = block_rows(block)
+        query_grad = jnp.zeros((BLOCK, 256), F32)
+        for n in range(3):
+            part = r.big[n * SLOT : (n + 1) * SLOT, pl.ds(pl.multiple_of(block * BLOCK, 256), BLOCK)]
+            query_grad += tn(part, r.kb[...] * head_mask(n).astype(BF))
+        r.dq[rows, :] = (query_grad * 0.125).astype(BF)
+
+        @pl.when(step < 3)
+        def _():
+            q_copy(code).start()
+
+        return carry
+
+    lax.fori_loop(0, 4, query_back, 0)
+    r.qin[head] = r.dq[block_rows(head), :]
+    up_pair(4)
+    up_pair(5)
+    for k in (1, 2, 3, 0):
+        ou_pair(k)
+    dn_sends()
+    up_sends()
+    r.pqk[2:6] = tn(r.dkv[...], r.nall[...]).astype(BF).reshape(4, 96, D)
+    qk_begin(range(2, 6))
+    r.pqk[0:2] = tn(r.dq[...], r.nall[...])[:192].astype(BF).reshape(2, 96, D)
+    qk_begin(range(2))
+    query_sum = jnp.sum(r.dq[...].astype(F32), axis=0, keepdims=True)
+    value_sum = jnp.sum(r.dkv[:, 128:384].astype(F32), axis=0, keepdims=True)
+    for group in range(4):
+        mine = jnp.where(head == group, 1.0, 0.0)
+        r.vec[4:5, group * 192 : (group + 1) * 192] = query_sum[:, :192] * mine
+        r.vec[5:6, group * 192 : (group + 1) * 192] = value_sum[:, 64:] * mine
+    dn_total()
+    up_total()
+    ou_total()
+
+    for code in (3, 2, 1):
+        kv_copy(code).wait_recv()
+        q_copy(code).wait_recv()
+    for group in range(4):
+        lanes = slice(group * 192, (group + 1) * 192)
+        r.wuo[0:256, lanes] = r.qin[group][:, :192]
+        r.wuo[256:512, lanes] = r.kvin[group][:, :192]
+        r.wuo[512:768, lanes] = r.kvin[group][:, 192:]
+    grad_first = nt(r.wuo[0:256, :], r.wqkv[:, 0:D])
+    grad_first += nt(r.wuo[256:512, :], r.wqkv[:, D : 2 * D])
+    grad_first += nt(r.wuo[512:768, :], r.wqkv[:, 2 * D :])
+    unit, inverse, _ = norm_parts(r.xv[...].astype(F32), gains[0:1, :], shifts[0:1, :])
+    r.grad_inputs[...] = r.gh[...] + norm_back(grad_first, unit, inverse, gains[0:1, :])
+    r.vec[0:1, :] = jnp.sum(grad_first * unit, axis=0, keepdims=True)
+    r.vec[2:3, :] = jnp.sum(grad_first, axis=0, keepdims=True)
+    for shard in range(8):
+        r.small[shard % 2, shard // 2, 0:8, 0:96] = r.vec[:, shard * 96 : (shard + 1) * 96]
+
+    def small_y():
+        return push(r.small.at[1 - y], r.ysm, r.ysms.at[0], r.ysmr.at[0], (other_y, head))
+
+    def small_z(k):
+        return push(
+            r.small.at[y, z_shard(k)], r.zsm.at[k], r.zsms.at[k], r.zsmr.at[k], (z_shard(k) * 2 + y, head)
+        )
+
+    def small_f(code):
+        return push(r.fsm.at[head], r.fsm.at[head], r.fsms.at[code - 1], r.fsmr.at[code - 1], (dp, peer(code)))
+
+    start(small_y)
+    for step in (2, 3, 4, 5, 0, 1):
+        qk_pair(step)
+    qk_sends()
+    small_y().wait_recv()
+    r.small[y] = r.small[y] + r.ysm[...]
+    for k in (1, 2, 3):
+        start(lambda k=k: small_z(k))
+    dn_relay()
+    up_relay()
+    ou_relay()
+    qk_total()
+    for k in (1, 2, 3):
+        small_z(k).wait_recv()
+    r.fsm[head] = r.small[y, z] + r.zsm[1] + r.zsm[2] + r.zsm[3]
+    for code in (2, 3, 1):
+        start(lambda code=code: small_f(code))
+    qk_relay()
+    dn_rest()
+    up_rest()
+    ou_rest()
+    qk_rest()
+    for code in (2, 3, 1):
+        small_f(code).wait_recv()
+    r.fsum[...] = r.fsm[0] + r.fsm[1] + r.fsm[2] + r.fsm[3]
+    for make, cond in sent:
+        when(cond, lambda make=make: make().wait_send())
+    for code in (1, 2, 3):
+        mix_copy(code).wait_send()
+        kv_copy(code).wait_send()
+        q_copy(code).wait_send()
+
+
+def per_device(x, norm_gains, norm_shifts, w_qkv, qv_bias, w_out, out_biases, w_up, up_bias, w_down, lengths, d_out):
+    full_bias = jnp.concatenate([qv_bias[0], jnp.zeros_like(qv_bias[0]), qv_bias[1]]).astype(F32).reshape(1, 3 * D)
+    values = dict(
+        x=x[0], gains=norm_gains, shifts=norm_shifts, w_qkv=w_qkv, full_bias=full_bias, w_out=w_out, biases=out_biases,
+        w_up=w_up, up_bias=up_bias.astype(F32).reshape(1, FF), w_down=w_down, lengths=lengths, d_out=d_out[0],
+    )
+    place = {True: pl.BlockSpec(memory_space=pl.ANY), False: pl.BlockSpec(memory_space=pltpu.VMEM)}
+    block_out, grad_inputs, fup, fqk, fdn, fou, fsum = pl.pallas_call(
+        one_kernel,
+        out_shape=[jax.ShapeDtypeStruct(shape, kind) for _, shape, kind in OUTPUTS],
+        in_specs=[place[name in IN_PLACE] for name in INPUTS],
+        out_specs=[place[False]] * len(OUTPUTS),
+        scratch_shapes=[pltpu.VMEM(shape, kind) for _, shape, kind in BUFFERS]
+        + [pltpu.SemaphoreType.DMA((count,)) for _, count in SEMAPHORES],
+        compiler_params=pltpu.CompilerParams(
+            collective_id=0, has_side_effects=True, vmem_limit_bytes=VMEM_LIMIT
+        ),
+        name="block",
+    )(*(values[name] for name in INPUTS))
+    down = fdn.reshape(4, 96, 6, 128).transpose(2, 0, 3, 1).reshape(FF, 96)
+    return (
+        block_out[None],
+        grad_inputs[None],
+        fsum[0:2, 0:96],
+        fsum[2:4, 0:96],
+        fqk.reshape(288, D).T.astype(F32),
+        fsum[4:6, 0:96],
+        fou[:, :, :192].transpose(0, 2, 1).reshape(D, 96).astype(F32),
+        fsum[6:8, 0:96],
+        fup.reshape(384, D).T.astype(F32),
+        fsum[8:11].reshape(384),
+        down.astype(F32),
+    )
+
+
 def solution(mesh):
     split = P("dp", "head", None)
     placed = (split,) + (P(),) * 9 + (P("dp", None), split)
     return jax.shard_map(
-        per_device,
+        per_device if dict(mesh.shape) == {"dp": 8, "head": 4} else general_device,
         mesh=mesh,
         in_specs=placed,
         out_specs=(split, split) + (P(None, "dp"),) * 7 + (P("dp"), P(None, "dp")),

time: 460 us -> 138 us (0.30)
  waiting for transfers between devices: 249 us -> 0 us
  blocking collectives: 65.7 us -> 0 us
  Pallas kernels: 60 us -> 122 us
  local copies, waits for them, and re-layouts: 42.8 us -> 11.6 us
  between operations: 14.1 us -> 0.72 us
  starting transfers between devices: 10.8 us -> 0 us
  other arithmetic: 12.6 us -> 3.05 us
    reduce_scatter x4 -> x0, waiting for transfers between devices: 175 us -> none  [scatter(): return lax.psum_scatter(values, 'dp', scatter_dimension=0, tiled=True)]
    pallas_call x5 -> x1, Pallas kernels: 60 us -> 122 us  [per_device(): pl.pallas_call(one_kernel, out_shape=[jax.ShapeDtypeStruct(shape, kind) f...]
    psum x1 -> x0, blocking collectives: 39.2 us -> none  [per_device(): small = lax.psum(small, ('dp', 'head'))]
    all_gather x4 -> x0, waiting for transfers between devices: 37.8 us -> none  [the longest x1 16.9 us: per_device(): low_all = lax.all_gather(hid_low, 'head', axis=0, tiled=True)]
    psum x1 -> x0, waiting for transfers between devices: 31.9 us -> none  [per_device(): qkv_part = lax.psum(scatter(spread.reshape(3 * D, D)), 'head')]
    all_gather x3 -> x0, blocking collectives: 26.5 us -> none  [the longest x1 9.16 us: per_device(): down_part = lax.all_gather(scatter(down_grad), 'head', axis=1, tiled=True)]
    unnamed x27 -> x12, local copies, waits for them, and re-layouts: 16.6 us -> 1.65 us
    reshape x11 -> x1, local copies, waits for them, and re-layouts: 11.9 us -> 1.26 us  [per_device(): fsum[8:11].reshape(384)]
  transfers between devices with their start and end apart: 11 -> 0, of which waited for: 9 -> 0; matrix products, arithmetic and copies ran while one was open for 9% -> 0% of each run, Pallas kernels for 8% -> 0%
where the time goes in v2:
time: 138 us
  Pallas kernels  122 us (88%)
  local copies, waits for them, and re-layouts  11.6 us (8%)
  other arithmetic  3.05 us (2%)
    pallas_call x1, Pallas kernels, per_device(): pl.pallas_call(one_kernel, out_shape=[jax.ShapeDtypeStruct(shape, kind) f...  122 us
    convert_element_type x3, local copies, waits for them, and re-layouts, per_device(): down.astype(F32)  3.95 us

profile of v2, /device:TPU:3, one launch (start us, length us, event | category | flops | bytes accessed | tf_op | source)
XLA Modules:
  0.0 137.7 jit_solution(6350820661109480407)
XLA Ops:
  0.6 0.8 fusion.3
  1.4 0.6 fusion.1.args_4_
  2.0 1.3 reshape.81
  3.3 122.3 %block.1 = (bf16[256,768]{1,0:T(8,128)(2,1)}, f32[256,768]{1,0:T(8,128)}, bf16[3,128,768]{2,1,0:T(8,128)(2,1)}, bf16[3,96,768]{2,1,0:T(8,128)(2,1)}, bf16[4,96,7...) custom-call(bf16[256,768]{1,0:T(8,128)(2,1)} %bitcast.27, bf16[2,768]{1,0:T(2,128)(2,1)} %args_1_.4, ...), custom_call_target="tpu_custom_call" | custom-call | tf_op jit(solution)/shard_map/block/pallas_call | solution.py:1047
  125.6 1.4 %fusion.2 = (f32[2,96]{1,0:T(2,128)}, f32[2,96]{1,0:T(2,128)}, f32[2,96]{1,0:T(2,128)}, f32[2,96]{1,0:T(2,128)}) fusion(f32[16,128]{1,0:T(8,128)} %get-tuple-element.20), kind=kLoop, calls=%fused_computation.7 | loop fusion | bytes 6144 | tf_op jit(solution)/shard_map/slice | solution.py:1068
  127.0 1.3 slice_bitcast_fusion
  128.3 1.7 %reshape.87 = f32[4,96,6,128]{3,2,1,0:T(8,128)S(1)} reshape(bf16[4,96,768]{2,1,0:T(8,128)(2,1)} %get-tuple-element.24) | data formatting | bytes 1769472 | tf_op jit(solution)/shard_map/convert_element_type | solution.py:1071
  130.0 0.8 copy.29
  130.7 0.0 copy-start.1
  130.8 1.5 %reshape.84 = f32[3072,96]{0,1:T(8,128)} reshape(f32[6,4,128,96]{2,1,0,3:T(4,128)S(1)} %copy.29) | data formatting | bytes 2359296 | tf_op jit(solution)/shard_map/convert_element_type | solution.py:1071
  132.2 0.0 copy-done.1
  132.2 0.1 bitcast_convert_fusion
  132.4 0.0 copy-start.4
  132.4 1.4 %copy.28 = f32[384,768]{0,1:T(8,128)} copy(f32[384,768]{1,0:T(8,128)S(1)} %bitcast_convert_fusion) | data formatting | bytes 2359296 | tf_op jit(solution)/shard_map/convert_element_type | solution.py:1069
  133.8 0.0 copy-start.2
  133.8 0.0 copy-done.4
  133.8 0.3 copy.27
  134.1 0.0 copy-start.3
  134.1 1.0 reshape.83
  135.0 0.0 copy-start
  135.0 0.0 copy-done.2
  135.0 1.0 convert_bitcast_fusion
  136.0 0.0 copy-done.3
  136.0 0.7 copy.32
  136.8 0.0 copy-done
  136.8 0.9 copy.33
  (3 shorter events, 0.0 us)
Async XLA Ops:
  130.7 1.5 %copy-start.1 = (bf16[3,128,768]{2,1,0:T(8,128)(2,1)S(1)}, bf16[3,128,768]{2,1,0:T(8,128)(2,1)}, u32[]{:S(2)}) copy-start(bf16[3,128,768]{2,1,0:T(8,128)(2,1)} %get-tuple-element.23) | copy-start | bytes 1769476
  132.4 1.4 %copy-start.4 = (bf16[4,96,256]{2,1,0:T(8,128)(2,1)S(1)}, bf16[4,96,256]{2,1,0:T(8,128)(2,1)}, u32[]{:S(2)}) copy-start(bf16[4,96,256]{2,1,0:T(8,128)(2,1)} %get-tuple-element.22) | copy-start | bytes 589828
  133.8 1.3 copy-start.2
  134.1 2.0 %copy-start.3 = (bf16[256,768]{1,0:T(8,128)(2,1)S(1)}, bf16[256,768]{1,0:T(8,128)(2,1)}, u32[]{:S(2)}) copy-start(bf16[256,768]{1,0:T(8,128)(2,1)} %get-tuple-element.18) | copy-start | bytes 1179652
  135.0 1.8 %copy-start = (f32[256,768]{1,0:T(8,128)S(1)}, f32[256,768]{1,0:T(8,128)}, u32[]{:S(2)}) copy-start(f32[256,768]{1,0:T(8,128)} %get-tuple-element.19) | copy-start | bytes 2359300

commit v3 on v2

--- a/solution.py
+++ b/solution.py
@@ -394,7 +394,8 @@
     ("mix", (SLOT, 256), BF),
     ("exact", (SLOT, 256), F32),
     ("lse", (SLOT, 128), F32),
-    ("mixin", (4, 256, 256), BF),
+    ("mixs", (4, 384, 128), BF),
+    ("mixin", (4, 384, 128), BF),
     ("gh", (256, D), F32),
     ("act", (SLOT, D), BF),
     ("gup", (SLOT, D), BF),
@@ -402,17 +403,21 @@
     ("dkv", (SLOT, 384), BF),
     ("dq", (SLOT, 256), BF),
     ("kvin", (4, 256, 384), BF),
-    ("qin", (4, 256, 256), BF),
-    ("pdn", (8, 96, D), BF),
-    ("pup", (6, 128, D), BF),
+    ("qs_", (4, 384, 128), BF),
+    ("qin", (4, 384, 128), BF),
+    ("pdy", (8, 96, 384), BF),
+    ("pdz", (8, 96, 384), BF),
+    ("pup", (6, D, 128), BF),
     ("pou", (8, 96, 256), BF),
     ("pqk", (6, 96, D), BF),
-    ("ydn", (4, 96, D), BF),
-    ("yup", (6, 128, D), BF),
+    ("ydy", (4, 96, 384), BF),
+    ("ydz", (1, 96, 384), BF),
+    ("yup", (6, D, 128), BF),
     ("you", (4, 96, 256), BF),
     ("yqk", (6, 96, D), BF),
-    ("zdn", (4, 96, D), BF),
-    ("zup", (9, 128, D), BF),
+    ("zdy", (4, 96, 384), BF),
+    ("zdz", (4, 2, 96, 384), BF),
+    ("zup", (12, D, 128), BF),
     ("zou", (4, 96, 256), BF),
     ("zqk", (9, 96, D), BF),
     ("vec", (8, D), F32),
@@ -425,20 +430,22 @@
     ("load", 22),
     ("ns", 5), ("nr", 5), ("ds", 5), ("dr", 5), ("ss", 5), ("sr", 5), ("ls", 5), ("lr", 5),
     ("ms", 3), ("mr", 3), ("kvs", 3), ("kvr", 3), ("qs", 3), ("qr", 3),
-    ("ydns", 4), ("ydnr", 4), ("zdns", 4), ("zdnr", 4), ("fdns", 3), ("fdnr", 3),
+    ("ydys", 4), ("ydyr", 4), ("zdys", 4), ("zdyr", 4), ("fdys", 3), ("fdyr", 3),
+    ("ydzs", 1), ("ydzr", 1), ("zdzs", 4), ("zdzr", 4), ("fdzs", 3), ("fdzr", 3),
     ("yous", 4), ("your", 4), ("zous", 4), ("zour", 4), ("fous", 3), ("four", 3),
-    ("yups", 6), ("yupr", 6), ("zups", 6), ("zupr", 9), ("fups", 9), ("fupr", 9),
+    ("yups", 6), ("yupr", 6), ("zups", 6), ("zupr", 12), ("fups", 9), ("fupr", 9),
     ("yqks", 6), ("yqkr", 6), ("zqks", 6), ("zqkr", 9), ("fqks", 9), ("fqkr", 9),
     ("ysms", 1), ("ysmr", 1), ("zsms", 4), ("zsmr", 4), ("fsms", 3), ("fsmr", 3),
 )
-INPUTS = ("x", "gains", "shifts", "w_qkv", "full_bias", "w_out", "biases", "w_up", "up_bias", "w_down", "lengths", "d_out")
+INPUTS = ("x", "gains", "shifts", "w_qkv", "qv_bias", "w_out", "biases", "w_up", "up_bias", "w_down", "lengths", "d_out")
 IN_PLACE = ("x", "w_qkv", "w_out", "w_up", "w_down", "d_out")
 OUTPUTS = (
     ("block_out", (256, D), BF),
     ("grad_inputs", (256, D), F32),
-    ("fup", (3, 128, D), BF),
+    ("fup", (3, D, 128), BF),
     ("fqk", (3, 96, D), BF),
-    ("fdn", (4, 96, D), BF),
+    ("fdy", (4, 96, 384), BF),
+    ("fdz", (4, 96, 384), BF),
     ("fou", (4, 96, 256), BF),
     ("fsum", (16, 128), F32),
 )
@@ -471,6 +478,12 @@
 
     def z_shard(k):
         return lax.rem(z + k, 4)
+
+    half = lax.div(z, 2)
+    inner = (z == 1) | (z == 2)
+    outer = (z == 0) | (z == 3)
+    beside = half * 2 + 1 - lax.rem(z, 2)
+    z_order = (3 * (1 - half), 2 - half, beside, z)
 
     sent = []
 
@@ -535,18 +548,15 @@
                 rows, to = block_rows(far, 128, (index - 3) * 128), sib
             return push(buf.at[rows, :], buf.at[rows, :], send.at[index], recv.at[index], (dp, to))
 
-        def arrival(index):
-            return copy_of(index)
-
-        def begin():
-            for index in (1, 2, 0):
+        def begin(these=(1, 2, 0)):
+            for index in these:
                 start(lambda index=index: copy_of(index))
 
         def wait(index):
             copy_of(index).wait_recv()
 
-        def relay():
-            for index in (1, 2):
+        def relay(these=(1, 2)):
+            for index in these:
                 wait(index)
                 start(lambda index=index: copy_of(index + 2))
 
@@ -569,6 +579,7 @@
     position = head * BLOCK + lax.broadcasted_iota(jnp.int32, (BLOCK, 1), 0)
     loaded("d")
     r.dall[block_rows(head), :] = (r.dv[...].astype(F32) * jnp.where(position < total, 1.0, 0.0)).astype(BF)
+    d_begin((1, 0))
     loaded("wqkv")
     aligned = lax.div(3 * head, 2) * 128
     odd = jnp.where(lax.rem(head, 2) == 1, 1.0, 0.0)
@@ -578,12 +589,12 @@
         moved = pltpu.roll(values, 192, 1)
         return (values * (1.0 - odd) + moved * odd) * on_heads
 
-    bias = []
+    r.vec[0:2, :] = r.qv_bias[...].astype(F32)
+    pair_bias = own_window(r.vec[:, pl.ds(pl.multiple_of(aligned, 128), 256)])
+    bias = jnp.concatenate([pair_bias[0:1], jnp.zeros((1, 256), F32), pair_bias[1:2]], axis=1)
     for part in range(3):
         window = pl.ds(pl.multiple_of(part * D + aligned, 128), 256)
         r.wqo[:, part * 256 : (part + 1) * 256] = own_window(r.wqkv[:, window].astype(F32)).astype(BF)
-        bias.append(own_window(jnp.broadcast_to(r.full_bias[:, window], (8, 256)))[0:1])
-    bias = jnp.concatenate(bias, axis=1)
 
     aux_k = jnp.where((onlane >= 196) & (onlane < 199), 1.0, 0.0)
     aux_v = jnp.where((onlane >= 192) & (onlane < 199) & (onlane != 195), 1.0, 0.0)
@@ -602,13 +613,22 @@
     project(sib)
     n_relay()
     project(far)
-    d_begin()
     n_rest()
     project(diag)
 
+    def packed(values):
+        third = values[:, 128:]
+        return jnp.concatenate([values[:, :128], third[:128] + pltpu.roll(third[128:], 64, 1)], axis=0).astype(BF)
+
+    def unpack(source, dst, base):
+        for group in range(4):
+            lane = group * 192
+            dst[base : base + 256, lane : lane + 128] = source[group, 0:256, :]
+            dst[base : base + 128, lane + 128 : lane + 192] = source[group, 256:384, 0:64]
+            dst[base + 128 : base + 256, lane + 128 : lane + 192] = source[group, 256:384, 64:128]
+
     def mix_copy(code):
-        rows = block_rows(peer(code))
-        return push(r.mix.at[rows, :], r.mixin.at[head], r.ms.at[code - 1], r.mr.at[code - 1], (dp, peer(code)))
+        return push(r.mixs.at[code], r.mixin.at[head], r.ms.at[code - 1], r.mr.at[code - 1], (dp, peer(code)))
 
     small_lane = lax.broadcasted_iota(jnp.int32, (1, 128), 1)
 
@@ -636,6 +656,7 @@
         r.exact[rows, :] = mixed
         r.lse[rows, :] = lse
         r.mix[rows, :] = mixed.astype(BF)
+        r.mixs[code] = packed(mixed)
 
         @pl.when(step < 3)
         def _():
@@ -644,16 +665,16 @@
         return carry
 
     lax.fori_loop(0, 4, attend, 0)
-    r.mixin[head] = r.mix[block_rows(head), :]
-    d_relay()
+    d_begin((2,))
+    r.mixin[head] = r.mixs[0]
+    d_relay((1,))
 
     loaded("wout")
     loaded("wup")
     loaded("wdown")
     for code in (3, 2, 1):
         mix_copy(code).wait_recv()
-    for group in range(4):
-        r.wqo[0:256, group * 192 : (group + 1) * 192] = r.mixin[group][:, :192]
+    unpack(r.mixin, r.wqo, 0)
     hidden = r.xv[...].astype(F32) + nn(r.wqo[0:256, :], r.wout[...]) + biases[0:1, :]
     unit, inverse, normed = norm_parts(hidden, gains[1:2, :], shifts[1:2, :])
     second = normed.astype(BF)
@@ -664,14 +685,12 @@
     back = jnp.zeros((BLOCK, D), F32)
     for tile in range(4):
         cut = slice(tile * D, (tile + 1) * D)
-        up = nn(second, r.wup[:, cut]) + r.up_bias[:, cut]
+        up = nn(second, r.wup[:, cut]) + r.up_bias[:, cut].astype(F32)
         value, slope = gelu_parts(up)
         w_down = r.big[cut, 0:D]
         down += nn(value.astype(BF), w_down)
         grad_up = nt(grad_low, w_down) * slope
         back += nt(grad_up.astype(BF), r.wup[:, cut])
-        if tile == 2:
-            s_relay()
     r.block_out[...] = (hidden + down + biases[1:2, :]).astype(BF)
     grad_block = grad_low.astype(F32)
     grad_hidden = grad_block + norm_back(back, unit, inverse, gains[1:2, :])
@@ -687,15 +706,26 @@
     loaded("wuo")
     loaded("wdo")
     loaded("woo")
-    for wait in (s_wait, d_wait):
-        wait(0)
-    s_rest()
-    d_rest()
     own_bias = jnp.concatenate(
         [r.up_bias[:, pl.ds(pl.multiple_of((4 * j + head) * 128, 128), 128)] for j in range(6)], axis=1
-    )
+    ).astype(F32)
 
     def feed(step, sums):
+        @pl.when(step == 1)
+        def _():
+            d_wait(0)
+            s_wait(0)
+
+        @pl.when(step == 2)
+        def _():
+            d_relay((2,))
+            s_relay()
+
+        @pl.when(step == 3)
+        def _():
+            d_rest()
+            s_rest()
+
         rows = block_rows(peer(step))
         up = nn(r.sall[rows, :], r.wuo[...]) + own_bias
         value, slope = gelu_parts(up)
@@ -704,9 +734,294 @@
         r.gup[rows, :] = grad_up.astype(BF)
         return sums + jnp.sum(grad_up, axis=0, keepdims=True)
 
-    sums = lax.fori_loop(0, 3, feed, jnp.zeros((1, D), F32))
-    l_relay()
-    sums = feed(jnp.int32(3), sums)
+    sums = lax.fori_loop(0, 4, feed, jnp.zeros((1, D), F32))
+    def parts_of(name):
+        refs = [getattr(r, part + name) for part in ("p", "y", "z", "f")]
+        return refs + [getattr(r, part + name + end) for part in ("y", "z", "f") for end in ("s", "r")]
+
+    def finals(fin, fs, fr):
+        def f_copy(code):
+            place = far if code == 3 else head
+            to = far if code == 2 else sib
+            return push(fin.at[place], fin.at[place], fs.at[code - 1], fr.at[code - 1], (dp, to))
+
+        def begin():
+            for code in (2, 1):
+                start(lambda code=code: f_copy(code))
+
+        def relay():
+            f_copy(2).wait_recv()
+            start(lambda: f_copy(3))
+
+        def rest():
+            f_copy(1).wait_recv()
+            f_copy(3).wait_recv()
+
+        return begin, relay, rest
+
+    def add_to(ref, at, more):
+        ref[at] = (ref[at].astype(F32) + more.astype(F32)).astype(BF)
+
+    def y_first(name):
+        own, ybuf, zbuf, fin, ys, yr, zs, zr, fs, fr = parts_of(name)
+        f_begin, relay, rest = finals(fin, fs, fr)
+
+        def y_copy(t):
+            src = own.at[z_order[t] * 2 + (1 - y)]
+            return push(src, ybuf.at[t], ys.at[t], yr.at[t], (other_y, head))
+
+        def near_copy(t):
+            return push(own.at[z_order[t] * 2 + y], zbuf.at[t], zs.at[t], zr.at[t], (beside * 2 + y, head))
+
+        def across_copy(t):
+            shard = z_order[t] * 2 + y
+            return push(own.at[shard], zbuf.at[3], zs.at[t], zr.at[3], (shard, head))
+
+        def begin():
+            for t in range(4):
+                start(lambda t=t: y_copy(t))
+
+        def pair(t):
+            y_copy(t).wait_recv()
+            add_to(own, z_order[t] * 2 + y, ybuf[t])
+            if t == 2:
+                near_copy(t).start()
+            elif t < 2:
+                pl.when(outer)(lambda: near_copy(t).start())
+
+        def fold(t):
+            @pl.when(inner)
+            def _():
+                near_copy(t).wait_recv()
+                add_to(own, z_order[t] * 2 + y, zbuf[t])
+                across_copy(t).start()
+
+        def total_up():
+            near_copy(2).wait_recv()
+            across_copy(0).wait_recv()
+            fin[head] = (own[dp].astype(F32) + zbuf[2].astype(F32) + zbuf[3].astype(F32)).astype(BF)
+            f_begin()
+            sent.append((lambda: near_copy(2), None))
+            for t in (0, 1):
+                sent.append((lambda t=t: near_copy(t), outer))
+                sent.append((lambda t=t: across_copy(t), inner))
+
+        return begin, pair, fold, total_up, relay, rest
+
+    def z_first(name):
+        own, ybuf, zbuf, fin, ys, yr, zs, zr, fs, fr = parts_of(name)
+        f_begin, relay, rest = finals(fin, fs, fr)
+
+        def both(t):
+            return pl.ds(z_order[t] * 2, 2)
+
+        def near_copy(t):
+            return push(own.at[both(t)], zbuf.at[t], zs.at[t], zr.at[t], (beside * 2 + y, head))
+
+        def across_copy(t):
+            return push(own.at[both(t)], zbuf.at[3], zs.at[t], zr.at[3], (z_order[t] * 2 + y, head))
+
+        def y_copy():
+            return push(own.at[z * 2 + (1 - y)], ybuf.at[0], ys.at[0], yr.at[0], (other_y, head))
+
+        def begin():
+            for t in (0, 1):
+                start(lambda t=t: near_copy(t), outer)
+            start(lambda: near_copy(2))
+
+        def fold(t):
+            @pl.when(inner)
+            def _():
+                near_copy(t).wait_recv()
+                add_to(own, both(t), zbuf[t])
+                across_copy(t).start()
+
+        def pair():
+            near_copy(2).wait_recv()
+            across_copy(0).wait_recv()
+            add_to(own, both(3), zbuf[2].astype(F32) + zbuf[3].astype(F32))
+            y_copy().start()
+
+        def total_up():
+            y_copy().wait_recv()
+            fin[head] = (own[dp].astype(F32) + ybuf[0].astype(F32)).astype(BF)
+            f_begin()
+            for t in (0, 1):
+                sent.append((lambda t=t: across_copy(t), inner))
+            sent.append((y_copy, None))
+
+        return begin, fold, pair, total_up, relay, rest
+
+    def direct(name):
+        own, ybuf, zbuf, fin, ys, yr, zs, zr, fs, fr = parts_of(name)
+        f_begin, relay, rest = finals(fin, fs, fr)
+
+        def y_copy(k):
+            src = own.at[z_shard(k) * 2 + (1 - y)]
+            return push(src, ybuf.at[k], ys.at[k], yr.at[k], (other_y, head))
+
+        def z_copy(k):
+            shard = z_shard(k) * 2 + y
+            return push(own.at[shard], zbuf.at[k], zs.at[k], zr.at[k], (shard, head))
+
+        def begin():
+            for k in (2, 1, 3, 0):
+                start(lambda k=k: y_copy(k))
+
+        def pair(k):
+            y_copy(k).wait_recv()
+            add_to(own, z_shard(k) * 2 + y, ybuf[k])
+            if k:
+                start(lambda: z_copy(k))
+
+        def total_up():
+            value = own[dp].astype(F32)
+            for k in (1, 2, 3):
+                z_copy(k).wait_recv()
+                value += zbuf[k].astype(F32)
+            fin[head] = value.astype(BF)
+            f_begin()
+
+        return begin, pair, total_up, relay, rest
+
+    def irregular(name, number_of, owner_of, straight):
+        own, ybuf, zbuf, fin, ys, yr, zs, zr, fs, fr = parts_of(name)
+
+        def facts(j):
+            number = number_of(j)
+            shard = lax.div(number, 3)
+            return shard, lax.div(shard, 2), lax.rem(shard, 2), lax.rem(number, 3)
+
+        def y_copy(j):
+            return push(own.at[j], ybuf.at[j], ys.at[j], yr.at[j], (other_y, head))
+
+        def near_copy(j):
+            slot = jnp.where(facts(j)[1] == beside, 6 + facts(j)[3], j)
+            return push(own.at[j], zbuf.at[slot], zs.at[j], zr.at[slot], (beside * 2 + y, head))
+
+        def near_arrival(j):
+            return push(own.at[j], zbuf.at[j], zs.at[j], zr.at[j], (beside * 2 + y, head))
+
+        def across_copy(j):
+            shard, _, _, place = facts(j)
+            return push(own.at[j], zbuf.at[9 + place], zs.at[j], zr.at[9 + place], (shard, head))
+
+        def z_copy(j):
+            shard, shard_z, _, place = facts(j)
+            slot = (lax.rem(shard_z + 4 - z, 4) - 1) * 3 + place
+            return push(own.at[j], zbuf.at[slot], zs.at[j], zr.at[slot], (shard, head))
+
+        def last_arrival(j, base):
+            place = base + facts(j)[3]
+            return push(own.at[j], zbuf.at[place], zs.at[j], zr.at[place], (dp, sib)), place
+
+        def f_copy(code, place):
+            index = (code - 1) * 3 + place
+            to = far if code == 2 else sib
+            return push(fin.at[place], fin.at[place], fs.at[index], fr.at[index], (dp, to))
+
+        def begin(these=range(6)):
+            for j in these:
+                start(lambda j=j: y_copy(j), facts(j)[2] != y)
+
+        def mine(j):
+            return facts(j)[2] == y
+
+        def other_half(j):
+            return lax.div(facts(j)[1], 2) != half
+
+        def to_near(j):
+            return mine(j) & ((facts(j)[1] == beside) | (other_half(j) & outer))
+
+        def to_across(j):
+            return mine(j) & other_half(j) & inner
+
+        def fold(j):
+            @pl.when(to_across(j))
+            def _():
+                near_arrival(j).wait_recv()
+                add_to(own, j, zbuf[j])
+                across_copy(j).start()
+
+        def to_shard(j):
+            return mine(j) & (facts(j)[1] != z)
+
+        def pair(j):
+            @pl.when(mine(j))
+            def _():
+                y_copy(j).wait_recv()
+                add_to(own, j, ybuf[j])
+
+            if straight:
+                pl.when(to_shard(j))(lambda: z_copy(j).start())
+            else:
+                pl.when(to_near(j))(lambda: near_copy(j).start())
+
+        def total_up():
+            for j in range(6):
+                if straight:
+                    sent.append((lambda j=j: z_copy(j), to_shard(j)))
+                else:
+                    sent.append((lambda j=j: near_copy(j), to_near(j)))
+                    sent.append((lambda j=j: across_copy(j), to_across(j)))
+                shard, _, _, place = facts(j)
+
+                def body(j=j, place=place):
+                    value = own[j].astype(F32)
+                    for base in (0, 3, 6) if straight else (6, 9):
+                        copy, slot = last_arrival(j, base)
+                        copy.wait_recv()
+                        value += zbuf[slot].astype(F32)
+                    fin[place] = value.astype(BF)
+                    f_copy(2, place).start()
+                    f_copy(1, place).start()
+
+                pl.when(shard == dp)(body)
+
+        def relay():
+            for place in range(3):
+                owner = owner_of(3 * dp + place)
+                for code in (1, 2):
+                    sent.append((lambda code=code, place=place: f_copy(code, place), owner == head))
+
+                def body(place=place):
+                    f_copy(2, place).wait_recv()
+                    f_copy(3, place).start()
+
+                pl.when(owner == far)(body)
+                sent.append((lambda place=place: f_copy(3, place), owner == far))
+
+        def rest():
+            for place in range(3):
+                owner = owner_of(3 * dp + place)
+                for code, source in ((1, sib), (3, diag)):
+                    pl.when(owner == source)(lambda code=code, place=place: f_copy(code, place).wait_recv())
+
+        return begin, pair, fold, total_up, relay, rest
+
+    dy_begin, dy_pair, dy_fold, dy_total, dy_relay, dy_rest = y_first("dy")
+    dz_begin, dz_fold, dz_pair, dz_total, dz_relay, dz_rest = z_first("dz")
+    ou_begin, ou_pair, ou_total, ou_relay, ou_rest = direct("ou")
+    up_begin, up_pair, up_fold, up_total, up_relay, up_rest = irregular(
+        "up", lambda j: 4 * j + head, lambda number: lax.rem(number, 4), False
+    )
+    qk_begin, qk_pair, _, qk_total, qk_relay, qk_rest = irregular(
+        "qk",
+        lambda j: (j // 2) * 8 + 2 * head + j % 2,
+        lambda number: lax.div(lax.rem(number, 8), 2),
+        True,
+    )
+
+    down_grad = tn(r.dall[...], r.act[...]).astype(BF)
+    r.pdz[...] = down_grad[:, 384:].reshape(8, 96, 384)
+    dz_begin()
+    r.pdy[...] = down_grad[:, :384].reshape(8, 96, 384)
+    dy_begin()
+    up_grad = tn(r.sall[...], r.gup[...]).astype(BF)
+    for j in range(6):
+        r.pup[j] = up_grad[:, j * 128 : (j + 1) * 128]
+    up_begin()
+
     r.small[...] = jnp.zeros_like(r.small)
     for j in range(6):
         number = 4 * j + head
@@ -715,199 +1030,69 @@
             :, j * 128 : (j + 1) * 128
         ]
 
-    def regular(name):
-        own, ybuf, zbuf, fin = (getattr(r, part + name) for part in ("p", "y", "z", "f"))
-        sems = [getattr(r, part + name + end) for part in ("y", "z", "f") for end in ("s", "r")]
-        ys, yr, zs, zr, fs, fr = sems
-
-        def y_copy(k):
-            src = own.at[z_shard(k) * 2 + (1 - y)]
-            return push(src, ybuf.at[k], ys.at[k], yr.at[k], (other_y, head))
-
-        def z_copy(k):
-            shard = z_shard(k) * 2 + y
-            return push(own.at[shard], zbuf.at[k], zs.at[k], zr.at[k], (shard, head))
-
-        def f_copy(code):
-            place = far if code == 3 else head
-            to = far if code == 2 else sib
-            return push(fin.at[place], fin.at[place], fs.at[code - 1], fr.at[code - 1], (dp, to))
-
-        def begin():
-            for k in (1, 2, 3, 0):
-                start(lambda k=k: y_copy(k))
-
-        def pair(k, last=None):
-            y_copy(k).wait_recv()
-            at = z_shard(k) * 2 + y
-            own[at] = (own[at].astype(F32) + ybuf[k].astype(F32)).astype(BF)
-            if isinstance(k, int):
-                if k:
-                    start(lambda: z_copy(k))
+    q_aug, g_aug = r.act, r.gup
+    tile_lane = lanes_of(128)
+    spot_row, spot_lane = (lax.broadcasted_iota(jnp.int32, (128, 128), axis) for axis in (0, 1))
+    spots = [
+        jnp.where((spot_lane == 68 + lax.div(spot_row, 3)) & (lax.rem(spot_row, 3) == n) & (spot_row < 9), 1.0, 0.0)
+        for n in range(3)
+    ]
+    spots = [spot.astype(BF) for spot in spots]
+
+    def aux_of(columns):
+        high, middle, low = split_three(columns)
+        return (high + pltpu.roll(middle, 3, 1) + pltpu.roll(low, 6, 1)).astype(BF)
+
+    def write_aug(dst, rows, source, aux, keep):
+        left = source[:, :128]
+        right = source[:, 128:].astype(F32)
+        for n in range(3):
+            if n < 2:
+                part = left * jnp.where(lax.div(tile_lane, 64) == n, 1.0, 0.0).astype(BF)
             else:
-
-                @pl.when(k > 0)
-                def _():
-                    z_copy(k).start()
-
-        def total_up():
-            for k in (1, 2, 3):
-                z_copy(k).wait_recv()
-            value = own[dp].astype(F32)
-            for k in (1, 2, 3):
-                value += zbuf[k].astype(F32)
-            fin[head] = value.astype(BF)
-            for code in (2, 1):
-                start(lambda code=code: f_copy(code))
-
-        def relay():
-            f_copy(2).wait_recv()
-            start(lambda: f_copy(3))
-
-        def rest():
-            f_copy(1).wait_recv()
-            f_copy(3).wait_recv()
-
-        def pair_sends():
-            for k in (1, 2, 3):
-                sent.append((lambda k=k: z_copy(k), None))
-
-        return begin, pair, total_up, relay, rest, pair_sends
-
-    def irregular(name, number_of, owner_of):
-        own, ybuf, zbuf, fin = (getattr(r, part + name) for part in ("p", "y", "z", "f"))
-        sems = [getattr(r, part + name + end) for part in ("y", "z", "f") for end in ("s", "r")]
-        ys, yr, zs, zr, fs, fr = sems
-
-        def facts(j):
-            number = number_of(j)
-            shard = lax.div(number, 3)
-            return shard, lax.div(shard, 2), lax.rem(shard, 2), lax.rem(number, 3)
-
-        def y_copy(j):
-            return push(own.at[j], ybuf.at[j], ys.at[j], yr.at[j], (other_y, head))
-
-        def z_copy(j):
-            shard, shard_z, shard_y, place = facts(j)
-            slot = (lax.rem(shard_z + 4 - z, 4) - 1) * 3 + place
-            return push(own.at[j], zbuf.at[slot], zs.at[j], zr.at[slot], (shard, head))
-
-        def z_arrival(j, k):
-            slot = (k - 1) * 3 + facts(j)[3]
-            return push(own.at[j], zbuf.at[slot], zs.at[j], zr.at[slot], (dp, sib)), slot
-
-        def f_copy(code, place):
-            index = (code - 1) * 3 + place
-            to = far if code == 2 else sib
-            return push(fin.at[place], fin.at[place], fs.at[index], fr.at[index], (dp, to))
-
-        def begin(these=range(6)):
-            for j in these:
-                start(lambda j=j: y_copy(j), facts(j)[2] != y)
-
-        def z_goes(j):
-            shard, shard_z, shard_y, place = facts(j)
-            return (shard_y == y) & (shard_z != z)
-
-        def pair(j):
-            @pl.when(facts(j)[2] == y)
-            def _():
-                y_copy(j).wait_recv()
-                own[j] = (own[j].astype(F32) + ybuf[j].astype(F32)).astype(BF)
-
-            @pl.when(z_goes(j))
-            def _():
-                z_copy(j).start()
-
-        def pair_sends():
-            for j in range(6):
-                sent.append((lambda j=j: z_copy(j), z_goes(j)))
-
-        def total_up():
-            for j in range(6):
-                shard, shard_z, shard_y, place = facts(j)
-
-                def body(j=j, place=place):
-                    value = own[j].astype(F32)
-                    for k in (1, 2, 3):
-                        copy, slot = z_arrival(j, k)
-                        copy.wait_recv()
-                        value += zbuf[slot].astype(F32)
-                    fin[place] = value.astype(BF)
-                    f_copy(2, place).start()
-                    f_copy(1, place).start()
-
-                pl.when(shard == dp)(body)
-
-        def relay():
-            for place in range(3):
-                owner = owner_of(3 * dp + place)
-                for code in (1, 2):
-                    sent.append((lambda code=code, place=place: f_copy(code, place), owner == head))
-
-                def body(place=place):
-                    f_copy(2, place).wait_recv()
-                    f_copy(3, place).start()
-
-                pl.when(owner == far)(body)
-                sent.append((lambda place=place: f_copy(3, place), owner == far))
-
-        def rest():
-            for place in range(3):
-                owner = owner_of(3 * dp + place)
-                for code, source in ((1, sib), (3, diag)):
-                    pl.when(owner == source)(lambda code=code, place=place: f_copy(code, place).wait_recv())
-
-        return begin, pair, total_up, relay, rest, pair_sends
-
-    dn_begin, dn_pair, dn_total, dn_relay, dn_rest, dn_sends = regular("dn")
-    ou_begin, ou_pair, ou_total, ou_relay, ou_rest, ou_sends = regular("ou")
-    up_begin, up_pair, up_total, up_relay, up_rest, up_sends = irregular(
-        "up", lambda j: 4 * j + head, lambda number: lax.rem(number, 4)
-    )
-    qk_begin, qk_pair, qk_total, qk_relay, qk_rest, qk_sends = irregular(
-        "qk",
-        lambda j: (j // 2) * 8 + 2 * head + j % 2,
-        lambda number: lax.div(lax.rem(number, 8), 2),
-    )
-
-    r.pdn[...] = tn(r.dall[...], r.act[...]).astype(BF).reshape(8, 96, D)
-    dn_begin()
-    r.pup[...] = tn(r.gup[...], r.sall[...]).astype(BF).reshape(6, 128, D)
-    up_begin()
-
+                part = jnp.zeros((256, 128), BF)
+            dst[rows, n * 256 : n * 256 + 128] = part
+            mask = jnp.where(tile_lane < 64, 1.0 if n == 2 else 0.0, keep)
+            dst[rows, n * 256 + 128 : (n + 1) * 256] = (right * mask + nn(aux, spots[n])).astype(BF)
+
+    def augment_q(block, carry):
+        rows = pl.ds(pl.multiple_of(block * 256, 256), 256)
+        write_aug(q_aug, rows, r.qb[rows, :], aux_of(-r.lse[rows, :]), 1.0)
+        return carry
+
+    lax.fori_loop(0, 4, augment_q, 0)
+    sum_row, sum_lane = (lax.broadcasted_iota(jnp.int32, (256, 128), axis) for axis in (0, 1))
+    head_sums = jnp.where((lax.div(sum_row, 64) == sum_lane) & (sum_row < 192), 1.0, 0.0).astype(BF)
+    r.woo[192:256, :] = jnp.zeros((64, D), BF)
+    dy_pair(0)
+    dy_pair(1)
+    dz_fold(0)
     l_wait(0)
+    l_relay()
     l_rest()
-    r.woo[192:256, :] = jnp.zeros((64, D), BF)
     r.gm[...] = nt(r.lall[...], r.woo[...]).astype(BF)
-    r.pou[...] = tn(r.lall[...], r.mix[...]).astype(BF).reshape(8, 96, 256)
-    ou_begin()
-    q_aug, g_aug = r.act, r.gup
-    for n in range(3):
-        mask = head_mask(n)
-
-        def augment(block, carry, n=n, mask=mask):
-            rows = pl.ds(pl.multiple_of(block * 256, 256), 256)
-            grads = r.gm[rows, :].astype(F32) * mask
-            inner = jnp.sum(grads * r.exact[rows, :], axis=1, keepdims=True)
-            queries = r.qb[rows, :].astype(F32) * (mask + on_aux)
-            for place, part in enumerate(split_three(-r.lse[rows, :][:, n : n + 1])):
-                queries = queries + part * lane_is(196 + place)
-            for place, part in enumerate(split_three(-inner)):
-                grads = grads + part * lane_is(196 + place)
-            q_aug[rows, n * 256 : (n + 1) * 256] = queries.astype(BF)
-            g_aug[rows, n * 256 : (n + 1) * 256] = grads.astype(BF)
-            return carry
-
-        lax.fori_loop(0, 4, augment, 0)
+
+    def augment_g(block, carry):
+        rows = pl.ds(pl.multiple_of(block * 256, 256), 256)
+        grads = r.gm[rows, :]
+        product = grads.astype(F32) * r.exact[rows, :]
+        inner = jnp.zeros((256, 128), F32)
+        for part in split_three(product):
+            inner += nn(part.astype(BF), head_sums)
+        write_aug(g_aug, rows, grads, aux_of(-inner), 0.0)
+        return carry
+
+    lax.fori_loop(0, 4, augment_g, 0)
+    dy_pair(2)
+    dy_pair(3)
+    dz_fold(1)
 
     def kv_copy(code):
         rows = block_rows(peer(code))
         return push(r.dkv.at[rows, :], r.kvin.at[head], r.kvs.at[code - 1], r.kvr.at[code - 1], (dp, peer(code)))
 
     def q_copy(code):
-        rows = block_rows(peer(code))
-        return push(r.dq.at[rows, :], r.qin.at[head], r.qs.at[code - 1], r.qr.at[code - 1], (dp, peer(code)))
+        return push(r.qs_.at[code], r.qin.at[head], r.qs.at[code - 1], r.qr.at[code - 1], (dp, peer(code)))
 
     def attend_back(step, carry):
         code = 3 - step
@@ -930,12 +1115,28 @@
         def _():
             kv_copy(code).start()
 
-        dn_pair(lax.rem(step + 1, 4))
-        up_pair(step)
+        @pl.when(step == 1)
+        def _():
+            dz_pair()
+            up_pair(0)
+            up_pair(1)
+
+        @pl.when(step == 2)
+        def _():
+            dy_fold(0)
+            up_pair(2)
+
+        @pl.when(step == 3)
+        def _():
+            dy_fold(1)
+            up_pair(3)
+
         return carry
 
     lax.fori_loop(0, 4, attend_back, 0)
     r.kvin[head] = r.dkv[block_rows(head), :]
+    r.pqk[2:6] = tn(r.dkv[...], r.nall[...]).astype(BF).reshape(4, 96, D)
+    qk_begin(range(2, 6))
 
     def query_back(step, carry):
         code = 3 - step
@@ -945,7 +1146,9 @@
         for n in range(3):
             part = r.big[n * SLOT : (n + 1) * SLOT, pl.ds(pl.multiple_of(block * BLOCK, 256), BLOCK)]
             query_grad += tn(part, r.kb[...] * head_mask(n).astype(BF))
-        r.dq[rows, :] = (query_grad * 0.125).astype(BF)
+        query_grad = query_grad * 0.125
+        r.dq[rows, :] = query_grad.astype(BF)
+        r.qs_[code] = packed(query_grad)
 
         @pl.when(step < 3)
         def _():
@@ -954,33 +1157,32 @@
         return carry
 
     lax.fori_loop(0, 4, query_back, 0)
-    r.qin[head] = r.dq[block_rows(head), :]
-    up_pair(4)
-    up_pair(5)
-    for k in (1, 2, 3, 0):
-        ou_pair(k)
-    dn_sends()
-    up_sends()
-    r.pqk[2:6] = tn(r.dkv[...], r.nall[...]).astype(BF).reshape(4, 96, D)
-    qk_begin(range(2, 6))
+    r.qin[head] = r.qs_[0]
     r.pqk[0:2] = tn(r.dq[...], r.nall[...])[:192].astype(BF).reshape(2, 96, D)
     qk_begin(range(2))
+    for j in (4, 5):
+        up_pair(j)
+    r.pou[...] = tn(r.lall[...], r.mix[...]).astype(BF).reshape(8, 96, 256)
+    ou_begin()
+    up_fold(0)
+    up_fold(1)
+    dy_total()
     query_sum = jnp.sum(r.dq[...].astype(F32), axis=0, keepdims=True)
     value_sum = jnp.sum(r.dkv[:, 128:384].astype(F32), axis=0, keepdims=True)
     for group in range(4):
         mine = jnp.where(head == group, 1.0, 0.0)
         r.vec[4:5, group * 192 : (group + 1) * 192] = query_sum[:, :192] * mine
         r.vec[5:6, group * 192 : (group + 1) * 192] = value_sum[:, 64:] * mine
-    dn_total()
-    up_total()
-    ou_total()
+    dz_total()
+    up_fold(2)
+    qk_pair(2)
 
     for code in (3, 2, 1):
         kv_copy(code).wait_recv()
         q_copy(code).wait_recv()
+    unpack(r.qin, r.wuo, 0)
     for group in range(4):
         lanes = slice(group * 192, (group + 1) * 192)
-        r.wuo[0:256, lanes] = r.qin[group][:, :192]
         r.wuo[256:512, lanes] = r.kvin[group][:, :192]
         r.wuo[512:768, lanes] = r.kvin[group][:, 192:]
     grad_first = nt(r.wuo[0:256, :], r.wqkv[:, 0:D])
@@ -1005,27 +1207,38 @@
         return push(r.fsm.at[head], r.fsm.at[head], r.fsms.at[code - 1], r.fsmr.at[code - 1], (dp, peer(code)))
 
     start(small_y)
-    for step in (2, 3, 4, 5, 0, 1):
-        qk_pair(step)
-    qk_sends()
+    up_fold(3)
+    qk_pair(3)
+    up_fold(4)
+    up_fold(5)
+    for j in (4, 5):
+        qk_pair(j)
+    qk_pair(0)
+    qk_pair(1)
+    for k in (2, 1, 3, 0):
+        ou_pair(k)
+    dy_relay()
+    dz_relay()
+    up_total()
     small_y().wait_recv()
     r.small[y] = r.small[y] + r.ysm[...]
     for k in (1, 2, 3):
         start(lambda k=k: small_z(k))
-    dn_relay()
+    qk_total()
+    ou_total()
     up_relay()
-    ou_relay()
-    qk_total()
     for k in (1, 2, 3):
         small_z(k).wait_recv()
     r.fsm[head] = r.small[y, z] + r.zsm[1] + r.zsm[2] + r.zsm[3]
     for code in (2, 3, 1):
         start(lambda code=code: small_f(code))
     qk_relay()
-    dn_rest()
+    ou_relay()
+    dy_rest()
+    dz_rest()
     up_rest()
+    qk_rest()
     ou_rest()
-    qk_rest()
     for code in (2, 3, 1):
         small_f(code).wait_recv()
     r.fsum[...] = r.fsm[0] + r.fsm[1] + r.fsm[2] + r.fsm[3]
@@ -1037,14 +1250,61 @@
         q_copy(code).wait_send()
 
 
+def emit_kernel(
+    block_in, inputs_in, fup, fqk, fdy, fdz, fou, fsum,
+    block_out, grad_inputs, gains, shifts, qkv, qv_bias, out, out_biases, up, up_bias, down,
+    block_v, inputs_v, fup_v, fqk_v, fdy_v, fdz_v, fou_v, fsum_v, up_v, qkv_v, down_v, out_v, sems,
+):
+    count = []
+
+    def begin(src, dst):
+        count.append(pltpu.make_async_copy(src, dst, sems.at[len(count)]))
+        count[-1].start()
+        return count[-1]
+
+    pairs = (
+        (fdy, fdy_v), (fdz, fdz_v), (fup, fup_v), (inputs_in, inputs_v), (block_in, block_v), (fqk, fqk_v), (fou, fou_v),
+        (fsum, fsum_v),
+    )
+    arrivals = [begin(src, dst) for src, dst in pairs]
+    results = []
+    arrivals[0].wait()
+    arrivals[1].wait()
+    for group in range(4):
+        for j in range(6):
+            place = (4 * j + group) * 128
+            source, at = (fdy_v, j * 128) if j < 3 else (fdz_v, j * 128 - 384)
+            down_v[:, place : place + 128] = source[group, :, at : at + 128].astype(F32)
+    results.append(begin(down_v, down))
+    arrivals[2].wait()
+    for i in range(3):
+        up_v[:, i * 128 : (i + 1) * 128] = fup_v[i].astype(F32)
+    results.append(begin(up_v, up))
+    for arrival, src, dst in ((3, inputs_v, grad_inputs), (4, block_v, block_out)):
+        arrivals[arrival].wait()
+        results.append(begin(src, dst))
+    arrivals[5].wait()
+    qkv_v[...] = fqk_v[...].reshape(288, D).astype(F32)
+    results.append(begin(qkv_v, qkv))
+    arrivals[6].wait()
+    for group in range(4):
+        out_v[:, group * 192 : (group + 1) * 192] = fou_v[group][:, :192].astype(F32)
+    results.append(begin(out_v, out))
+    arrivals[7].wait()
+    for index, ref in enumerate((gains, shifts, qv_bias, out_biases)):
+        ref[...] = fsum_v[2 * index : 2 * index + 2, 0:96]
+    up_bias[...] = fsum_v[8:11, :]
+    for copy in results:
+        copy.wait()
+
+
 def per_device(x, norm_gains, norm_shifts, w_qkv, qv_bias, w_out, out_biases, w_up, up_bias, w_down, lengths, d_out):
-    full_bias = jnp.concatenate([qv_bias[0], jnp.zeros_like(qv_bias[0]), qv_bias[1]]).astype(F32).reshape(1, 3 * D)
     values = dict(
-        x=x[0], gains=norm_gains, shifts=norm_shifts, w_qkv=w_qkv, full_bias=full_bias, w_out=w_out, biases=out_biases,
-        w_up=w_up, up_bias=up_bias.astype(F32).reshape(1, FF), w_down=w_down, lengths=lengths, d_out=d_out[0],
+        x=x[0], gains=norm_gains, shifts=norm_shifts, w_qkv=w_qkv, qv_bias=qv_bias, w_out=w_out, biases=out_biases,
+        w_up=w_up, up_bias=up_bias.reshape(1, FF), w_down=w_down, lengths=lengths, d_out=d_out[0],
     )
     place = {True: pl.BlockSpec(memory_space=pl.ANY), False: pl.BlockSpec(memory_space=pltpu.VMEM)}
-    block_out, grad_inputs, fup, fqk, fdn, fou, fsum = pl.pallas_call(
+    block_out, grad_inputs, fup, fqk, fdy, fdz, fou, fsum = pl.pallas_call(
         one_kernel,
         out_shape=[jax.ShapeDtypeStruct(shape, kind) for _, shape, kind in OUTPUTS],
         in_specs=[place[name in IN_PLACE] for name in INPUTS],
@@ -1056,19 +1316,22 @@
         ),
         name="block",
     )(*(values[name] for name in INPUTS))
-    down = fdn.reshape(4, 96, 6, 128).transpose(2, 0, 3, 1).reshape(FF, 96)
+    anywhere = pl.BlockSpec(memory_space=pl.ANY)
+    shapes = [(256, D), (256, D), (2, 96), (2, 96), (288, D), (2, 96), (96, D), (2, 96), (D, 384), (3, 128), (96, FF)]
+    outs = pl.pallas_call(
+        emit_kernel,
+        out_shape=[jax.ShapeDtypeStruct(shape, F32 if n else BF) for n, shape in enumerate(shapes)],
+        in_specs=[anywhere] * 8,
+        out_specs=[anywhere] * 2 + [anywhere if shape[0] > 16 else place[False] for shape in shapes[2:]],
+        scratch_shapes=[pltpu.VMEM(shape, kind) for _, shape, kind in OUTPUTS]
+        + [pltpu.VMEM(shape, F32) for shape in ((D, 384), (288, D), (96, FF), (96, D))]
+        + [pltpu.SemaphoreType.DMA((14,))],
+        compiler_params=pltpu.CompilerParams(vmem_limit_bytes=VMEM_LIMIT),
+        name="emit",
+    )(block_out, grad_inputs, fup, fqk, fdy, fdz, fou, fsum)
     return (
-        block_out[None],
-        grad_inputs[None],
-        fsum[0:2, 0:96],
-        fsum[2:4, 0:96],
-        fqk.reshape(288, D).T.astype(F32),
-        fsum[4:6, 0:96],
-        fou[:, :, :192].transpose(0, 2, 1).reshape(D, 96).astype(F32),
-        fsum[6:8, 0:96],
-        fup.reshape(384, D).T.astype(F32),
-        fsum[8:11].reshape(384),
-        down.astype(F32),
+        outs[0][None], outs[1][None], outs[2], outs[3], outs[4].T, outs[5], outs[6].T, outs[7], outs[8],
+        outs[9].reshape(384), outs[10].T,
     )
 
 

time: 138 us -> 111 us (0.80)
  Pallas kernels: 122 us -> 107 us
  local copies, waits for them, and re-layouts: 11.6 us -> 1.3 us
  other arithmetic: 3.05 us -> 0 us
    pallas_call x1, Pallas kernels: 122 us -> 103 us  [per_device(): pl.pallas_call(one_kernel, out_shape=[jax.ShapeDtypeStruct(shape, kind) f...]
    convert_element_type x6 -> x0, local copies, waits for them, and re-layouts: 6.56 us -> none  [the longest x3 3.95 us: per_device(): down.astype(F32)]
    pallas_call x0 -> x1, Pallas kernels: none -> 4.1 us  [per_device(): pl.pallas_call(emit_kernel, out_shape=[jax.ShapeDtypeStruct(shape, F32 if...]
    slice x2 -> x0, local copies, waits for them, and re-layouts: 2.17 us -> none  [the longest x1 1.4 us: per_device(): fsum[6:8, 0:96]]
    convert_element_type x4 -> x0, other arithmetic: 1.75 us -> none  [the longest x1 1 us: per_device(): fqk.reshape(288, D).T.astype(F32)]
    unnamed x12 -> x0, local copies, waits for them, and re-layouts: 1.65 us -> none
where the time goes in v3:
time: 111 us; the launch traced here: 109 us
  Pallas kernels  107 us (96%)
  local copies, waits for them, and re-layouts  1.3 us (1%)
    pallas_call x1, Pallas kernels, per_device(): pl.pallas_call(one_kernel, out_shape=[jax.ShapeDtypeStruct(shape, kind) f...  103 us
    pallas_call x1, Pallas kernels, per_device(): pl.pallas_call(emit_kernel, out_shape=[jax.ShapeDtypeStruct(shape, F32 if...  4.1 us

profile of v3, /device:TPU:3, one launch (start us, length us, event | category | flops | bytes accessed | tf_op | source)
XLA Modules:
  0.0 109.4 jit_solution(9112379477377291148)
XLA Ops:
  0.6 1.3 %reshape.28.args_8_ = bf16[1,3072]{1,0:T(2,128)(2,1)} reshape(bf16[3072]{0:T(1024)(128)(2,1)} %param.20) | data formatting | bytes 12288 | tf_op jit(solution)/shard_map/reshape | solution.py:1304
  1.9 103.1 %block.1 = (bf16[256,768]{1,0:T(8,128)(2,1)}, f32[256,768]{1,0:T(8,128)}, bf16[3,768,128]{2,1,0:T(8,128)(2,1)}, bf16[3,96,768]{2,1,0:T(8,128)(2,1)}, bf16[4,96,3...) custom-call(bf16[256,768]{1,0:T(8,128)(2,1)} %bitcast.8, ...), custom_call_target="tpu_custom_call" | custom-call | tf_op jit(solution)/shard_map/block/pallas_call | solution.py:1307
  105.1 4.1 %emit.1 = (bf16[256,768]{1,0:T(8,128)(2,1)}, f32[256,768]{1,0:T(8,128)}, f32[2,96]{1,0:T(2,128)}, f32[2,96]{1,0:T(2,128)}, f32[288,768]{1,0:T(8,128)}, /*index=5...) custom-call(bf16[256,768]{1,0:T(8,128)(2,1)} %get-tuple-element.30.b, ...), custom_call_target="tpu_custom_call" | custom-call | tf_op jit(solution)/shard_map/emit/pallas_call | solution.py:1321

commit v4 on v3

--- a/solution.py
+++ b/solution.py
@@ -399,42 +399,40 @@
     ("gh", (256, D), F32),
     ("act", (SLOT, D), BF),
     ("gup", (SLOT, D), BF),
-    ("gm", (SLOT, 256), BF),
-    ("dkv", (SLOT, 384), BF),
-    ("dq", (SLOT, 256), BF),
     ("kvin", (4, 256, 384), BF),
     ("qs_", (4, 384, 128), BF),
     ("qin", (4, 384, 128), BF),
-    ("pdy", (8, 96, 384), BF),
-    ("pdz", (8, 96, 384), BF),
+    ("pdy", (8, 96, 256), BF),
+    ("pdz", (8, 96, 512), BF),
     ("pup", (6, D, 128), BF),
-    ("pou", (8, 96, 256), BF),
-    ("pqk", (6, 96, D), BF),
-    ("ydy", (4, 96, 384), BF),
-    ("ydz", (1, 96, 384), BF),
+    ("pou", (8, 144, 128), BF),
+    ("pqk", (12, 48, D), BF),
+    ("ydy", (4, 96, 256), BF),
+    ("ydz", (1, 96, 512), BF),
     ("yup", (6, D, 128), BF),
-    ("you", (4, 96, 256), BF),
-    ("yqk", (6, 96, D), BF),
-    ("zdy", (4, 96, 384), BF),
-    ("zdz", (4, 2, 96, 384), BF),
+    ("you", (4, 144, 128), BF),
+    ("yqk", (12, 48, D), BF),
+    ("zdy", (4, 96, 256), BF),
+    ("zdz", (4, 2, 96, 512), BF),
     ("zup", (12, D, 128), BF),
-    ("zou", (4, 96, 256), BF),
-    ("zqk", (9, 96, D), BF),
+    ("zou", (4, 144, 128), BF),
+    ("zqk", (24, 48, D), BF),
     ("vec", (8, D), F32),
+    ("bias_rows", (24, 128), F32),
     ("small", (2, 4, 16, 128), F32),
     ("ysm", (4, 16, 128), F32),
     ("zsm", (4, 16, 128), F32),
     ("fsm", (4, 16, 128), F32),
 )
 SEMAPHORES = (
-    ("load", 22),
+    ("load", 22), ("give", 8),
     ("ns", 5), ("nr", 5), ("ds", 5), ("dr", 5), ("ss", 5), ("sr", 5), ("ls", 5), ("lr", 5),
     ("ms", 3), ("mr", 3), ("kvs", 3), ("kvr", 3), ("qs", 3), ("qr", 3),
     ("ydys", 4), ("ydyr", 4), ("zdys", 4), ("zdyr", 4), ("fdys", 3), ("fdyr", 3),
     ("ydzs", 1), ("ydzr", 1), ("zdzs", 4), ("zdzr", 4), ("fdzs", 3), ("fdzr", 3),
     ("yous", 4), ("your", 4), ("zous", 4), ("zour", 4), ("fous", 3), ("four", 3),
     ("yups", 6), ("yupr", 6), ("zups", 6), ("zupr", 12), ("fups", 9), ("fupr", 9),
-    ("yqks", 6), ("yqkr", 6), ("zqks", 6), ("zqkr", 9), ("fqks", 9), ("fqkr", 9),
+    ("yqks", 12), ("yqkr", 12), ("zqks", 12), ("zqkr", 24), ("fqks", 18), ("fqkr", 18),
     ("ysms", 1), ("ysmr", 1), ("zsms", 4), ("zsmr", 4), ("fsms", 3), ("fsmr", 3),
 )
 INPUTS = ("x", "gains", "shifts", "w_qkv", "qv_bias", "w_out", "biases", "w_up", "up_bias", "w_down", "lengths", "d_out")
@@ -443,10 +441,10 @@
     ("block_out", (256, D), BF),
     ("grad_inputs", (256, D), F32),
     ("fup", (3, D, 128), BF),
-    ("fqk", (3, 96, D), BF),
-    ("fdy", (4, 96, 384), BF),
-    ("fdz", (4, 96, 384), BF),
-    ("fou", (4, 96, 256), BF),
+    ("fqk", (6, 48, D), BF),
+    ("fdy", (4, 96, 256), BF),
+    ("fdz", (4, 96, 512), BF),
+    ("fou", (4, 144, 128), BF),
     ("fsum", (16, 128), F32),
 )
 
@@ -461,7 +459,7 @@
 
 def one_kernel(*args):
     r = Refs()
-    names = [*INPUTS] + [o[0] for o in OUTPUTS] + [b[0] for b in BUFFERS] + [s[0] for s in SEMAPHORES]
+    names = [*INPUTS] + ["to_" + o[0] for o in OUTPUTS] + [b[0] for b in OUTPUTS + BUFFERS] + [s[0] for s in SEMAPHORES]
     for name, ref in zip(names, args, strict=True):
         setattr(r, name, ref)
     dp, head = lax.axis_index("dp"), lax.axis_index("head")
@@ -497,6 +495,13 @@
             body()
         else:
             pl.when(cond)(body)
+
+    given = []
+
+    def give(name):
+        copy = pltpu.make_async_copy(getattr(r, name), getattr(r, "to_" + name), r.give.at[len(given)])
+        copy.start()
+        given.append(copy)
 
     def start(make, cond=None):
         when(cond, lambda: make().start())
@@ -550,7 +555,7 @@
 
         def begin(these=(1, 2, 0)):
             for index in these:
-                start(lambda index=index: copy_of(index))
+                copy_of(index).start()
 
         def wait(index):
             copy_of(index).wait_recv()
@@ -558,18 +563,22 @@
         def relay(these=(1, 2)):
             for index in these:
                 wait(index)
-                start(lambda index=index: copy_of(index + 2))
+                copy_of(index + 2).start()
 
         def rest():
             for index in (3, 4):
                 wait(index)
 
-        return begin, wait, relay, rest
-
-    n_begin, n_wait, n_relay, n_rest = gather(r.nall, r.ns, r.nr)
-    d_begin, d_wait, d_relay, d_rest = gather(r.dall, r.ds, r.dr)
-    s_begin, s_wait, s_relay, s_rest = gather(r.sall, r.ss, r.sr)
-    l_begin, l_wait, l_relay, l_rest = gather(r.lall, r.ls, r.lr)
+        def drain():
+            for index in range(5):
+                copy_of(index).wait_send()
+
+        return begin, wait, relay, rest, drain
+
+    n_begin, n_wait, n_relay, n_rest, n_drain = gather(r.nall, r.ns, r.nr)
+    d_begin, d_wait, d_relay, d_rest, d_drain = gather(r.dall, r.ds, r.dr)
+    s_begin, s_wait, s_relay, s_rest, s_drain = gather(r.sall, r.ss, r.sr)
+    l_begin, l_wait, l_relay, l_rest, l_drain = gather(r.lall, r.ls, r.lr)
 
     loaded("x")
     first = norm_parts(r.xv[...].astype(F32), gains[0:1, :], shifts[0:1, :])[2]
@@ -662,10 +671,13 @@
         def _():
             mix_copy(code).start()
 
+        @pl.when(step == 1)
+        def _():
+            d_begin((2,))
+
         return carry
 
     lax.fori_loop(0, 4, attend, 0)
-    d_begin((2,))
     r.mixin[head] = r.mixs[0]
     d_relay((1,))
 
@@ -681,17 +693,20 @@
     r.sall[block_rows(head), :] = second
     s_begin()
     grad_low = r.dall[block_rows(head), :]
+    up_bias = r.up_bias[...].astype(F32)
+    r.bias_rows[...] = up_bias
     down = jnp.zeros((BLOCK, D), F32)
     back = jnp.zeros((BLOCK, D), F32)
     for tile in range(4):
         cut = slice(tile * D, (tile + 1) * D)
-        up = nn(second, r.wup[:, cut]) + r.up_bias[:, cut].astype(F32)
+        up = nn(second, r.wup[:, cut]) + jnp.concatenate([up_bias[6 * tile + i : 6 * tile + i + 1] for i in range(6)], axis=1)
         value, slope = gelu_parts(up)
         w_down = r.big[cut, 0:D]
         down += nn(value.astype(BF), w_down)
         grad_up = nt(grad_low, w_down) * slope
         back += nt(grad_up.astype(BF), r.wup[:, cut])
     r.block_out[...] = (hidden + down + biases[1:2, :]).astype(BF)
+    give("block_out")
     grad_block = grad_low.astype(F32)
     grad_hidden = grad_block + norm_back(back, unit, inverse, gains[1:2, :])
     r.gh[...] = grad_hidden
@@ -706,9 +721,7 @@
     loaded("wuo")
     loaded("wdo")
     loaded("woo")
-    own_bias = jnp.concatenate(
-        [r.up_bias[:, pl.ds(pl.multiple_of((4 * j + head) * 128, 128), 128)] for j in range(6)], axis=1
-    ).astype(F32)
+    own_bias = jnp.concatenate([r.bias_rows[pl.ds(4 * j + head, 1), :] for j in range(6)], axis=1)
 
     def feed(step, sums):
         @pl.when(step == 1)
@@ -852,51 +865,19 @@
 
         return begin, fold, pair, total_up, relay, rest
 
-    def direct(name):
-        own, ybuf, zbuf, fin, ys, yr, zs, zr, fs, fr = parts_of(name)
-        f_begin, relay, rest = finals(fin, fs, fr)
-
-        def y_copy(k):
-            src = own.at[z_shard(k) * 2 + (1 - y)]
-            return push(src, ybuf.at[k], ys.at[k], yr.at[k], (other_y, head))
-
-        def z_copy(k):
-            shard = z_shard(k) * 2 + y
-            return push(own.at[shard], zbuf.at[k], zs.at[k], zr.at[k], (shard, head))
-
-        def begin():
-            for k in (2, 1, 3, 0):
-                start(lambda k=k: y_copy(k))
-
-        def pair(k):
-            y_copy(k).wait_recv()
-            add_to(own, z_shard(k) * 2 + y, ybuf[k])
-            if k:
-                start(lambda: z_copy(k))
-
-        def total_up():
-            value = own[dp].astype(F32)
-            for k in (1, 2, 3):
-                z_copy(k).wait_recv()
-                value += zbuf[k].astype(F32)
-            fin[head] = value.astype(BF)
-            f_begin()
-
-        return begin, pair, total_up, relay, rest
-
-    def irregular(name, number_of, owner_of, straight):
+    def irregular(name, count, per_shard, number_of, owner_of):
         own, ybuf, zbuf, fin, ys, yr, zs, zr, fs, fr = parts_of(name)
 
         def facts(j):
             number = number_of(j)
-            shard = lax.div(number, 3)
-            return shard, lax.div(shard, 2), lax.rem(shard, 2), lax.rem(number, 3)
+            shard = lax.div(number, per_shard)
+            return shard, lax.div(shard, 2), lax.rem(shard, 2), lax.rem(number, per_shard)
 
         def y_copy(j):
             return push(own.at[j], ybuf.at[j], ys.at[j], yr.at[j], (other_y, head))
 
         def near_copy(j):
-            slot = jnp.where(facts(j)[1] == beside, 6 + facts(j)[3], j)
+            slot = jnp.where(facts(j)[1] == beside, count + facts(j)[3], j)
             return push(own.at[j], zbuf.at[slot], zs.at[j], zr.at[slot], (beside * 2 + y, head))
 
         def near_arrival(j):
@@ -904,23 +885,18 @@
 
         def across_copy(j):
             shard, _, _, place = facts(j)
-            return push(own.at[j], zbuf.at[9 + place], zs.at[j], zr.at[9 + place], (shard, head))
-
-        def z_copy(j):
-            shard, shard_z, _, place = facts(j)
-            slot = (lax.rem(shard_z + 4 - z, 4) - 1) * 3 + place
-            return push(own.at[j], zbuf.at[slot], zs.at[j], zr.at[slot], (shard, head))
+            return push(own.at[j], zbuf.at[count + per_shard + place], zs.at[j], zr.at[count + per_shard + place], (shard, head))
 
         def last_arrival(j, base):
             place = base + facts(j)[3]
             return push(own.at[j], zbuf.at[place], zs.at[j], zr.at[place], (dp, sib)), place
 
         def f_copy(code, place):
-            index = (code - 1) * 3 + place
+            index = (code - 1) * per_shard + place
             to = far if code == 2 else sib
             return push(fin.at[place], fin.at[place], fs.at[index], fr.at[index], (dp, to))
 
-        def begin(these=range(6)):
+        def begin(these=range(count)):
             for j in these:
                 start(lambda j=j: y_copy(j), facts(j)[2] != y)
 
@@ -943,32 +919,23 @@
                 add_to(own, j, zbuf[j])
                 across_copy(j).start()
 
-        def to_shard(j):
-            return mine(j) & (facts(j)[1] != z)
-
         def pair(j):
             @pl.when(mine(j))
             def _():
                 y_copy(j).wait_recv()
                 add_to(own, j, ybuf[j])
 
-            if straight:
-                pl.when(to_shard(j))(lambda: z_copy(j).start())
-            else:
-                pl.when(to_near(j))(lambda: near_copy(j).start())
-
-        def total_up():
-            for j in range(6):
-                if straight:
-                    sent.append((lambda j=j: z_copy(j), to_shard(j)))
-                else:
-                    sent.append((lambda j=j: near_copy(j), to_near(j)))
-                    sent.append((lambda j=j: across_copy(j), to_across(j)))
+            pl.when(to_near(j))(lambda: near_copy(j).start())
+
+        def total_up(these=range(count)):
+            for j in these:
+                sent.append((lambda j=j: near_copy(j), to_near(j)))
+                sent.append((lambda j=j: across_copy(j), to_across(j)))
                 shard, _, _, place = facts(j)
 
                 def body(j=j, place=place):
                     value = own[j].astype(F32)
-                    for base in (0, 3, 6) if straight else (6, 9):
+                    for base in (count, count + per_shard):
                         copy, slot = last_arrival(j, base)
                         copy.wait_recv()
                         value += zbuf[slot].astype(F32)
@@ -979,8 +946,8 @@
                 pl.when(shard == dp)(body)
 
         def relay():
-            for place in range(3):
-                owner = owner_of(3 * dp + place)
+            for place in range(per_shard):
+                owner = owner_of(per_shard * dp + place)
                 for code in (1, 2):
                     sent.append((lambda code=code, place=place: f_copy(code, place), owner == head))
 
@@ -992,8 +959,8 @@
                 sent.append((lambda place=place: f_copy(3, place), owner == far))
 
         def rest():
-            for place in range(3):
-                owner = owner_of(3 * dp + place)
+            for place in range(per_shard):
+                owner = owner_of(per_shard * dp + place)
                 for code, source in ((1, sib), (3, diag)):
                     pl.when(owner == source)(lambda code=code, place=place: f_copy(code, place).wait_recv())
 
@@ -1001,21 +968,21 @@
 
     dy_begin, dy_pair, dy_fold, dy_total, dy_relay, dy_rest = y_first("dy")
     dz_begin, dz_fold, dz_pair, dz_total, dz_relay, dz_rest = z_first("dz")
-    ou_begin, ou_pair, ou_total, ou_relay, ou_rest = direct("ou")
+    ou_begin, ou_pair, ou_fold, ou_total, ou_relay, ou_rest = y_first("ou")
     up_begin, up_pair, up_fold, up_total, up_relay, up_rest = irregular(
-        "up", lambda j: 4 * j + head, lambda number: lax.rem(number, 4), False
+        "up", 6, 3, lambda j: 4 * j + head, lambda number: lax.rem(number, 4)
     )
-    qk_begin, qk_pair, _, qk_total, qk_relay, qk_rest = irregular(
+    qk_begin, qk_pair, qk_fold, qk_total, qk_relay, qk_rest = irregular(
         "qk",
-        lambda j: (j // 2) * 8 + 2 * head + j % 2,
-        lambda number: lax.div(lax.rem(number, 8), 2),
-        True,
+        12,
+        6,
+        lambda j: ((j // 4) * 8 + 2 * head + j // 2 % 2) * 2 + j % 2,
+        lambda number: lax.div(lax.rem(lax.div(number, 2), 8), 2),
     )
 
-    down_grad = tn(r.dall[...], r.act[...]).astype(BF)
-    r.pdz[...] = down_grad[:, 384:].reshape(8, 96, 384)
+    r.pdz[...] = tn(r.dall[...], r.act[:, 256:]).astype(BF).reshape(8, 96, 512)
     dz_begin()
-    r.pdy[...] = down_grad[:, :384].reshape(8, 96, 384)
+    r.pdy[...] = tn(r.dall[...], r.act[:, :256]).astype(BF).reshape(8, 96, 256)
     dy_begin()
     up_grad = tn(r.sall[...], r.gup[...]).astype(BF)
     for j in range(6):
@@ -1064,17 +1031,27 @@
     sum_row, sum_lane = (lax.broadcasted_iota(jnp.int32, (256, 128), axis) for axis in (0, 1))
     head_sums = jnp.where((lax.div(sum_row, 64) == sum_lane) & (sum_row < 192), 1.0, 0.0).astype(BF)
     r.woo[192:256, :] = jnp.zeros((64, D), BF)
-    dy_pair(0)
-    dy_pair(1)
+    for t in range(4):
+        dy_pair(t)
     dz_fold(0)
+    s_drain()
+    d_drain()
+    dkv, dq, gm = r.sall.at[:, 0:384], r.sall.at[:, 384:640], r.dall.at[:, 0:256]
     l_wait(0)
     l_relay()
     l_rest()
-    r.gm[...] = nt(r.lall[...], r.woo[...]).astype(BF)
+    gm[...] = nt(r.lall[...], r.woo[...]).astype(BF)
+
+    out_grad = tn(r.lall[...], r.mix[...]).reshape(8, 96, 256)
+    r.pou[:, 0:96, :] = out_grad[:, :, :128].astype(BF)
+    third = out_grad[:, :, 128:].reshape(8, 2, 48, 128)
+    moved = pltpu.roll(third[:, 1].reshape(384, 128), 64, 1).reshape(8, 48, 128)
+    r.pou[:, 96:144, :] = (third[:, 0] + moved).astype(BF)
+    ou_begin()
 
     def augment_g(block, carry):
         rows = pl.ds(pl.multiple_of(block * 256, 256), 256)
-        grads = r.gm[rows, :]
+        grads = gm[rows, :]
         product = grads.astype(F32) * r.exact[rows, :]
         inner = jnp.zeros((256, 128), F32)
         for part in split_three(product):
@@ -1083,13 +1060,11 @@
         return carry
 
     lax.fori_loop(0, 4, augment_g, 0)
-    dy_pair(2)
-    dy_pair(3)
     dz_fold(1)
 
     def kv_copy(code):
         rows = block_rows(peer(code))
-        return push(r.dkv.at[rows, :], r.kvin.at[head], r.kvs.at[code - 1], r.kvr.at[code - 1], (dp, peer(code)))
+        return push(r.sall.at[rows, 0:384], r.kvin.at[head], r.kvs.at[code - 1], r.kvr.at[code - 1], (dp, peer(code)))
 
     def q_copy(code):
         return push(r.qs_.at[code], r.qin.at[head], r.qs.at[code - 1], r.qr.at[code - 1], (dp, peer(code)))
@@ -1108,8 +1083,8 @@
             r.big[pl.ds(pl.multiple_of(n * SLOT + block * BLOCK, 256), BLOCK), :] = grad_scores
             key_grad += nn(grad_scores, q_aug[:, lanes]) * mask
             value_grad += nn(probs.astype(BF), g_aug[:, lanes]) * mask
-        r.dkv[rows, 0:192] = key_grad[:, :192].astype(BF)
-        r.dkv[rows, 192:384] = value_grad[:, :192].astype(BF)
+        dkv[rows, 0:192] = key_grad[:, :192].astype(BF)
+        dkv[rows, 192:384] = value_grad[:, :192].astype(BF)
 
         @pl.when(step < 3)
         def _():
@@ -1118,25 +1093,26 @@
         @pl.when(step == 1)
         def _():
             dz_pair()
-            up_pair(0)
-            up_pair(1)
+            dy_fold(0)
+            for j in (0, 1, 2):
+                up_pair(j)
 
         @pl.when(step == 2)
-        def _():
-            dy_fold(0)
-            up_pair(2)
-
-        @pl.when(step == 3)
         def _():
             dy_fold(1)
             up_pair(3)
 
+        @pl.when(step == 3)
+        def _():
+            up_pair(4)
+            up_pair(5)
+
         return carry
 
     lax.fori_loop(0, 4, attend_back, 0)
-    r.kvin[head] = r.dkv[block_rows(head), :]
-    r.pqk[2:6] = tn(r.dkv[...], r.nall[...]).astype(BF).reshape(4, 96, D)
-    qk_begin(range(2, 6))
+    r.kvin[head] = dkv[block_rows(head), :]
+    r.pqk[4:12] = tn(dkv[...], r.nall[...]).astype(BF).reshape(8, 48, D)
+    qk_begin(range(4, 12))
 
     def query_back(step, carry):
         code = 3 - step
@@ -1147,7 +1123,7 @@
             part = r.big[n * SLOT : (n + 1) * SLOT, pl.ds(pl.multiple_of(block * BLOCK, 256), BLOCK)]
             query_grad += tn(part, r.kb[...] * head_mask(n).astype(BF))
         query_grad = query_grad * 0.125
-        r.dq[rows, :] = query_grad.astype(BF)
+        dq[rows, :] = query_grad.astype(BF)
         r.qs_[code] = packed(query_grad)
 
         @pl.when(step < 3)
@@ -1158,24 +1134,20 @@
 
     lax.fori_loop(0, 4, query_back, 0)
     r.qin[head] = r.qs_[0]
-    r.pqk[0:2] = tn(r.dq[...], r.nall[...])[:192].astype(BF).reshape(2, 96, D)
-    qk_begin(range(2))
-    for j in (4, 5):
-        up_pair(j)
-    r.pou[...] = tn(r.lall[...], r.mix[...]).astype(BF).reshape(8, 96, 256)
-    ou_begin()
-    up_fold(0)
-    up_fold(1)
+    r.pqk[0:4] = tn(dq[...], r.nall[...])[:192].astype(BF).reshape(4, 48, D)
+    qk_begin(range(4))
+    for t in range(4):
+        ou_pair(t)
+    for j in (0, 1, 2):
+        up_fold(j)
     dy_total()
-    query_sum = jnp.sum(r.dq[...].astype(F32), axis=0, keepdims=True)
-    value_sum = jnp.sum(r.dkv[:, 128:384].astype(F32), axis=0, keepdims=True)
-    for group in range(4):
-        mine = jnp.where(head == group, 1.0, 0.0)
-        r.vec[4:5, group * 192 : (group + 1) * 192] = query_sum[:, :192] * mine
-        r.vec[5:6, group * 192 : (group + 1) * 192] = value_sum[:, 64:] * mine
     dz_total()
-    up_fold(2)
-    qk_pair(2)
+    for j in range(4, 8):
+        qk_pair(j)
+    for j in (3, 4, 5):
+        up_fold(j)
+    for j in range(8, 12):
+        qk_pair(j)
 
     for code in (3, 2, 1):
         kv_copy(code).wait_recv()
@@ -1190,8 +1162,15 @@
     grad_first += nt(r.wuo[512:768, :], r.wqkv[:, 2 * D :])
     unit, inverse, _ = norm_parts(r.xv[...].astype(F32), gains[0:1, :], shifts[0:1, :])
     r.grad_inputs[...] = r.gh[...] + norm_back(grad_first, unit, inverse, gains[0:1, :])
+    give("grad_inputs")
     r.vec[0:1, :] = jnp.sum(grad_first * unit, axis=0, keepdims=True)
     r.vec[2:3, :] = jnp.sum(grad_first, axis=0, keepdims=True)
+    query_sum = jnp.sum(dq[...].astype(F32), axis=0, keepdims=True)
+    value_sum = jnp.sum(dkv[:, 128:384].astype(F32), axis=0, keepdims=True)
+    for group in range(4):
+        mine = jnp.where(head == group, 1.0, 0.0)
+        r.vec[4:5, group * 192 : (group + 1) * 192] = query_sum[:, :192] * mine
+        r.vec[5:6, group * 192 : (group + 1) * 192] = value_sum[:, 64:] * mine
     for shard in range(8):
         r.small[shard % 2, shard // 2, 0:8, 0:96] = r.vec[:, shard * 96 : (shard + 1) * 96]
 
@@ -1207,47 +1186,56 @@
         return push(r.fsm.at[head], r.fsm.at[head], r.fsms.at[code - 1], r.fsmr.at[code - 1], (dp, peer(code)))
 
     start(small_y)
-    up_fold(3)
-    qk_pair(3)
-    up_fold(4)
-    up_fold(5)
-    for j in (4, 5):
+    for j in range(4):
         qk_pair(j)
-    qk_pair(0)
-    qk_pair(1)
-    for k in (2, 1, 3, 0):
-        ou_pair(k)
+    ou_fold(0)
+    ou_fold(1)
+    for j in range(4, 12):
+        qk_fold(j)
+    up_total()
+    for j in range(4):
+        qk_fold(j)
+    ou_total()
     dy_relay()
     dz_relay()
-    up_total()
     small_y().wait_recv()
     r.small[y] = r.small[y] + r.ysm[...]
     for k in (1, 2, 3):
         start(lambda k=k: small_z(k))
-    qk_total()
-    ou_total()
     up_relay()
+    qk_total(range(4, 12))
+    ou_relay()
+    qk_total(range(4))
     for k in (1, 2, 3):
         small_z(k).wait_recv()
     r.fsm[head] = r.small[y, z] + r.zsm[1] + r.zsm[2] + r.zsm[3]
     for code in (2, 3, 1):
         start(lambda code=code: small_f(code))
+    dy_rest()
+    give("fdy")
+    dz_rest()
+    give("fdz")
     qk_relay()
-    ou_relay()
-    dy_rest()
-    dz_rest()
     up_rest()
+    give("fup")
+    ou_rest()
+    give("fou")
     qk_rest()
-    ou_rest()
+    give("fqk")
     for code in (2, 3, 1):
         small_f(code).wait_recv()
     r.fsum[...] = r.fsm[0] + r.fsm[1] + r.fsm[2] + r.fsm[3]
+    give("fsum")
+    n_drain()
+    l_drain()
     for make, cond in sent:
         when(cond, lambda make=make: make().wait_send())
     for code in (1, 2, 3):
         mix_copy(code).wait_send()
         kv_copy(code).wait_send()
         q_copy(code).wait_send()
+    for copy in given:
+        copy.wait()
 
 
 def emit_kernel(
@@ -1273,7 +1261,7 @@
     for group in range(4):
         for j in range(6):
             place = (4 * j + group) * 128
-            source, at = (fdy_v, j * 128) if j < 3 else (fdz_v, j * 128 - 384)
+            source, at = (fdy_v, j * 128) if j < 2 else (fdz_v, j * 128 - 256)
             down_v[:, place : place + 128] = source[group, :, at : at + 128].astype(F32)
     results.append(begin(down_v, down))
     arrivals[2].wait()
@@ -1288,7 +1276,10 @@
     results.append(begin(qkv_v, qkv))
     arrivals[6].wait()
     for group in range(4):
-        out_v[:, group * 192 : (group + 1) * 192] = fou_v[group][:, :192].astype(F32)
+        piece, lane = fou_v[group].astype(F32), group * 192
+        out_v[:, lane : lane + 128] = piece[0:96]
+        out_v[0:48, lane + 128 : lane + 192] = piece[96:144, 0:64]
+        out_v[48:96, lane + 128 : lane + 192] = piece[96:144, 64:128]
     results.append(begin(out_v, out))
     arrivals[7].wait()
     for index, ref in enumerate((gains, shifts, qv_bias, out_biases)):
@@ -1301,15 +1292,15 @@
 def per_device(x, norm_gains, norm_shifts, w_qkv, qv_bias, w_out, out_biases, w_up, up_bias, w_down, lengths, d_out):
     values = dict(
         x=x[0], gains=norm_gains, shifts=norm_shifts, w_qkv=w_qkv, qv_bias=qv_bias, w_out=w_out, biases=out_biases,
-        w_up=w_up, up_bias=up_bias.reshape(1, FF), w_down=w_down, lengths=lengths, d_out=d_out[0],
+        w_up=w_up, up_bias=up_bias.reshape(24, 128), w_down=w_down, lengths=lengths, d_out=d_out[0],
     )
     place = {True: pl.BlockSpec(memory_space=pl.ANY), False: pl.BlockSpec(memory_space=pltpu.VMEM)}
     block_out, grad_inputs, fup, fqk, fdy, fdz, fou, fsum = pl.pallas_call(
         one_kernel,
         out_shape=[jax.ShapeDtypeStruct(shape, kind) for _, shape, kind in OUTPUTS],
         in_specs=[place[name in IN_PLACE] for name in INPUTS],
-        out_specs=[place[False]] * len(OUTPUTS),
-        scratch_shapes=[pltpu.VMEM(shape, kind) for _, shape, kind in BUFFERS]
+        out_specs=[place[True]] * len(OUTPUTS),
+        scratch_shapes=[pltpu.VMEM(shape, kind) for _, shape, kind in OUTPUTS + BUFFERS]
         + [pltpu.SemaphoreType.DMA((count,)) for _, count in SEMAPHORES],
         compiler_params=pltpu.CompilerParams(
             collective_id=0, has_side_effects=True, vmem_limit_bytes=VMEM_LIMIT

time: 111 us -> 102 us (0.919)
  the two profiles are of different devices: /device:TPU:3 before, /device:TPU:11 now
where the time goes in v4:
time: 102 us
  Pallas kernels  101 us (99%)
    pallas_call x1, Pallas kernels, per_device(): pl.pallas_call(one_kernel, out_shape=[jax.ShapeDtypeStruct(shape, kind) f...  96.9 us
    pallas_call x1, Pallas kernels, per_device(): pl.pallas_call(emit_kernel, out_shape=[jax.ShapeDtypeStruct(shape, F32 if...  4.14 us

profile of v4, /device:TPU:11, one launch (start us, length us, event | category | flops | bytes accessed | tf_op | source)
XLA Modules:
  0.0 101.9 jit_solution(9145516878172355217)
XLA Ops:
  0.6 96.9 %block.1 = (bf16[256,768]{1,0:T(8,128)(2,1)}, f32[256,768]{1,0:T(8,128)}, bf16[3,768,128]{2,1,0:T(8,128)(2,1)}, bf16[6,48,768]{2,1,0:T(8,128)(2,1)}, bf16[4,96,2...) custom-call(bf16[256,768]{1,0:T(8,128)(2,1)} %bitcast.9, ...), custom_call_target="tpu_custom_call" | custom-call | tf_op jit(solution)/shard_map/block/pallas_call | solution.py:1298
  97.6 4.1 %emit.1 = (bf16[256,768]{1,0:T(8,128)(2,1)}, f32[256,768]{1,0:T(8,128)}, f32[2,96]{1,0:T(2,128)}, f32[2,96]{1,0:T(2,128)}, f32[288,768]{1,0:T(8,128)}, /*index=5...) custom-call(bf16[256,768]{1,0:T(8,128)(2,1)} %get-tuple-element.30.b, ...), custom_call_target="tpu_custom_call" | custom-call | tf_op jit(solution)/shard_map/emit/pallas_call | solution.py:1312

commit v5 on v4

--- a/solution.py
+++ b/solution.py
@@ -399,7 +399,10 @@
     ("gh", (256, D), F32),
     ("act", (SLOT, D), BF),
     ("gup", (SLOT, D), BF),
-    ("kvin", (4, 256, 384), BF),
+    ("kin", (4, 384, 128), BF),
+    ("vin", (4, 384, 128), BF),
+    ("ks_", (4, 384, 128), BF),
+    ("vs_", (4, 384, 128), BF),
     ("qs_", (4, 384, 128), BF),
     ("qin", (4, 384, 128), BF),
     ("pdy", (8, 96, 256), BF),
@@ -422,18 +425,23 @@
     ("small", (2, 4, 16, 128), F32),
     ("ysm", (4, 16, 128), F32),
     ("zsm", (4, 16, 128), F32),
-    ("fsm", (4, 16, 128), F32),
+    ("fsm", (4, 2, 4, 16, 128), F32),
+    ("last", (4, 16, 128), F32),
+    ("lasty", (2, 8, 128), F32),
+    ("lastz", (5, 8, 128), F32),
+    ("lastf", (8, 128), F32),
 )
 SEMAPHORES = (
     ("load", 22), ("give", 8),
     ("ns", 5), ("nr", 5), ("ds", 5), ("dr", 5), ("ss", 5), ("sr", 5), ("ls", 5), ("lr", 5),
-    ("ms", 3), ("mr", 3), ("kvs", 3), ("kvr", 3), ("qs", 3), ("qr", 3),
+    ("ms", 3), ("mr", 3), ("ks", 3), ("kr", 3), ("vs", 3), ("vr", 3), ("qs", 3), ("qr", 3),
     ("ydys", 4), ("ydyr", 4), ("zdys", 4), ("zdyr", 4), ("fdys", 3), ("fdyr", 3),
     ("ydzs", 1), ("ydzr", 1), ("zdzs", 4), ("zdzr", 4), ("fdzs", 3), ("fdzr", 3),
     ("yous", 4), ("your", 4), ("zous", 4), ("zour", 4), ("fous", 3), ("four", 3),
     ("yups", 6), ("yupr", 6), ("zups", 6), ("zupr", 12), ("fups", 9), ("fupr", 9),
     ("yqks", 12), ("yqkr", 12), ("zqks", 12), ("zqkr", 24), ("fqks", 18), ("fqkr", 18),
     ("ysms", 1), ("ysmr", 1), ("zsms", 4), ("zsmr", 4), ("fsms", 3), ("fsmr", 3),
+    ("las", 3), ("lar", 3), ("lays", 1), ("layr", 1), ("lazs", 4), ("lazr", 4),
 )
 INPUTS = ("x", "gains", "shifts", "w_qkv", "qv_bias", "w_out", "biases", "w_up", "up_bias", "w_down", "lengths", "d_out")
 IN_PLACE = ("x", "w_qkv", "w_out", "w_up", "w_down", "d_out")
@@ -543,14 +551,19 @@
     whole = lengths[:, 0:1] == SLOT
     total = jnp.sum(lengths, axis=1, keepdims=True)
 
-    def gather(buf, send, recv):
+    def piece_rows(block, offset, size):
+        return pl.ds(pl.multiple_of(block * BLOCK + offset, 32), size)
+
+    def gather(buf, send, recv, cut=128):
+        pieces = ((0, cut), (cut, BLOCK - cut))
+
         def copy_of(index):
             if index == 0:
                 rows, to = block_rows(head), sib
             elif index < 3:
-                rows, to = block_rows(head, 128, (index - 1) * 128), far
+                rows, to = piece_rows(head, *pieces[index - 1]), far
             else:
-                rows, to = block_rows(far, 128, (index - 3) * 128), sib
+                rows, to = piece_rows(far, *pieces[index - 3]), sib
             return push(buf.at[rows, :], buf.at[rows, :], send.at[index], recv.at[index], (dp, to))
 
         def begin(these=(1, 2, 0)):
@@ -576,7 +589,7 @@
         return begin, wait, relay, rest, drain
 
     n_begin, n_wait, n_relay, n_rest, n_drain = gather(r.nall, r.ns, r.nr)
-    d_begin, d_wait, d_relay, d_rest, d_drain = gather(r.dall, r.ds, r.dr)
+    d_begin, d_wait, d_relay, d_rest, d_drain = gather(r.dall, r.ds, r.dr, 160)
     s_begin, s_wait, s_relay, s_rest, s_drain = gather(r.sall, r.ss, r.sr)
     l_begin, l_wait, l_relay, l_rest, l_drain = gather(r.lall, r.ls, r.lr)
 
@@ -989,11 +1002,11 @@
         r.pup[j] = up_grad[:, j * 128 : (j + 1) * 128]
     up_begin()
 
-    r.small[...] = jnp.zeros_like(r.small)
+    r.fsm[head] = jnp.zeros((2, 4, 16, 128), F32)
     for j in range(6):
         number = 4 * j + head
         shard = lax.div(number, 3)
-        r.small[lax.rem(shard, 2), lax.div(shard, 2), pl.ds(8 + lax.rem(number, 3), 1), :] = sums[
+        r.fsm[head, lax.rem(shard, 2), lax.div(shard, 2), pl.ds(8 + lax.rem(number, 3), 1), :] = sums[
             :, j * 128 : (j + 1) * 128
         ]
 
@@ -1031,14 +1044,18 @@
     sum_row, sum_lane = (lax.broadcasted_iota(jnp.int32, (256, 128), axis) for axis in (0, 1))
     head_sums = jnp.where((lax.div(sum_row, 64) == sum_lane) & (sum_row < 192), 1.0, 0.0).astype(BF)
     r.woo[192:256, :] = jnp.zeros((64, D), BF)
-    for t in range(4):
-        dy_pair(t)
-    dz_fold(0)
+    l_relay((1,))
+    dy_pair(0)
+    dy_pair(1)
     s_drain()
     d_drain()
-    dkv, dq, gm = r.sall.at[:, 0:384], r.sall.at[:, 384:640], r.dall.at[:, 0:256]
+    dv, dq, dk = (r.sall.at[:, part * 256 : (part + 1) * 256] for part in range(3))
+    gm = r.dall.at[:, 0:256]
     l_wait(0)
-    l_relay()
+    l_relay((2,))
+    dz_fold(0)
+    dy_pair(2)
+    dy_pair(3)
     l_rest()
     gm[...] = nt(r.lall[...], r.woo[...]).astype(BF)
 
@@ -1062,9 +1079,11 @@
     lax.fori_loop(0, 4, augment_g, 0)
     dz_fold(1)
 
-    def kv_copy(code):
-        rows = block_rows(peer(code))
-        return push(r.sall.at[rows, 0:384], r.kvin.at[head], r.kvs.at[code - 1], r.kvr.at[code - 1], (dp, peer(code)))
+    def k_copy(code):
+        return push(r.ks_.at[code], r.kin.at[head], r.ks.at[code - 1], r.kr.at[code - 1], (dp, peer(code)))
+
+    def v_copy(code):
+        return push(r.vs_.at[code], r.vin.at[head], r.vs.at[code - 1], r.vr.at[code - 1], (dp, peer(code)))
 
     def q_copy(code):
         return push(r.qs_.at[code], r.qin.at[head], r.qs.at[code - 1], r.qr.at[code - 1], (dp, peer(code)))
@@ -1073,7 +1092,6 @@
         code = 3 - step
         block = peer(code)
         rows = block_rows(block)
-        key_grad = jnp.zeros((BLOCK, 256), F32)
         value_grad = jnp.zeros((BLOCK, 256), F32)
         for n in range(3):
             mask = head_mask(n)
@@ -1081,38 +1099,33 @@
             probs = jnp.exp(nt(r.kb[rows, :], q_aug[:, lanes]))
             grad_scores = (probs * nt(r.vb[rows, :], g_aug[:, lanes])).astype(BF)
             r.big[pl.ds(pl.multiple_of(n * SLOT + block * BLOCK, 256), BLOCK), :] = grad_scores
-            key_grad += nn(grad_scores, q_aug[:, lanes]) * mask
             value_grad += nn(probs.astype(BF), g_aug[:, lanes]) * mask
-        dkv[rows, 0:192] = key_grad[:, :192].astype(BF)
-        dkv[rows, 192:384] = value_grad[:, :192].astype(BF)
+        dv[rows, :] = value_grad.astype(BF)
+        r.vs_[code] = packed(value_grad)
 
         @pl.when(step < 3)
         def _():
-            kv_copy(code).start()
-
-        @pl.when(step == 1)
+            v_copy(code).start()
+
+        @pl.when(step == 2)
         def _():
             dz_pair()
             dy_fold(0)
-            for j in (0, 1, 2):
-                up_pair(j)
-
-        @pl.when(step == 2)
+            up_pair(0)
+            up_pair(1)
+
+        @pl.when(step == 3)
         def _():
             dy_fold(1)
-            up_pair(3)
-
-        @pl.when(step == 3)
-        def _():
-            up_pair(4)
-            up_pair(5)
+            up_pair(2)
 
         return carry
 
     lax.fori_loop(0, 4, attend_back, 0)
-    r.kvin[head] = dkv[block_rows(head), :]
-    r.pqk[4:12] = tn(dkv[...], r.nall[...]).astype(BF).reshape(8, 48, D)
-    qk_begin(range(4, 12))
+    r.vin[head] = r.vs_[0]
+    r.pqk[8:12] = tn(dv[...], r.nall[...])[:192].astype(BF).reshape(4, 48, D)
+    qk_begin(range(8, 12))
+    up_pair(3)
 
     def query_back(step, carry):
         code = 3 - step
@@ -1136,81 +1149,136 @@
     r.qin[head] = r.qs_[0]
     r.pqk[0:4] = tn(dq[...], r.nall[...])[:192].astype(BF).reshape(4, 48, D)
     qk_begin(range(4))
+    up_pair(4)
+    up_pair(5)
+
+    def key_back(step, carry):
+        code = 3 - step
+        block = peer(code)
+        rows = block_rows(block)
+        key_grad = jnp.zeros((BLOCK, 256), F32)
+        for n in range(3):
+            part = r.big[pl.ds(pl.multiple_of(n * SLOT + block * BLOCK, 256), BLOCK), :]
+            key_grad += nn(part, q_aug[:, n * 256 : (n + 1) * 256]) * head_mask(n)
+        dk[rows, :] = key_grad.astype(BF)
+        r.ks_[code] = packed(key_grad)
+
+        @pl.when(step < 3)
+        def _():
+            k_copy(code).start()
+
+        return carry
+
+    lax.fori_loop(0, 4, key_back, 0)
+    r.kin[head] = r.ks_[0]
+    r.pqk[4:8] = tn(dk[...], r.nall[...])[:192].astype(BF).reshape(4, 48, D)
+    qk_begin(range(4, 8))
+    query_sum = jnp.sum(dq[...].astype(F32), axis=0, keepdims=True)
+    value_sum = jnp.sum(dv[...].astype(F32), axis=0, keepdims=True)
+    for group in range(4):
+        mine = jnp.where(head == group, 1.0, 0.0)
+        r.vec[4:5, group * 192 : (group + 1) * 192] = query_sum[:, :192] * mine
+        r.vec[5:6, group * 192 : (group + 1) * 192] = value_sum[:, :192] * mine
+    for shard in range(8):
+        r.fsm[head, shard % 2, shard // 2, 0:8, 0:96] = r.vec[:, shard * 96 : (shard + 1) * 96]
+
+    def small_y():
+        return push(r.small.at[1 - y], r.ysm, r.ysms.at[0], r.ysmr.at[0], (other_y, head))
+
+    def small_z(k):
+        return push(
+            r.small.at[y, z_shard(k)], r.zsm.at[k], r.zsms.at[k], r.zsmr.at[k], (z_shard(k) * 2 + y, head)
+        )
+
+    def small_f(code):
+        return push(r.fsm.at[head], r.fsm.at[head], r.fsms.at[code - 1], r.fsmr.at[code - 1], (dp, peer(code)))
+
+    for code in (2, 3, 1):
+        start(lambda code=code: small_f(code))
     for t in range(4):
         ou_pair(t)
     for j in (0, 1, 2):
         up_fold(j)
     dy_total()
     dz_total()
-    for j in range(4, 8):
+    for j in range(8, 12):
         qk_pair(j)
     for j in (3, 4, 5):
         up_fold(j)
-    for j in range(8, 12):
+    for j in range(4):
         qk_pair(j)
 
     for code in (3, 2, 1):
-        kv_copy(code).wait_recv()
+        k_copy(code).wait_recv()
+        v_copy(code).wait_recv()
         q_copy(code).wait_recv()
     unpack(r.qin, r.wuo, 0)
-    for group in range(4):
-        lanes = slice(group * 192, (group + 1) * 192)
-        r.wuo[256:512, lanes] = r.kvin[group][:, :192]
-        r.wuo[512:768, lanes] = r.kvin[group][:, 192:]
+    unpack(r.kin, r.wuo, 256)
+    unpack(r.vin, r.wuo, 512)
     grad_first = nt(r.wuo[0:256, :], r.wqkv[:, 0:D])
     grad_first += nt(r.wuo[256:512, :], r.wqkv[:, D : 2 * D])
     grad_first += nt(r.wuo[512:768, :], r.wqkv[:, 2 * D :])
+    ou_fold(0)
+    ou_fold(1)
+    for code in (1, 2, 3):
+        small_f(code).wait_recv()
+    r.small[...] = r.fsm[0] + r.fsm[1] + r.fsm[2] + r.fsm[3]
+    start(small_y)
+    for j in range(8, 12):
+        qk_fold(j)
     unit, inverse, _ = norm_parts(r.xv[...].astype(F32), gains[0:1, :], shifts[0:1, :])
     r.grad_inputs[...] = r.gh[...] + norm_back(grad_first, unit, inverse, gains[0:1, :])
     give("grad_inputs")
-    r.vec[0:1, :] = jnp.sum(grad_first * unit, axis=0, keepdims=True)
-    r.vec[2:3, :] = jnp.sum(grad_first, axis=0, keepdims=True)
-    query_sum = jnp.sum(dq[...].astype(F32), axis=0, keepdims=True)
-    value_sum = jnp.sum(dkv[:, 128:384].astype(F32), axis=0, keepdims=True)
-    for group in range(4):
-        mine = jnp.where(head == group, 1.0, 0.0)
-        r.vec[4:5, group * 192 : (group + 1) * 192] = query_sum[:, :192] * mine
-        r.vec[5:6, group * 192 : (group + 1) * 192] = value_sum[:, 64:] * mine
+    pair = jnp.concatenate(
+        [jnp.sum(grad_first * unit, axis=0, keepdims=True), jnp.sum(grad_first, axis=0, keepdims=True)], axis=0
+    )
+    r.last[head] = jnp.zeros((16, 128), F32)
     for shard in range(8):
-        r.small[shard % 2, shard // 2, 0:8, 0:96] = r.vec[:, shard * 96 : (shard + 1) * 96]
-
-    def small_y():
-        return push(r.small.at[1 - y], r.ysm, r.ysms.at[0], r.ysmr.at[0], (other_y, head))
-
-    def small_z(k):
-        return push(
-            r.small.at[y, z_shard(k)], r.zsm.at[k], r.zsms.at[k], r.zsmr.at[k], (z_shard(k) * 2 + y, head)
-        )
-
-    def small_f(code):
-        return push(r.fsm.at[head], r.fsm.at[head], r.fsms.at[code - 1], r.fsmr.at[code - 1], (dp, peer(code)))
-
-    start(small_y)
-    for j in range(4):
+        at = shard % 2 * 8 + shard // 2 * 2
+        r.last[head, at : at + 2, 0:96] = pair[:, shard * 96 : (shard + 1) * 96]
+
+    def last_head(code):
+        return push(r.last.at[head], r.last.at[head], r.las.at[code - 1], r.lar.at[code - 1], (dp, peer(code)))
+
+    def last_y():
+        return push(r.lasty.at[1 - y], r.lastz.at[4], r.lays.at[0], r.layr.at[0], (other_y, head))
+
+    def last_z(k):
+        return push(r.lastz.at[0], r.lastz.at[k], r.lazs.at[k], r.lazr.at[k], (z_shard(k) * 2 + y, head))
+
+    for code in (2, 3, 1):
+        start(lambda code=code: last_head(code))
+    for j in range(4, 8):
         qk_pair(j)
-    ou_fold(0)
-    ou_fold(1)
-    for j in range(4, 12):
-        qk_fold(j)
     up_total()
     for j in range(4):
         qk_fold(j)
-    ou_total()
-    dy_relay()
-    dz_relay()
     small_y().wait_recv()
     r.small[y] = r.small[y] + r.ysm[...]
     for k in (1, 2, 3):
         start(lambda k=k: small_z(k))
+    for code in (1, 2, 3):
+        last_head(code).wait_recv()
+    over_head = r.last[0] + r.last[1] + r.last[2] + r.last[3]
+    r.lasty[0] = over_head[0:8]
+    r.lasty[1] = over_head[8:16]
+    start(last_y)
+    dy_relay()
+    dz_relay()
+    ou_total()
+    qk_total(range(8, 12))
+    for j in range(4, 8):
+        qk_fold(j)
+    last_y().wait_recv()
+    r.lastz[0] = r.lasty[y] + r.lastz[4]
+    for k in (1, 2, 3):
+        start(lambda k=k: last_z(k))
+    qk_total(range(4))
     up_relay()
-    qk_total(range(4, 12))
     ou_relay()
-    qk_total(range(4))
+    qk_total(range(4, 8))
     for k in (1, 2, 3):
-        small_z(k).wait_recv()
-    r.fsm[head] = r.small[y, z] + r.zsm[1] + r.zsm[2] + r.zsm[3]
-    for code in (2, 3, 1):
-        start(lambda code=code: small_f(code))
+        last_z(k).wait_recv()
     dy_rest()
     give("fdy")
     dz_rest()
@@ -1222,9 +1290,12 @@
     give("fou")
     qk_rest()
     give("fqk")
-    for code in (2, 3, 1):
-        small_f(code).wait_recv()
-    r.fsum[...] = r.fsm[0] + r.fsm[1] + r.fsm[2] + r.fsm[3]
+    for k in (1, 2, 3):
+        small_z(k).wait_recv()
+    r.fsum[...] = r.small[y, z] + r.zsm[1] + r.zsm[2] + r.zsm[3]
+    r.lastf[...] = r.lastz[0] + r.lastz[1] + r.lastz[2] + r.lastz[3]
+    r.fsum[0:1, :] = r.lastf[pl.ds(2 * z, 1), :]
+    r.fsum[2:3, :] = r.lastf[pl.ds(2 * z + 1, 1), :]
     give("fsum")
     n_drain()
     l_drain()
@@ -1232,7 +1303,8 @@
         when(cond, lambda make=make: make().wait_send())
     for code in (1, 2, 3):
         mix_copy(code).wait_send()
-        kv_copy(code).wait_send()
+        k_copy(code).wait_send()
+        v_copy(code).wait_send()
         q_copy(code).wait_send()
     for copy in given:
         copy.wait()

time: 102 us -> 99.5 us (0.975)
  the two profiles are of different devices: /device:TPU:11 before, /device:TPU:3 now
where the time goes in v5:
time: 99.5 us; the launch traced here: 97.8 us
  Pallas kernels  96.9 us (97%)
    pallas_call x1, Pallas kernels, per_device(): pl.pallas_call(one_kernel, out_shape=[jax.ShapeDtypeStruct(shape, kind) f...  92.8 us
    pallas_call x1, Pallas kernels, per_device(): pl.pallas_call(emit_kernel, out_shape=[jax.ShapeDtypeStruct(shape, F32 if...  4.14 us

profile of v5, /device:TPU:3, one launch (start us, length us, event | category | flops | bytes accessed | tf_op | source)
XLA Modules:
  0.0 97.8 jit_solution(17533046384332678783)
XLA Ops:
  0.6 92.8 %block.1 = (bf16[256,768]{1,0:T(8,128)(2,1)}, f32[256,768]{1,0:T(8,128)}, bf16[3,768,128]{2,1,0:T(8,128)(2,1)}, bf16[6,48,768]{2,1,0:T(8,128)(2,1)}, bf16[4,96,2...) custom-call(bf16[256,768]{1,0:T(8,128)(2,1)} %bitcast.9, ...), custom_call_target="tpu_custom_call" | custom-call | tf_op jit(solution)/shard_map/block/pallas_call | solution.py:1370
  93.4 4.1 %emit.1 = (bf16[256,768]{1,0:T(8,128)(2,1)}, f32[256,768]{1,0:T(8,128)}, f32[2,96]{1,0:T(2,128)}, f32[2,96]{1,0:T(2,128)}, f32[288,768]{1,0:T(8,128)}, /*index=5...) custom-call(bf16[256,768]{1,0:T(8,128)(2,1)} %get-tuple-element.30.b, ...), custom_call_target="tpu_custom_call" | custom-call | tf_op jit(solution)/shard_map/emit/pallas_call | solution.py:1384

commit v6 on v5

--- a/solution.py
+++ b/solution.py
@@ -1197,14 +1197,12 @@
         start(lambda code=code: small_f(code))
     for t in range(4):
         ou_pair(t)
-    for j in (0, 1, 2):
+    for j in range(8, 12):
+        qk_pair(j)
+    for j in range(6):
         up_fold(j)
     dy_total()
     dz_total()
-    for j in range(8, 12):
-        qk_pair(j)
-    for j in (3, 4, 5):
-        up_fold(j)
     for j in range(4):
         qk_pair(j)
 
@@ -1313,7 +1311,7 @@
 def emit_kernel(
     block_in, inputs_in, fup, fqk, fdy, fdz, fou, fsum,
     block_out, grad_inputs, gains, shifts, qkv, qv_bias, out, out_biases, up, up_bias, down,
-    block_v, inputs_v, fup_v, fqk_v, fdy_v, fdz_v, fou_v, fsum_v, up_v, qkv_v, down_v, out_v, sems,
+    block_v, inputs_v, fup_v, fqk_v, fdy_v, fdz_v, fou_v, fsum_v, up_v, qkv_v, down_v, out_v, gains_v, shifts_v, qv_v, ob_v, ub_v, sems,
 ):
     count = []
 
@@ -1336,6 +1334,12 @@
             source, at = (fdy_v, j * 128) if j < 2 else (fdz_v, j * 128 - 256)
             down_v[:, place : place + 128] = source[group, :, at : at + 128].astype(F32)
     results.append(begin(down_v, down))
+    arrivals[7].wait()
+    for index, (ref, dst) in enumerate(((gains_v, gains), (shifts_v, shifts), (qv_v, qv_bias), (ob_v, out_biases))):
+        ref[...] = fsum_v[2 * index : 2 * index + 2, 0:96]
+        results.append(begin(ref, dst))
+    ub_v[...] = fsum_v[8:11, :]
+    results.append(begin(ub_v, up_bias))
     arrivals[2].wait()
     for i in range(3):
         up_v[:, i * 128 : (i + 1) * 128] = fup_v[i].astype(F32)
@@ -1353,10 +1357,6 @@
         out_v[0:48, lane + 128 : lane + 192] = piece[96:144, 0:64]
         out_v[48:96, lane + 128 : lane + 192] = piece[96:144, 64:128]
     results.append(begin(out_v, out))
-    arrivals[7].wait()
-    for index, ref in enumerate((gains, shifts, qv_bias, out_biases)):
-        ref[...] = fsum_v[2 * index : 2 * index + 2, 0:96]
-    up_bias[...] = fsum_v[8:11, :]
     for copy in results:
         copy.wait()
 
@@ -1385,10 +1385,11 @@
         emit_kernel,
         out_shape=[jax.ShapeDtypeStruct(shape, F32 if n else BF) for n, shape in enumerate(shapes)],
         in_specs=[anywhere] * 8,
-        out_specs=[anywhere] * 2 + [anywhere if shape[0] > 16 else place[False] for shape in shapes[2:]],
+        out_specs=[anywhere] * len(shapes),
         scratch_shapes=[pltpu.VMEM(shape, kind) for _, shape, kind in OUTPUTS]
         + [pltpu.VMEM(shape, F32) for shape in ((D, 384), (288, D), (96, FF), (96, D))]
-        + [pltpu.SemaphoreType.DMA((14,))],
+        + [pltpu.VMEM(shape, F32) for shape in ((2, 96),) * 4 + ((3, 128),)]
+        + [pltpu.SemaphoreType.DMA((19,))],
         compiler_params=pltpu.CompilerParams(vmem_limit_bytes=VMEM_LIMIT),
         name="emit",
     )(block_out, grad_inputs, fup, fqk, fdy, fdz, fou, fsum)

time: 99.5 us -> 99.2 us (level); the launches traced: 97.8 us -> 98.5 us
    pallas_call x1, Pallas kernels: 92.8 us -> 94 us  [per_device(): pl.pallas_call(one_kernel, out_shape=[jax.ShapeDtypeStruct(shape, kind) f...]
where the time goes in v6:
time: 99.2 us; the launch traced here: 98.5 us
  Pallas kernels  97.6 us (98%)
    pallas_call x1, Pallas kernels, per_device(): pl.pallas_call(one_kernel, out_shape=[jax.ShapeDtypeStruct(shape, kind) f...  94 us
    pallas_call x1, Pallas kernels, per_device(): pl.pallas_call(emit_kernel, out_shape=[jax.ShapeDtypeStruct(shape, F32 if...  3.66 us

profile of v6, /device:TPU:3, one launch (start us, length us, event | category | flops | bytes accessed | tf_op | source)
XLA Modules:
  0.0 98.5 jit_solution(5289793979380601651)
XLA Ops:
  0.6 94.0 %block.1 = (bf16[256,768]{1,0:T(8,128)(2,1)}, f32[256,768]{1,0:T(8,128)}, bf16[3,768,128]{2,1,0:T(8,128)(2,1)}, bf16[6,48,768]{2,1,0:T(8,128)(2,1)}, bf16[4,96,2...) custom-call(bf16[256,768]{1,0:T(8,128)(2,1)} %bitcast.9, ...), custom_call_target="tpu_custom_call" | custom-call | tf_op jit(solution)/shard_map/block/pallas_call | solution.py:1370
  94.6 3.7 %emit.1 = (bf16[256,768]{1,0:T(8,128)(2,1)}, f32[256,768]{1,0:T(8,128)}, f32[2,96]{1,0:T(2,128)}, f32[2,96]{1,0:T(2,128)}, f32[288,768]{1,0:T(8,128)}, /*index=5...) custom-call(bf16[256,768]{1,0:T(8,128)(2,1)} %get-tuple-element.30.b, ...), custom_call_target="tpu_custom_call" | custom-call | tf_op jit(solution)/shard_map/emit/pallas_call | solution.py:1384

commit v7 on v6

--- a/solution.py
+++ b/solution.py
@@ -1263,10 +1263,10 @@
     start(last_y)
     dy_relay()
     dz_relay()
+    for j in range(4, 8):
+        qk_fold(j)
     ou_total()
     qk_total(range(8, 12))
-    for j in range(4, 8):
-        qk_fold(j)
     last_y().wait_recv()
     r.lastz[0] = r.lasty[y] + r.lastz[4]
     for k in (1, 2, 3):

time: 99.2 us -> 99.2 us (level)
  no operation moved by 1% of the time
where the time goes in v7:
time: 99.2 us; the launch traced here: 98.5 us
  Pallas kernels  97.6 us (98%)
    pallas_call x1, Pallas kernels, per_device(): pl.pallas_call(one_kernel, out_shape=[jax.ShapeDtypeStruct(shape, kind) f...  94 us
    pallas_call x1, Pallas kernels, per_device(): pl.pallas_call(emit_kernel, out_shape=[jax.ShapeDtypeStruct(shape, F32 if...  3.66 us

profile of v7, /device:TPU:3, one launch (start us, length us, event | category | flops | bytes accessed | tf_op | source)
XLA Modules:
  0.0 98.5 jit_solution(12418746550625453284)
XLA Ops:
  0.6 94.0 %block.1 = (bf16[256,768]{1,0:T(8,128)(2,1)}, f32[256,768]{1,0:T(8,128)}, bf16[3,768,128]{2,1,0:T(8,128)(2,1)}, bf16[6,48,768]{2,1,0:T(8,128)(2,1)}, bf16[4,96,2...) custom-call(bf16[256,768]{1,0:T(8,128)(2,1)} %bitcast.9, ...), custom_call_target="tpu_custom_call" | custom-call | tf_op jit(solution)/shard_map/block/pallas_call | solution.py:1370
  94.6 3.7 %emit.1 = (bf16[256,768]{1,0:T(8,128)(2,1)}, f32[256,768]{1,0:T(8,128)}, f32[2,96]{1,0:T(2,128)}, f32[2,96]{1,0:T(2,128)}, f32[288,768]{1,0:T(8,128)}, /*index=5...) custom-call(bf16[256,768]{1,0:T(8,128)(2,1)} %get-tuple-element.30.b, ...), custom_call_target="tpu_custom_call" | custom-call | tf_op jit(solution)/shard_map/emit/pallas_call | solution.py:1384
